TPU v7x, 32 devices: a whole 2x2x4 slice. The times are simulated.
32 devices in a mesh: groups: 2 (over y), seq: 8 (over z, core), panel: 2 (over x).
Axes of the slice: x: 2, y: 2, z: 4, core: 2. Of those that a mesh axis runs over, the one named last changes fastest.
Arguments:
- queries: bfloat16 [4096, 3072], P(('groups', 'seq'), 'panel'), parts along dimension 0, may hold values from -120 to 120
- key_rows: bfloat16 [4096, 3072], P(('groups', 'seq'), 'panel'), parts along dimension 0, may hold values from -6 to 6
- value_rows: bfloat16 [4096, 3072], P(('groups', 'seq'), 'panel'), parts along dimension 0, may hold values from -6 to 6
- block_lists: int32 [24, 16, 8], P('panel'), may hold values from 0 to 15, as said below
- block_counts: int32 [24, 16], P('panel'), may hold values from 4 to 8, as said below
Outputs:
- attended: bfloat16 [4096, 3072], P(('groups', 'seq', 'panel')), parts along dimension 0
There are 2 independent parts, one for each index of `groups`. A program takes and returns all parts, laid end to end along the dimension named above; an argument that names none is the same for every part. Nothing has to cross between parts.
Inputs may be any that keep to these rules, and one draw needn't show every extreme that they name: `block_lists`: entry 0 of each list is the tile's own block index; the entries of one list are distinct; for each head, the lists of the 2 tiles held by one index of seq name together at most 1 distinct blocks among the 2 blocks of any other index of seq, and exactly 1 of some other index. `block_counts`: some list has all 8 entries live.
All inputs are finite; a program needn't handle non-finite values.
Results may differ from a plain program's by a relative error of at most 0.008.
Values may be sent and summed in bfloat16 or wider, within the bound.
No kernel may reach another device: no remote copies, remote signals or barrier semaphores. Data moves between devices by JAX's collectives and lax.ppermute only.
A program may use at most 128 MiB of HBM per device.

v0:
```python
import jax
import jax.numpy as jnp
from jax import lax
from jax.sharding import PartitionSpec as P

HEAD_DIM = 128
BLOCK = 128


def shards(queries, key_rows, value_rows, block_lists, block_counts):
    local_rows = queries.shape[0]
    heads_here = queries.shape[1] // HEAD_DIM
    tiles_here = local_rows // BLOCK
    listed_len = block_lists.shape[2]
    scale = HEAD_DIM ** (-0.5)
    position = lax.axis_index("seq")
    my_lists = lax.dynamic_slice_in_dim(block_lists, position * tiles_here, tiles_here, 1)
    my_counts = lax.dynamic_slice_in_dim(block_counts, position * tiles_here, tiles_here, 1)
    slot_live = jnp.arange(listed_len, dtype=jnp.int32)[None, None, :] < my_counts[:, :, None]
    query_heads = queries.reshape(local_rows, heads_here, HEAD_DIM).transpose(1, 0, 2)
    start_top = jnp.full((heads_here, local_rows), -1e30, jnp.float32)
    start_total = jnp.zeros((heads_here, local_rows), jnp.float32)
    start_mixed = jnp.zeros((heads_here, local_rows, HEAD_DIM), jnp.float32)
    key_piece = lax.all_gather(key_rows, "seq", axis=0, tiled=True)
    value_piece = lax.all_gather(value_rows, "seq", axis=0, tiled=True)
    piece_rows = key_piece.shape[0]
    piece_blocks = piece_rows // BLOCK
    piece_ids = jnp.arange(piece_blocks, dtype=jnp.int32)
    hits = (my_lists[:, :, :, None] == piece_ids[None, None, None, :]) & slot_live[:, :, :, None]
    keep = jnp.any(hits, axis=2)
    key_heads = key_piece.reshape(piece_rows, heads_here, HEAD_DIM).transpose(1, 0, 2)
    value_heads = value_piece.reshape(piece_rows, heads_here, HEAD_DIM).transpose(1, 0, 2)

    def one_head(items):
        query_head, key_head, value_head, keep_head, old_top, old_total, old_mixed = items
        mask = jnp.repeat(jnp.repeat(keep_head, BLOCK, axis=0), BLOCK, axis=1)
        scores = (
            lax.dot_general(
                query_head, key_head, (((1,), (1,)), ((), ())), preferred_element_type=jnp.float32
            )
            * scale
        )
        masked = jnp.where(mask, scores, -1e30)
        new_top = jnp.maximum(old_top, jnp.max(masked, axis=1))
        weights = jnp.where(mask, jnp.exp(masked - new_top[:, None]), 0.0)
        factor = jnp.exp(old_top - new_top)
        new_total = old_total * factor + jnp.sum(weights, axis=1)
        rounded = weights.astype(jnp.bfloat16)
        new_mixed = old_mixed * factor[:, None] + jnp.dot(
            rounded, value_head, preferred_element_type=jnp.float32
        )
        return (new_top, new_total, new_mixed)

    final_top, final_total, final_mixed = lax.map(
        one_head, (query_heads, key_heads, value_heads, keep, start_top, start_total, start_mixed)
    )
    results = (final_mixed / final_total[:, :, None]).astype(jnp.bfloat16)
    joined = results.transpose(1, 0, 2).reshape(local_rows, heads_here * HEAD_DIM)
    return lax.all_to_all(joined, "panel", split_axis=0, concat_axis=1, tiled=True)


def solution(mesh):
    return jax.shard_map(
        shards,
        mesh=mesh,
        in_specs=(
            P(("groups", "seq"), "panel"),
            P(("groups", "seq"), "panel"),
            P(("groups", "seq"), "panel"),
            P("panel", None, None),
            P("panel", None),
        ),
        out_specs=P(("groups", "seq", "panel"), None),
        check_vma=False,
    )
```

profile of v0, /device:TPU:0, one launch (start us, length us, event | category | flops | bytes accessed | tf_op | source)
XLA Modules:
  0.0 240.1 jit_solution(3011953316735453202)
XLA Ops:
  6.5 2.4 %copy.37 = bf16[256,1536]{0,1:T(8,128)(2,1)} copy(bf16[256,1536]{1,0:T(8,128)(2,1)} %param.8) | data formatting | bytes 1572864 | tf_op args[1]
  9.0 1.2 copy.38
  11.1 65.9 %all-gather.3.cloned.1.call-done = bf16[2048,1536]{0,1:T(8,128)(2,1)} async-done(((bf16[256,1536]{0,1:T(8,128)(2,1)}), bf16[2048,1536]{0,1:T(8,128)(2,1)}) %all-gather.3.cloned.1.call-update) | async-done | bytes 6291472 | tf_op jit(solution)/shard_map/all_gather | solution.py:24
  77.1 64.9 %all-gather.5.cloned.1.call-done = bf16[2048,1536]{0,1:T(8,128)(2,1)} async-done(((bf16[256,1536]{0,1:T(8,128)(2,1)}), bf16[2048,1536]{0,1:T(8,128)(2,1)}) %all-gather.5.cloned.1.call-update) | async-done | bytes 6291472 | tf_op jit(solution)/shard_map/all_gather | solution.py:25
  142.0 73.7 %while.12 = (s32[]{:T(128)}, f32[12,256]{1,0:T(8,128)S(1)}, f32[12,256,128]{2,1,0:T(8,128)}, pred[12,2,16]{2,1,0:T(4,128)(4,1)S(1)}, bf16[12,256,128]{1,2,0:T(8,...) while((s32[]{:T(128)}, f32[12,256]{1,0:T(8,128)S(1)}, ...), condition=%wide.region_4.5_spmd, body=%wide.region_1.4_spmd.sunk | while | flops 273187584 | bytes 9657549 | solution.py:54
  142.0 1.3 broadcast_in_dim.39
  143.3 1.8 fusion.28
  145.1 0.6 fusion.29
  145.8 2.4 fusion.30
  148.2 1.3 broadcast_in_dim.39
  149.5 1.8 fusion.28
  151.2 0.6 fusion.29
  151.9 2.4 fusion.30
  154.3 1.3 broadcast_in_dim.39
  155.6 1.8 fusion.28
  157.4 0.6 fusion.29
  158.1 2.4 fusion.30
  160.4 1.3 broadcast_in_dim.39
  161.7 1.8 fusion.28
  164.2 2.4 fusion.30
  166.6 1.3 broadcast_in_dim.39
  167.9 1.8 fusion.28
  170.4 2.4 fusion.30
  172.7 1.3 broadcast_in_dim.39
  174.0 1.8 fusion.28
  176.5 2.4 fusion.30
  178.9 1.3 broadcast_in_dim.39
  180.2 1.8 fusion.28
  182.7 2.4 fusion.30
  185.0 1.3 broadcast_in_dim.39
  186.3 1.8 fusion.28
  188.8 2.4 fusion.30
  191.2 1.3 broadcast_in_dim.39
  192.5 1.8 fusion.28
  195.0 2.4 fusion.30
  197.3 1.3 broadcast_in_dim.39
  198.6 1.8 fusion.28
  200.4 0.6 fusion.29
  201.1 2.4 fusion.30
  203.5 1.3 broadcast_in_dim.39
  204.8 1.8 fusion.28
  207.2 2.4 fusion.30
  209.6 1.3 broadcast_in_dim.39
  210.9 1.8 fusion.28
  213.4 2.4 fusion.30
  215.7 1.9 fusion.17
  218.2 13.9 %all_to_all.19 = bf16[2,128,1536]{1,2,0:T(8,128)(2,1)S(1)} all-to-all(bf16[2,128,1536]{1,2,0:T(8,128)(2,1)S(1)} %copy.43), channel_id=1, replica_groups=mesh['groups'=2,'seq'=8,'panel'=2] {'panel'}, dimensions={0} | all-to-all | bytes 1572864 | tf_op jit(solution)/shard_map/all_to_all | solution.py:59
  232.1 1.2 copy.44
  (91 shorter events, 7.6 us)
Async XLA Ops:
  6.5 3.8 %copy-start = (s32[12,16,8]{1,2,0:T(8,128)S(1)}, s32[12,16,8]{1,2,0:T(8,128)}, u32[]{:S(2)}) copy-start(s32[12,16,8]{1,2,0:T(8,128)} %param.10) | copy-start | bytes 18436
  6.5 2.5 %copy-start.1 = (bf16[256,1536]{1,0:T(8,128)(2,1)S(1)}, bf16[256,1536]{1,0:T(8,128)(2,1)}, u32[]{:S(2)}) copy-start(bf16[256,1536]{1,0:T(8,128)(2,1)} %param.9) | copy-start | bytes 2359300
  6.5 4.0 %copy-start.2 = (bf16[256,1536]{1,0:T(8,128)(2,1)S(1)}, bf16[256,1536]{1,0:T(8,128)(2,1)}, u32[]{:S(2)}) copy-start(bf16[256,1536]{1,0:T(8,128)(2,1)} %param.7) | copy-start | bytes 2359300
  6.5 70.5 %all-gather.3.cloned.1.call-start = ((), (), s32[]{:S(2)}) async-start(), calls=%async_computation.1 | async-start | bytes 7077888 | tf_op jit(solution)/shard_map/all_gather | solution.py:24
  9.0 1.8 copy-start.3
  9.0 133.0 %all-gather.5.cloned.1.call-start = ((), (), s32[]{:S(2)}) async-start(), calls=%async_computation.2 | async-start | bytes 7077888 | tf_op jit(solution)/shard_map/all_gather | solution.py:25
Sparse Core Ops, SparseCore 0:
  9.1 67.9 all-gather.2
  78.6 63.3 all-gather.4
where the time goes:
time: 241 us; the launch traced here: 240 us
  waiting for transfers between devices  131 us (54%)
  matrix products  49.4 us (20%)
  local copies, waits for them, and re-layouts  22.1 us (9%)
  blocking collectives  13.9 us (6%)
  between operations  13.5 us (6%)
  other arithmetic  10.1 us (4%)
    all_gather x1, waiting for transfers between devices, shards(): key_piece = lax.all_gather(key_rows, 'seq', axis=0, tiled=True)  65.9 us
    all_gather x1, waiting for transfers between devices, shards(): value_piece = lax.all_gather(value_rows, 'seq', axis=0, tiled=True)  64.9 us
    dot_general x12, matrix products, one_head(): jnp.dot(rounded, value_head, preferred_element_type=jnp.float32)  28.3 us
    dot_general x12, matrix products, one_head(): lax.dot_general(query_head, key_head, (((1,), (1,)), ((), ())), preferred...  21.1 us
    broadcast_in_dim x24, local copies, waits for them, and re-layouts, one_head(): mask = jnp.repeat(jnp.repeat(keep_head, BLOCK, axis=0), BLOCK, axis=1)  15.6 us
    all_to_all x1, blocking collectives, shards(): lax.all_to_all(joined, 'panel', split_axis=0, concat_axis=1, tiled=True)  13.9 us
    reduce_sum x12, other arithmetic, one_head(): new_total = old_total * factor + jnp.sum(weights, axis=1)  7.78 us
  transfers between devices with their start and end apart: 2, of which 2 were waited for; matrix products, arithmetic and copies ran while one was open for 1% of the time, Pallas kernels for 0%

commit v1 on v0

v1 whole, which is shorter than its diff:
```python
import functools

import jax
import jax.numpy as jnp
from jax import lax
from jax.experimental import pallas as pl
from jax.experimental.pallas import tpu as pltpu
from jax.sharding import PartitionSpec as P

HEAD_DIM = 128
BLOCK = 128
LOG2_E = 1.4426950408889634
DEAD = -1e30


def tables(block_lists, block_counts, owner, seq_size):
    heads, tiles, listed = block_lists.shape
    per_index = tiles // seq_size
    lists = lax.dynamic_slice_in_dim(block_lists, owner * per_index, per_index, 1)
    counts = lax.dynamic_slice_in_dim(block_counts, owner * per_index, per_index, 1)
    slot_live = jnp.arange(listed, dtype=jnp.int32) < counts[:, :, None]
    ids = jnp.arange(tiles, dtype=jnp.int32)
    hits = (lists[:, :, :, None] == ids) & slot_live[:, :, :, None]
    keep = jnp.any(hits, axis=2).astype(jnp.int32).reshape(heads, per_index, seq_size, per_index)
    low, high = keep[..., 0], keep[..., 1]
    taken = jnp.max(high, axis=1)
    live = jnp.where(taken[:, None, :] == 1, high, low)
    other = jnp.where(taken[:, None, :] == 1, low, high)
    bits = jnp.array([2 << tile for tile in range(per_index)], jnp.int32)[None, :, None]
    code = taken + jnp.sum(live * bits, axis=1)
    code_other = (1 - taken) + jnp.sum(other * bits, axis=1)
    mine = jnp.arange(seq_size) == owner
    extra = jnp.sum(jnp.where(mine, code_other, 0), axis=1, keepdims=True)
    return jnp.concatenate([code, extra], axis=1)


def attend(query, codes, key_block, value_block):
    rows = query.shape[0]
    factor = HEAD_DIM ** (-0.5) * LOG2_E
    masked = []
    for j, code in enumerate(codes):
        scores = lax.dot_general(
            query, key_block(j, code & 1), (((1,), (1,)), ((), ())), preferred_element_type=jnp.float32
        )
        parts = []
        for tile in range(rows // BLOCK):
            bias = jnp.where((code >> (tile + 1)) & 1 == 1, 0.0, DEAD).astype(jnp.float32)
            parts.append(scores[tile * BLOCK : (tile + 1) * BLOCK] * factor + bias)
        masked.append(jnp.concatenate(parts, axis=0))
    top = jnp.max(functools.reduce(jnp.maximum, masked), axis=1, keepdims=True)
    total, mixed = None, None
    for j, code in enumerate(codes):
        weights = jnp.exp2(masked[j] - top)
        total = weights if total is None else total + weights
        product = jnp.dot(
            weights.astype(jnp.bfloat16), value_block(j, code & 1), preferred_element_type=jnp.float32
        )
        mixed = product if mixed is None else mixed + product
    return mixed / jnp.sum(total, axis=1, keepdims=True)


def gathered_kernel(seq_size, own_rows, info_ref, code_ref, query_ref, key_ref, value_ref, out_ref):
    head = pl.program_id(0)
    owner = info_ref[0]

    def block(ref):
        def read(j, which):
            index = owner if j == seq_size else j
            return ref[pl.ds(pl.multiple_of(index * own_rows + which * BLOCK, BLOCK), BLOCK), :]

        return read

    codes = [code_ref[head * (seq_size + 1) + j] for j in range(seq_size + 1)]
    out_ref[...] = attend(query_ref[...], codes, block(key_ref), block(value_ref)).astype(out_ref.dtype)


def gathered(queries, key_rows, value_rows, block_lists, block_counts, seq_size):
    rows, width = queries.shape
    heads = width // HEAD_DIM
    position = lax.axis_index("seq")
    keys = lax.all_gather(key_rows, "seq", axis=0, tiled=True)
    values = lax.all_gather(value_rows, "seq", axis=0, tiled=True)
    codes = tables(block_lists, block_counts, position, seq_size).reshape(-1)
    all_rows = keys.shape[0]
    out = pl.pallas_call(
        functools.partial(gathered_kernel, seq_size, rows),
        out_shape=jax.ShapeDtypeStruct((rows, width), queries.dtype),
        grid_spec=pltpu.PrefetchScalarGridSpec(
            num_scalar_prefetch=2,
            grid=(heads,),
            in_specs=[
                pl.BlockSpec((rows, HEAD_DIM), lambda h, *_: (0, h)),
                pl.BlockSpec((all_rows, HEAD_DIM), lambda h, *_: (0, h)),
                pl.BlockSpec((all_rows, HEAD_DIM), lambda h, *_: (0, h)),
            ],
            out_specs=pl.BlockSpec((rows, HEAD_DIM), lambda h, *_: (0, h)),
        ),
        name="attend_gathered",
    )(position.reshape(1), codes, queries, keys, values)
    return lax.all_to_all(out, "panel", split_axis=0, concat_axis=1, tiled=True)


def solution(mesh):
    seq_size = mesh.shape["seq"]
    return jax.shard_map(
        functools.partial(gathered, seq_size=seq_size),
        mesh=mesh,
        in_specs=(
            P(("groups", "seq"), "panel"),
            P(("groups", "seq"), "panel"),
            P(("groups", "seq"), "panel"),
            P("panel", None, None),
            P("panel", None),
        ),
        out_specs=P(("groups", "seq", "panel"), None),
        check_vma=False,
    )
```

time: 241 us -> 181 us (0.75)
  matrix products: 49.4 us -> 0 us
  local copies, waits for them, and re-layouts: 22.1 us -> 2.81 us
  Pallas kernels: 0 us -> 16.4 us
  other arithmetic: 10.1 us -> 1.1 us
    dot_general x24 -> x0, matrix products: 49.4 us -> none  [the longest x12 28.3 us: one_head(): jnp.dot(rounded, value_head, preferred_element_type=jnp.float32)]
    pallas_call x0 -> x1, Pallas kernels: none -> 16.4 us  [gathered(): pl.pallas_call(functools.partial(gathered_kernel, seq_size, rows), out_sh...]
    broadcast_in_dim x24 -> x0, local copies, waits for them, and re-layouts: 15.6 us -> none  [one_head(): mask = jnp.repeat(jnp.repeat(keep_head, BLOCK, axis=0), BLOCK, axis=1)]
    reduce_sum x12 -> x1, other arithmetic: 7.78 us -> 0.73 us  [tables(): code = taken + jnp.sum(live * bits, axis=1)]
    unnamed x11 -> x2, local copies, waits for them, and re-layouts: 3.9 us -> 0.01 us
  transfers between devices with their start and end apart: 2 -> 2, of which waited for: 2 -> 2; matrix products, arithmetic and copies ran while one was open for 1% -> 2% of each run, Pallas kernels for 0% -> 0%
where the time goes in v1:
time: 181 us
  waiting for transfers between devices  132 us (73%)
  Pallas kernels  16.4 us (9%)
  blocking collectives  15 us (8%)
  between operations  13.4 us (7%)
  local copies, waits for them, and re-layouts  2.81 us (2%)
    all_gather x1, waiting for transfers between devices, gathered(): keys = lax.all_gather(key_rows, 'seq', axis=0, tiled=True)  65.4 us
    all_gather x1, waiting for transfers between devices, gathered(): values = lax.all_gather(value_rows, 'seq', axis=0, tiled=True)  65 us
    pallas_call x1, Pallas kernels, gathered(): pl.pallas_call(functools.partial(gathered_kernel, seq_size, rows), out_sh...  16.4 us
    all_to_all x1, blocking collectives, gathered(): return lax.all_to_all(out, 'panel', split_axis=0, concat_axis=1, tiled=True)  15 us
  transfers between devices with their start and end apart: 2, of which 2 were waited for; matrix products, arithmetic and copies ran while one was open for 2% of the time, Pallas kernels for 0%

profile of v1, /device:TPU:0, one launch (start us, length us, event | category | flops | bytes accessed | tf_op | source)
XLA Modules:
  0.0 180.6 jit_solution(1264324695965978644)
XLA Ops:
  6.5 0.0 copy-start
  6.5 0.0 all-gather.3.cloned.1.call-start
  6.5 0.7 all-gather.3.cloned.1.call-update
  7.3 0.0 all-gather.5.cloned.1.call-start
  7.3 0.7 all-gather.5.cloned.1.call-update
  8.0 0.0 copy-done
  8.0 0.1 constant_dynamic-slice_fusion.1
  8.1 0.1 copy.18
  8.2 0.8 constant_dynamic-slice_fusion
  9.0 0.1 iota_compare_fusion.1
  9.1 0.1 fusion.1
  9.3 0.1 copy.19
  9.4 0.7 multiply_reduce_fusion.1
  10.1 0.1 fusion.2
  10.2 0.1 copy.20
  10.3 0.7 reshape.24.code_ref
  11.0 65.4 %all-gather.3.cloned.1.call-done.key_ref = bf16[2048,1536]{1,0:T(8,128)(2,1)} async-done(((bf16[256,1536]{1,0:T(8,128)(2,1)}), bf16[2048,1536]{1,0:T(8,128)(2,1)}) %all-gather.3.cloned.1.call-update) | async-done | bytes 6291472 | tf_op jit(solution)/shard_map/all_gather | solution.py:81
  76.4 65.0 %all-gather.5.cloned.1.call-done.value_ref = bf16[2048,1536]{1,0:T(8,128)(2,1)} async-done(((bf16[256,1536]{1,0:T(8,128)(2,1)}), bf16[2048,1536]{1,0:T(8,128)(2,1)}) %all-gather.5.cloned.1.call-update) | async-done | bytes 6291472 | tf_op jit(solution)/shard_map/all_gather | solution.py:82
  141.4 16.4 %attend_gathered.1 = bf16[256,1536]{1,0:T(8,128)(2,1)} custom-call(s32[1]{0:T(128)} %bitcast.info_ref, s32[108]{0:T(128)} %reshape.24.code_ref, bf16[256,1536]{1,0:T(8,128)(2,1)} %query_ref.1, bf16[2048,1536]{1,0:T(8,128)(2,1)} %all-gather.3.cloned.1.call-done.key_ref, bf16[2048,1536]{1,0:T(8,128)(2,1)} %all-gather.5.cloned.1.call-done.value_ref), custom_call_target="tpu_custom_call" | custom-call | tf_op jit(solution)/shard_map/attend_gathered/pallas_call | solution.py:85
  157.8 15.0 %all_to_all.19 = bf16[2,128,1536]{2,1,0:T(8,128)(2,1)S(1)} all-to-all(bf16[2,128,1536]{2,1,0:T(8,128)(2,1)} %bitcast.9), channel_id=1, replica_groups=mesh['groups'=2,'seq'=8,'panel'=2] {'panel'}, dimensions={0} | all-to-all | bytes 1572864 | tf_op jit(solution)/shard_map/all_to_all | solution.py:100
  172.8 1.0 copy.22
  (5 shorter events, 0.1 us)
Async XLA Ops:
  6.5 1.5 copy-start
  6.5 69.9 %all-gather.3.cloned.1.call-start = ((), (), s32[]{:S(2)}) async-start(), calls=%async_computation.1 | async-start | bytes 7077888 | tf_op jit(solution)/shard_map/all_gather | solution.py:81
  7.3 134.2 %all-gather.5.cloned.1.call-start = ((), (), s32[]{:S(2)}) async-start(), calls=%async_computation.2 | async-start | bytes 7077888 | tf_op jit(solution)/shard_map/all_gather | solution.py:82
Sparse Core Ops, SparseCore 0:
  9.0 67.4 all-gather.2
  78.1 63.3 all-gather.4

commit v2 on v1

--- a/solution.py
+++ b/solution.py
@@ -7,10 +7,14 @@
 from jax.experimental.pallas import tpu as pltpu
 from jax.sharding import PartitionSpec as P
 
+
 HEAD_DIM = 128
 BLOCK = 128
 LOG2_E = 1.4426950408889634
 DEAD = -1e30
+CORES = 2
+CHUNKS = 3
+VMEM_GRANT = 12 << 20
 
 
 def tables(block_lists, block_counts, owner, seq_size):
@@ -100,10 +104,219 @@
     return lax.all_to_all(out, "panel", split_axis=0, concat_axis=1, tiled=True)
 
 
+def pieces_of(seq_pairs, panel_size, shift):
+    return [
+        (source * panel_size + panel, target * panel_size + (panel + shift) % panel_size)
+        for source, target in seq_pairs
+        for panel in range(panel_size)
+    ]
+
+
+def send(value, pairs, axes="seq"):
+    return lax.ppermute(value, axes, pairs)
+
+
+def pack_kernel(starts, sizes, key_ref, value_ref, *refs):
+    outs, sems = refs[:-1], refs[-1]
+    rows = key_ref.shape[0]
+    copies = []
+    for k, (start, size) in enumerate(zip(starts, sizes)):
+        columns = pl.ds(start * HEAD_DIM, size * HEAD_DIM)
+        for kind, ref in enumerate((key_ref, value_ref)):
+            copies.append(
+                pltpu.make_async_copy(ref.at[:, columns], outs[k].at[pl.ds(kind * rows, rows), :], sems.at[k, kind])
+            )
+            copies[-1].start()
+    for copy in copies:
+        copy.wait()
+
+
+def relayed_kernel(seq_size, panel_size, heads, start, size, *refs):
+    info_ref, code_ref, own_query, guest_query = refs[:4]
+    whole = refs[4:10]
+    stacked = refs[10:15]
+    own_out = refs[15 : 15 + panel_size]
+    guest_out = refs[15 + panel_size : 15 + 2 * panel_size]
+    held = refs[-1]
+    panel = info_ref[1]
+    rows = own_query.shape[0]
+    piece = rows // panel_size
+
+    def unit(h, side, spot):
+        query, home, outs = ((own_query, 0, own_out), (guest_query, 4, guest_out))[side]
+        local = pl.ds(pl.multiple_of(h * HEAD_DIM, HEAD_DIM), HEAD_DIM)
+        full = pl.ds(pl.multiple_of((h + start) * HEAD_DIM, HEAD_DIM), HEAD_DIM)
+
+        def read(kind):
+            def block(j, which):
+                slot = home if j == seq_size else j
+                if 1 <= slot <= 3:
+                    ref, first, columns = whole[2 * (slot - 1) + kind], 0, full
+                else:
+                    ref, first, columns = stacked[slot - 3 if slot else 0], kind * rows, local
+                return ref[pl.ds(pl.multiple_of(first + which * BLOCK, BLOCK), BLOCK), columns]
+
+            return block
+
+        first = (side * heads + h + start) * (seq_size + 1)
+        codes = [code_ref[first + j] for j in range(seq_size + 1)]
+        result = attend(query[:, full], codes, read(0), read(1))
+        held[spot] = result
+        for shift in range(panel_size):
+            first_row = pl.multiple_of(lax.rem(panel + shift, panel_size) * piece, piece)
+            outs[shift][:, local] = held[spot, pl.ds(first_row, piece), :].astype(outs[shift].dtype)
+
+    @pl.when(info_ref[0] == 1)
+    def _():
+        if size > 1:
+
+            @pl.loop(0, size // 2)
+            def _(pair):
+                for h in range(2):
+                    for side in range(2):
+                        unit(pair * 2 + h, side, h * 2 + side)
+
+        for h in range(size - size % 2, size):
+            for side in range(2):
+                unit(h, side, side)
+
+
+def assemble_kernel(panel_size, starts, sizes, aliased, info_ref, *refs):
+    out_ref, sems = refs[-2:]
+    refs = refs[1:] if aliased else refs
+    count = len(sizes)
+    width = out_ref.shape[1] // panel_size
+    panel = info_ref[1]
+    inner = info_ref[0] == 1
+    copies = []
+    for shift in range(panel_size):
+        source = lax.rem(panel + panel_size - shift, panel_size)
+        for chunk, (start, size) in enumerate(zip(starts, sizes)):
+            columns = pl.ds(pl.multiple_of(source * width + start * HEAD_DIM, HEAD_DIM), size * HEAD_DIM)
+            own, guest = (
+                pltpu.make_async_copy(
+                    refs[(side * count + chunk) * panel_size + shift],
+                    out_ref.at[:, columns],
+                    sems.at[shift, chunk],
+                )
+                for side in range(2)
+            )
+            pl.when(inner)(own.start)
+            pl.when(jnp.logical_not(inner))(guest.start)
+            copies.append(own)
+    for copy in copies:
+        copy.wait()
+
+
+def relayed(queries, key_rows, value_rows, block_lists, block_counts, seq_size, panel_size):
+    rows, width = queries.shape
+    heads = width // HEAD_DIM
+    chips = seq_size // CORES
+    position = lax.axis_index("seq")
+    panel = lax.axis_index("panel")
+    chip, core = position // CORES, position % CORES
+    last = chips - 1
+    cores = range(CORES)
+    inward = [(source * CORES + c, target * CORES + c) for source, target in ((0, 1), (last, last - 1)) for c in cores]
+    across = [(source * CORES + c, target * CORES + c) for source, target in ((1, 2), (2, 1)) for c in cores]
+    partner = [(z * CORES + c, z * CORES + CORES - 1 - c) for z in (1, 2) for c in cores]
+    inner = [(z * CORES + c, z * CORES + c) for z in (1, 2) for c in cores]
+    outward = [(target, source) for source, target in inward]
+    in_vmem, in_smem, anywhere = (pl.BlockSpec(memory_space=s) for s in (pltpu.VMEM, pltpu.SMEM, pl.ANY))
+
+    chunks = min(CHUNKS, heads)
+    starts = [heads * k // chunks for k in range(chunks)]
+    sizes = [heads * (k + 1) // chunks - heads * k // chunks for k in range(chunks)]
+
+    middle = [send(x, across) for x in (key_rows, value_rows)]
+    packed = pl.pallas_call(
+        functools.partial(pack_kernel, starts, sizes),
+        out_shape=[jax.ShapeDtypeStruct((2 * rows, size * HEAD_DIM), key_rows.dtype) for size in sizes],
+        in_specs=[anywhere] * 2,
+        out_specs=[in_vmem] * chunks,
+        scratch_shapes=[pltpu.SemaphoreType.DMA((chunks, 2))],
+        compiler_params=pltpu.CompilerParams(vmem_limit_bytes=VMEM_GRANT),
+        name="pack",
+    )(key_rows, value_rows)
+    beside = [send(x, partner) for x in (key_rows, value_rows)]
+    ends = [send(x, inward) for x in packed]
+    guest_query = send(queries, inward)
+    middle_beside = [send(x, partner) for x in middle]
+
+    is_inner = (chip >= 1) & (chip < last)
+    end = jnp.where(chip * 2 < chips, 0, last)
+    guest = end * CORES + core
+    order = jnp.stack(
+        [
+            z * CORES + c
+            for z in (chip, last - chip, end, last - end)
+            for c in (core, CORES - 1 - core)
+        ]
+    )
+    pick = (order[:, None] == jnp.arange(seq_size)).astype(jnp.int32)
+
+    def arranged(owner):
+        codes = tables(block_lists, block_counts, owner, seq_size)
+        return jnp.concatenate([jnp.sum(codes[:, None, :seq_size] * pick, axis=2), codes[:, seq_size:]], axis=1)
+
+    codes = jnp.stack([arranged(position), arranged(guest)]).reshape(-1)
+    info = jnp.stack([is_inner.astype(jnp.int32), panel])
+
+    own_pieces, guest_pieces = [], []
+    for k, (start, size) in enumerate(zip(starts, sizes)):
+        far = send(ends[k], across)
+        ends_beside = send(ends[k], partner)
+        far_beside = send(far, partner)
+        stacked = [packed[k], ends[k], ends_beside, far, far_beside]
+        outs = pl.pallas_call(
+            functools.partial(relayed_kernel, seq_size, panel_size, heads, start, size),
+            out_shape=[jax.ShapeDtypeStruct((rows // panel_size, size * HEAD_DIM), queries.dtype)] * (2 * panel_size),
+            in_specs=[in_smem] * 2 + [in_vmem] * 13,
+            out_specs=[in_vmem] * (2 * panel_size),
+            scratch_shapes=[pltpu.VMEM((4, rows, HEAD_DIM), jnp.float32)],
+            compiler_params=pltpu.CompilerParams(vmem_limit_bytes=VMEM_GRANT),
+            cost_estimate=pl.CostEstimate(
+                flops=size * 8 * rows * (seq_size + 1) * BLOCK * HEAD_DIM,
+                bytes_accessed=size * HEAD_DIM * 2 * rows * 20,
+                transcendentals=size * 2 * rows * (seq_size + 1) * BLOCK,
+            ),
+        )(info, codes, queries, guest_query, *beside, *middle, *middle_beside, *stacked)
+        both = ("seq", "panel")
+        for shift in range(panel_size):
+            mine, theirs = outs[shift], outs[panel_size + shift]
+            if shift:
+                mine = send(mine, pieces_of(inner, panel_size, shift), both)
+            own_pieces.append(mine)
+            guest_pieces.append(send(theirs, pieces_of(outward, panel_size, shift), both))
+
+    split = (chunks - 1) * panel_size
+    out = None
+    for lo, hi, first, final in ((0, split, 0, chunks - 1), (split, chunks * panel_size, chunks - 1, chunks)):
+        if lo == hi:
+            continue
+        pieces = own_pieces[lo:hi] + guest_pieces[lo:hi]
+        before = [] if out is None else [out]
+        out = pl.pallas_call(
+            functools.partial(assemble_kernel, panel_size, starts[first:final], sizes[first:final], len(before)),
+            out_shape=jax.ShapeDtypeStruct((rows // panel_size, width * panel_size), queries.dtype),
+            in_specs=[in_smem] + [anywhere] * len(before) + [in_vmem] * len(pieces),
+            out_specs=anywhere,
+            scratch_shapes=[pltpu.SemaphoreType.DMA((panel_size, final - first))],
+            input_output_aliases={1: 0} if before else {},
+            compiler_params=pltpu.CompilerParams(vmem_limit_bytes=VMEM_GRANT),
+        )(info, *before, *pieces)
+    return out
+
+
 def solution(mesh):
-    seq_size = mesh.shape["seq"]
+    seq_size, panel_size = mesh.shape["seq"], mesh.shape["panel"]
+    relay = seq_size // CORES - 2 == 2
+    if relay:
+        body = functools.partial(relayed, seq_size=seq_size, panel_size=panel_size)
+    else:
+        body = functools.partial(gathered, seq_size=seq_size)
     return jax.shard_map(
-        functools.partial(gathered, seq_size=seq_size),
+        body,
         mesh=mesh,
         in_specs=(
             P(("groups", "seq"), "panel"),

time: 181 us -> 149 us (0.82)
  waiting for transfers between devices: 132 us -> 80.8 us
  starting transfers between devices: 0.04 us -> 47.5 us
  blocking collectives: 15 us -> 0 us
  between operations: 13.4 us -> 0.35 us
  Pallas kernels: 16.4 us -> 10.5 us
  local copies, waits for them, and re-layouts: 2.81 us -> 7.8 us
    all_gather x2 -> x0, waiting for transfers between devices: 130 us -> none  [the longest x1 65.4 us: gathered(): keys = lax.all_gather(key_rows, 'seq', axis=0, tiled=True)]
    ppermute x0 -> x28, waiting for transfers between devices: none -> 80.8 us  [send(): return lax.ppermute(value, axes, pairs)]
    ppermute x0 -> x28, starting transfers between devices: none -> 47.5 us  [send(): return lax.ppermute(value, axes, pairs)]
    all_to_all x1 -> x0, blocking collectives: 15 us -> none  [gathered(): return lax.all_to_all(out, 'panel', split_axis=0, concat_axis=1, tiled=True)]
    unnamed x2 -> x20, local copies, waits for them, and re-layouts: 0.01 us -> 6.81 us
    pallas_call x1 -> x6, Pallas kernels: 16.4 us -> 10.5 us  [the longest x3 6.51 us: relayed(): pl.pallas_call(functools.partial(relayed_kernel, seq_size, panel_size, he...]
  transfers between devices with their start and end apart: 2 -> 28, of which waited for: 2 -> 10; matrix products, arithmetic and copies ran while one was open for 2% -> 1% of each run, Pallas kernels for 0% -> 6%
where the time goes in v2:
time: 149 us; the launch traced here: 148 us
  waiting for transfers between devices  80.8 us (54%)
  starting transfers between devices  47.5 us (32%)
  Pallas kernels  10.5 us (7%)
  local copies, waits for them, and re-layouts  7.8 us (5%)
    ppermute x28, waiting for transfers between devices, send(): return lax.ppermute(value, axes, pairs)  80.8 us
    ppermute x28, starting transfers between devices, send(): return lax.ppermute(value, axes, pairs)  47.5 us
    unnamed x20, local copies, waits for them, and re-layouts  6.81 us
    pallas_call x3, Pallas kernels, relayed(): pl.pallas_call(functools.partial(relayed_kernel, seq_size, panel_size, he...  6.51 us
  transfers between devices with their start and end apart: 28, of which 10 were waited for; matrix products, arithmetic and copies ran while one was open for 1% of the time, Pallas kernels for 6%

profile of v2, /device:TPU:0, one launch (start us, length us, event | category | flops | bytes accessed | tf_op | source)
XLA Modules:
  0.0 147.9 jit_solution(2283994489070096181)
XLA Ops:
  0.0 0.8 collective-permute-start.1
  0.8 0.7 collective-permute-start.3
  1.6 1.1 copy-done.5
  2.7 1.1 copy-done.6
  3.8 1.3 pack.1
  5.2 9.8 %collective-permute-start.7 = (bf16[512,512]{1,0:T(8,128)(2,1)}, bf16[512,512]{1,0:T(8,128)(2,1)}, u32[]{:S(2)}, u32[]{:S(2)}) collective-permute-start(bf16[512,512]{1,0:T(8,128)(2,1)} %get-tuple-element.20.refs_10_), channel_id=1, source_target_pairs={{0,4},{2,6},{12,8},{14,10},{1,5},{3,7},{13,9},{15,11},{16,20},{18,... | collective-permute-start | bytes 1572872 | tf_op jit(solution)/shard_map/ppermute | solution.py:116
  14.9 2.1 %collective-permute-start.12 = (bf16[512,512]{1,0:T(8,128)(2,1)}, bf16[512,512]{1,0:T(8,128)(2,1)}, u32[]{:S(2)}, u32[]{:S(2)}) collective-permute-start(bf16[512,512]{1,0:T(8,128)(2,1)} %get-tuple-element.23.refs_10_), channel_id=1, source_target_pairs={{0,4},{2,6},{12,8},{14,10},{1,5},{3,7},{13,9},{15,11},{16,20},{18,... | collective-permute-start | bytes 1572872 | tf_op jit(solution)/shard_map/ppermute | solution.py:116
  17.0 2.1 %collective-permute-start.21 = (bf16[512,512]{1,0:T(8,128)(2,1)}, bf16[512,512]{1,0:T(8,128)(2,1)}, u32[]{:S(2)}, u32[]{:S(2)}) collective-permute-start(bf16[512,512]{1,0:T(8,128)(2,1)} %get-tuple-element.30.refs_10_), channel_id=1, source_target_pairs={{0,4},{2,6},{12,8},{14,10},{1,5},{3,7},{13,9},{15,11},{16,20},{18,... | collective-permute-start | bytes 1572872 | tf_op jit(solution)/shard_map/ppermute | solution.py:116
  19.1 0.7 copy-done.8
  21.0 5.8 %collective-permute-done.7.refs_11_ = bf16[512,512]{1,0:T(8,128)(2,1)} collective-permute-done((bf16[512,512]{1,0:T(8,128)(2,1)}, bf16[512,512]{1,0:T(8,128)(2,1)}, u32[]{:S(2)}, u32[]{:S(2)}) %collective-permute-start.7) | collective-permute-done | bytes 524320 | tf_op jit(solution)/shard_map/ppermute | solution.py:116
  26.7 0.7 collective-permute-start.2
  27.5 10.5 %collective-permute-done.12.refs_11_ = bf16[512,512]{1,0:T(8,128)(2,1)} collective-permute-done((bf16[512,512]{1,0:T(8,128)(2,1)}, bf16[512,512]{1,0:T(8,128)(2,1)}, u32[]{:S(2)}, u32[]{:S(2)}) %collective-permute-start.12) | collective-permute-done | bytes 524320 | tf_op jit(solution)/shard_map/ppermute | solution.py:116
  38.0 0.7 collective-permute-start.4
  38.7 9.8 %collective-permute-done.21.refs_11_ = bf16[512,512]{1,0:T(8,128)(2,1)} collective-permute-done((bf16[512,512]{1,0:T(8,128)(2,1)}, bf16[512,512]{1,0:T(8,128)(2,1)}, u32[]{:S(2)}, u32[]{:S(2)}) %collective-permute-start.21) | collective-permute-done | bytes 524320 | tf_op jit(solution)/shard_map/ppermute | solution.py:116
  48.5 4.4 %collective-permute-start = (bf16[256,1536]{1,0:T(8,128)(2,1)S(1)}, bf16[256,1536]{1,0:T(8,128)(2,1)S(1)}, u32[]{:S(2)}, u32[]{:S(2)}) collective-permute-start(bf16[256,1536]{1,0:T(8,128)(2,1)S(1)} %copy-done), channel_id=1, source_target_pairs={{0,4},{2,6},{12,8},{14,10},{1,5},{3,7},{13,9},{15,11},{16,20},{18,... | collective-permute-start | bytes 2359304 | tf_op jit(solution)/shard_map/ppermute | solution.py:116
  52.9 1.5 collective-permute-start.9
  55.1 1.5 %collective-permute-start.8 = (bf16[512,512]{1,0:T(8,128)(2,1)}, bf16[512,512]{1,0:T(8,128)(2,1)}, u32[]{:S(2)}, u32[]{:S(2)}) collective-permute-start(bf16[512,512]{1,0:T(8,128)(2,1)} %collective-permute-done.7.refs_11_), channel_id=1, source_target_pairs={{4,6},{6,4},{8,10},{10,8},{5,7},{7,5},{9,11},{11,9},{20,22},{22,20... | collective-permute-start | bytes 1572872 | tf_op jit(solution)/shard_map/ppermute | solution.py:116
  56.7 1.6 %collective-permute-start.5 = (bf16[256,1536]{1,0:T(8,128)(2,1)S(1)}, bf16[256,1536]{1,0:T(8,128)(2,1)}, u32[]{:S(2)}, u32[]{:S(2)}) collective-permute-start(bf16[256,1536]{1,0:T(8,128)(2,1)S(1)} %collective-permute-done.3.refs_6_), channel_id=1, source_target_pairs={{4,6},{6,4},{8,10},{10,8},{5,7},{7,5},{9,11},{11,9},{20,22},{22,20... | collective-permute-start | bytes 2359304 | tf_op jit(solution)/shard_map/ppermute | solution.py:116
  58.3 1.5 collective-permute-start.14
  59.8 9.4 %collective-permute-done.refs_3_ = bf16[256,1536]{1,0:T(8,128)(2,1)S(1)} collective-permute-done((bf16[256,1536]{1,0:T(8,128)(2,1)S(1)}, bf16[256,1536]{1,0:T(8,128)(2,1)S(1)}, u32[]{:S(2)}, u32[]{:S(2)}) %collective-permute-start) | collective-permute-done | bytes 786464 | tf_op jit(solution)/shard_map/ppermute | solution.py:116
  69.2 0.9 copy-done.3
  70.0 1.5 collective-permute-start.23
  71.5 1.5 collective-permute-start.10
  73.2 1.6 %collective-permute-start.6 = (bf16[256,1536]{1,0:T(8,128)(2,1)}, bf16[256,1536]{1,0:T(8,128)(2,1)}, u32[]{:S(2)}, u32[]{:S(2)}) collective-permute-start(bf16[256,1536]{1,0:T(8,128)(2,1)} %copy-done.1), channel_id=1, source_target_pairs={{4,6},{6,4},{8,10},{10,8},{5,7},{7,5},{9,11},{11,9},{20,22},{22,20... | collective-permute-start | bytes 2359304 | tf_op jit(solution)/shard_map/ppermute | solution.py:116
  74.9 1.5 collective-permute-start.13
  76.4 1.4 collective-permute-start.15
  77.8 1.5 %collective-permute-start.22 = (bf16[512,512]{1,0:T(8,128)(2,1)}, bf16[512,512]{1,0:T(8,128)(2,1)}, u32[]{:S(2)}, u32[]{:S(2)}) collective-permute-start(bf16[512,512]{1,0:T(8,128)(2,1)} %collective-permute-done.21.refs_11_), channel_id=1, source_target_pairs={{4,6},{6,4},{8,10},{10,8},{5,7},{7,5},{9,11},{11,9},{20,22},{22,20... | collective-permute-start | bytes 1572872 | tf_op jit(solution)/shard_map/ppermute | solution.py:116
  79.3 1.5 %collective-permute-start.24 = (bf16[512,512]{1,0:T(8,128)(2,1)}, bf16[512,512]{1,0:T(8,128)(2,1)}, u32[]{:S(2)}, u32[]{:S(2)}) collective-permute-start(bf16[512,512]{1,0:T(8,128)(2,1)} %collective-permute-done.23.refs_13_), channel_id=1, source_target_pairs={{4,6},{6,4},{8,10},{10,8},{5,7},{7,5},{9,11},{11,9},{20,22},{22,20... | collective-permute-start | bytes 1572872 | tf_op jit(solution)/shard_map/ppermute | solution.py:116
  81.3 1.1 copy-done.2
  82.4 1.1 copy-done.4
  83.5 2.2 %shard_map.73 = (bf16[128,512]{1,0:T(8,128)(2,1)S(1)}, bf16[128,512]{1,0:T(8,128)(2,1)S(1)}, bf16[128,512]{1,0:T(8,128)(2,1)S(1)}, bf16[128,512]{1,0:T(8,128)(2,1)S(1)}) custom-call(s32[2]{0:T(128)S(1)} %pad_add_fusion.3.refs_0_.info_ref, s32[216]{0:T(256)S(1)} %reshape.60.refs_1_, bf16[256,1536]{1,0:T(8,128)(2,1)S(1)} %copy-done, ...), custom_call_target="tpu_custom_call" | custom-call | flops 1207959552 | bytes 5242880 | tf_op jit(solution)/shard_map/pallas_call | solution.py:271
  85.7 0.7 collective-permute-start.11
  86.4 1.3 collective-permute-start.17
  87.7 1.3 collective-permute-start.18
  89.0 2.2 %shard_map.74 = (bf16[128,512]{1,0:T(8,128)(2,1)S(1)}, bf16[128,512]{1,0:T(8,128)(2,1)S(1)}, bf16[128,512]{1,0:T(8,128)(2,1)S(1)}, bf16[128,512]{1,0:T(8,128)(2,1)S(1)}) custom-call(s32[2]{0:T(128)S(1)} %pad_add_fusion.3.refs_0_.info_ref, s32[216]{0:T(256)S(1)} %reshape.60.refs_1_, bf16[256,1536]{1,0:T(8,128)(2,1)S(1)} %copy-done, ...), custom_call_target="tpu_custom_call" | custom-call | flops 1207959552 | bytes 5242880 | tf_op jit(solution)/shard_map/pallas_call | solution.py:271
  91.9 1.3 collective-permute-start.19
  93.2 2.2 %shard_map.76 = (bf16[128,512]{1,0:T(8,128)(2,1)S(1)}, bf16[128,512]{1,0:T(8,128)(2,1)S(1)}, bf16[128,512]{1,0:T(8,128)(2,1)S(1)}, bf16[128,512]{1,0:T(8,128)(2,1)S(1)}) custom-call(s32[2]{0:T(128)S(1)} %pad_add_fusion.3.refs_0_.info_ref, s32[216]{0:T(256)S(1)} %reshape.60.refs_1_, bf16[256,1536]{1,0:T(8,128)(2,1)S(1)} %copy-done, ...), custom_call_target="tpu_custom_call" | custom-call | flops 1207959552 | bytes 5242880 | tf_op jit(solution)/shard_map/pallas_call | solution.py:271
  95.4 1.3 collective-permute-start.20
  96.7 22.9 %collective-permute-done.17.refs_4_ = bf16[128,512]{1,0:T(8,128)(2,1)S(1)} collective-permute-done((bf16[128,512]{1,0:T(8,128)(2,1)S(1)}, bf16[128,512]{1,0:T(8,128)(2,1)S(1)}, u32[]{:S(2)}, u32[]{:S(2)}) %collective-permute-start.17) | collective-permute-done | bytes 131104 | tf_op jit(solution)/shard_map/ppermute | solution.py:116
  120.2 1.6 %collective-permute-done.18.refs_5_ = bf16[128,512]{1,0:T(8,128)(2,1)S(1)} collective-permute-done((bf16[128,512]{1,0:T(8,128)(2,1)S(1)}, bf16[128,512]{1,0:T(8,128)(2,1)S(1)}, u32[]{:S(2)}, u32[]{:S(2)}) %collective-permute-start.18) | collective-permute-done | bytes 131104 | tf_op jit(solution)/shard_map/ppermute | solution.py:116
  121.8 1.3 collective-permute-start.26
  123.1 1.3 collective-permute-start.27
  124.4 6.5 %collective-permute-done.19.refs_6_ = bf16[128,512]{1,0:T(8,128)(2,1)S(1)} collective-permute-done((bf16[128,512]{1,0:T(8,128)(2,1)S(1)}, bf16[128,512]{1,0:T(8,128)(2,1)S(1)}, u32[]{:S(2)}, u32[]{:S(2)}) %collective-permute-start.19) | collective-permute-done | bytes 131104 | tf_op jit(solution)/shard_map/ppermute | solution.py:116
  130.9 9.3 %collective-permute-done.20.refs_7_ = bf16[128,512]{1,0:T(8,128)(2,1)S(1)} collective-permute-done((bf16[128,512]{1,0:T(8,128)(2,1)S(1)}, bf16[128,512]{1,0:T(8,128)(2,1)S(1)}, u32[]{:S(2)}, u32[]{:S(2)}) %collective-permute-start.20) | collective-permute-done | bytes 131104 | tf_op jit(solution)/shard_map/ppermute | solution.py:116
  140.3 1.4 shard_map.75.refs_0_
  141.7 3.2 %collective-permute-done.26.refs_3_ = bf16[128,512]{1,0:T(8,128)(2,1)S(1)} collective-permute-done((bf16[128,512]{1,0:T(8,128)(2,1)S(1)}, bf16[128,512]{1,0:T(8,128)(2,1)S(1)}, u32[]{:S(2)}, u32[]{:S(2)}) %collective-permute-start.26) | collective-permute-done | bytes 131104 | tf_op jit(solution)/shard_map/ppermute | solution.py:116
  144.8 1.7 %collective-permute-done.27.refs_4_ = bf16[128,512]{1,0:T(8,128)(2,1)S(1)} collective-permute-done((bf16[128,512]{1,0:T(8,128)(2,1)S(1)}, bf16[128,512]{1,0:T(8,128)(2,1)S(1)}, u32[]{:S(2)}, u32[]{:S(2)}) %collective-permute-start.27) | collective-permute-done | bytes 131104 | tf_op jit(solution)/shard_map/ppermute | solution.py:116
  146.6 1.3 shard_map.77
  (65 shorter events, 4.0 us)
Async XLA Ops:
  0.0 48.5 %copy-start = (bf16[256,1536]{1,0:T(8,128)(2,1)S(1)}, bf16[256,1536]{1,0:T(8,128)(2,1)}, u32[]{:S(2)}) copy-start(bf16[256,1536]{1,0:T(8,128)(2,1)} %refs_2_.5) | copy-start | bytes 2359300
  0.0 52.9 %collective-permute-start.1 = (bf16[256,1536]{1,0:T(8,128)(2,1)}, bf16[256,1536]{1,0:T(8,128)(2,1)S(1)}, u32[]{:S(2)}, u32[]{:S(2)}) collective-permute-start(bf16[256,1536]{1,0:T(8,128)(2,1)} %key_ref.1), channel_id=1, source_target_pairs={{4,6},{6,4},{8,10},{10,8},{5,7},{7,5},{9,11},{11,9},{20,22},{22,20... | collective-permute-start | bytes 2359304 | tf_op jit(solution)/shard_map/ppermute | solution.py:116
  0.8 54.3 %collective-permute-start.3 = (bf16[256,1536]{1,0:T(8,128)(2,1)}, bf16[256,1536]{1,0:T(8,128)(2,1)S(1)}, u32[]{:S(2)}, u32[]{:S(2)}) collective-permute-start(bf16[256,1536]{1,0:T(8,128)(2,1)} %key_ref.1), channel_id=1, source_target_pairs={{4,8},{6,10},{8,4},{10,6},{5,9},{7,11},{9,5},{11,7},{20,24},{22,26... | collective-permute-start | bytes 2359304 | tf_op jit(solution)/shard_map/ppermute | solution.py:116
  1.6 1.1 copy-start.5
  2.7 1.1 copy-start.6
  5.2 21.6 %collective-permute-start.7 = (bf16[512,512]{1,0:T(8,128)(2,1)}, bf16[512,512]{1,0:T(8,128)(2,1)}, u32[]{:S(2)}, u32[]{:S(2)}) collective-permute-start(bf16[512,512]{1,0:T(8,128)(2,1)} %get-tuple-element.20.refs_10_), channel_id=1, source_target_pairs={{0,4},{2,6},{12,8},{14,10},{1,5},{3,7},{13,9},{15,11},{16,20},{18,... | collective-permute-start | bytes 1572872 | tf_op jit(solution)/shard_map/ppermute | solution.py:116
  14.9 23.0 %collective-permute-start.12 = (bf16[512,512]{1,0:T(8,128)(2,1)}, bf16[512,512]{1,0:T(8,128)(2,1)}, u32[]{:S(2)}, u32[]{:S(2)}) collective-permute-start(bf16[512,512]{1,0:T(8,128)(2,1)} %get-tuple-element.23.refs_10_), channel_id=1, source_target_pairs={{0,4},{2,6},{12,8},{14,10},{1,5},{3,7},{13,9},{15,11},{16,20},{18,... | collective-permute-start | bytes 1572872 | tf_op jit(solution)/shard_map/ppermute | solution.py:116
  17.0 31.4 %collective-permute-start.21 = (bf16[512,512]{1,0:T(8,128)(2,1)}, bf16[512,512]{1,0:T(8,128)(2,1)}, u32[]{:S(2)}, u32[]{:S(2)}) collective-permute-start(bf16[512,512]{1,0:T(8,128)(2,1)} %get-tuple-element.30.refs_10_), channel_id=1, source_target_pairs={{0,4},{2,6},{12,8},{14,10},{1,5},{3,7},{13,9},{15,11},{16,20},{18,... | collective-permute-start | bytes 1572872 | tf_op jit(solution)/shard_map/ppermute | solution.py:116
  19.1 0.8 copy-start.7
  19.1 0.7 copy-start.8
  26.7 29.9 %collective-permute-start.2 = (bf16[256,1536]{1,0:T(8,128)(2,1)}, bf16[256,1536]{1,0:T(8,128)(2,1)S(1)}, u32[]{:S(2)}, u32[]{:S(2)}) collective-permute-start(bf16[256,1536]{1,0:T(8,128)(2,1)} %value_ref.1), channel_id=1, source_target_pairs={{4,6},{6,4},{8,10},{10,8},{5,7},{7,5},{9,11},{11,9},{20,22},{22,20... | collective-permute-start | bytes 2359304 | tf_op jit(solution)/shard_map/ppermute | solution.py:116
  38.0 20.3 %collective-permute-start.4 = (bf16[256,1536]{1,0:T(8,128)(2,1)}, bf16[256,1536]{1,0:T(8,128)(2,1)S(1)}, u32[]{:S(2)}, u32[]{:S(2)}) collective-permute-start(bf16[256,1536]{1,0:T(8,128)(2,1)} %value_ref.1), channel_id=1, source_target_pairs={{4,8},{6,10},{8,4},{10,6},{5,9},{7,11},{9,5},{11,7},{20,24},{22,26... | collective-permute-start | bytes 2359304 | tf_op jit(solution)/shard_map/ppermute | solution.py:116
  48.5 20.7 %collective-permute-start = (bf16[256,1536]{1,0:T(8,128)(2,1)S(1)}, bf16[256,1536]{1,0:T(8,128)(2,1)S(1)}, u32[]{:S(2)}, u32[]{:S(2)}) collective-permute-start(bf16[256,1536]{1,0:T(8,128)(2,1)S(1)} %copy-done), channel_id=1, source_target_pairs={{0,4},{2,6},{12,8},{14,10},{1,5},{3,7},{13,9},{15,11},{16,20},{18,... | collective-permute-start | bytes 2359304 | tf_op jit(solution)/shard_map/ppermute | solution.py:116
  52.9 18.6 %collective-permute-start.9 = (bf16[512,512]{1,0:T(8,128)(2,1)}, bf16[512,512]{1,0:T(8,128)(2,1)}, u32[]{:S(2)}, u32[]{:S(2)}) collective-permute-start(bf16[512,512]{1,0:T(8,128)(2,1)} %collective-permute-done.7.refs_11_), channel_id=1, source_target_pairs={{4,8},{6,10},{8,4},{10,6},{5,9},{7,11},{9,5},{11,7},{20,24},{22,26... | collective-permute-start | bytes 1572872 | tf_op jit(solution)/shard_map/ppermute | solution.py:116
  54.4 0.7 copy-start.9
  55.1 18.0 %collective-permute-start.8 = (bf16[512,512]{1,0:T(8,128)(2,1)}, bf16[512,512]{1,0:T(8,128)(2,1)}, u32[]{:S(2)}, u32[]{:S(2)}) collective-permute-start(bf16[512,512]{1,0:T(8,128)(2,1)} %collective-permute-done.7.refs_11_), channel_id=1, source_target_pairs={{4,6},{6,4},{8,10},{10,8},{5,7},{7,5},{9,11},{11,9},{20,22},{22,20... | collective-permute-start | bytes 1572872 | tf_op jit(solution)/shard_map/ppermute | solution.py:116
  56.7 22.6 %collective-permute-start.5 = (bf16[256,1536]{1,0:T(8,128)(2,1)S(1)}, bf16[256,1536]{1,0:T(8,128)(2,1)}, u32[]{:S(2)}, u32[]{:S(2)}) collective-permute-start(bf16[256,1536]{1,0:T(8,128)(2,1)S(1)} %collective-permute-done.3.refs_6_), channel_id=1, source_target_pairs={{4,6},{6,4},{8,10},{10,8},{5,7},{7,5},{9,11},{11,9},{20,22},{22,20... | collective-permute-start | bytes 2359304 | tf_op jit(solution)/shard_map/ppermute | solution.py:116
  58.3 10.9 %copy-start.1 = (bf16[256,1536]{1,0:T(8,128)(2,1)}, bf16[256,1536]{1,0:T(8,128)(2,1)S(1)}, u32[]{:S(2)}) copy-start(bf16[256,1536]{1,0:T(8,128)(2,1)S(1)} %collective-permute-done.4.refs_7_) | copy-start | bytes 2359300
  58.3 16.6 %collective-permute-start.14 = (bf16[512,512]{1,0:T(8,128)(2,1)}, bf16[512,512]{1,0:T(8,128)(2,1)}, u32[]{:S(2)}, u32[]{:S(2)}) collective-permute-start(bf16[512,512]{1,0:T(8,128)(2,1)} %collective-permute-done.12.refs_11_), channel_id=1, source_target_pairs={{4,8},{6,10},{8,4},{10,6},{5,9},{7,11},{9,5},{11,7},{20,24},{22,26... | collective-permute-start | bytes 1572872 | tf_op jit(solution)/shard_map/ppermute | solution.py:116
  69.2 0.9 copy-start.3
  70.0 6.3 %collective-permute-start.23 = (bf16[512,512]{1,0:T(8,128)(2,1)}, bf16[512,512]{1,0:T(8,128)(2,1)}, u32[]{:S(2)}, u32[]{:S(2)}) collective-permute-start(bf16[512,512]{1,0:T(8,128)(2,1)} %collective-permute-done.21.refs_11_), channel_id=1, source_target_pairs={{4,8},{6,10},{8,4},{10,6},{5,9},{7,11},{9,5},{11,7},{20,24},{22,26... | collective-permute-start | bytes 1572872 | tf_op jit(solution)/shard_map/ppermute | solution.py:116
  71.5 6.3 %collective-permute-start.10 = (bf16[512,512]{1,0:T(8,128)(2,1)}, bf16[512,512]{1,0:T(8,128)(2,1)}, u32[]{:S(2)}, u32[]{:S(2)}) collective-permute-start(bf16[512,512]{1,0:T(8,128)(2,1)} %collective-permute-done.9.refs_13_), channel_id=1, source_target_pairs={{4,6},{6,4},{8,10},{10,8},{5,7},{7,5},{9,11},{11,9},{20,22},{22,20... | collective-permute-start | bytes 1572872 | tf_op jit(solution)/shard_map/ppermute | solution.py:116
  73.2 8.1 %collective-permute-start.6 = (bf16[256,1536]{1,0:T(8,128)(2,1)}, bf16[256,1536]{1,0:T(8,128)(2,1)}, u32[]{:S(2)}, u32[]{:S(2)}) collective-permute-start(bf16[256,1536]{1,0:T(8,128)(2,1)} %copy-done.1), channel_id=1, source_target_pairs={{4,6},{6,4},{8,10},{10,8},{5,7},{7,5},{9,11},{11,9},{20,22},{22,20... | collective-permute-start | bytes 2359304 | tf_op jit(solution)/shard_map/ppermute | solution.py:116
  74.9 11.5 %collective-permute-start.13 = (bf16[512,512]{1,0:T(8,128)(2,1)}, bf16[512,512]{1,0:T(8,128)(2,1)}, u32[]{:S(2)}, u32[]{:S(2)}) collective-permute-start(bf16[512,512]{1,0:T(8,128)(2,1)} %collective-permute-done.12.refs_11_), channel_id=1, source_target_pairs={{4,6},{6,4},{8,10},{10,8},{5,7},{7,5},{9,11},{11,9},{20,22},{22,20... | collective-permute-start | bytes 1572872 | tf_op jit(solution)/shard_map/ppermute | solution.py:116
  76.4 11.3 %collective-permute-start.15 = (bf16[512,512]{1,0:T(8,128)(2,1)}, bf16[512,512]{1,0:T(8,128)(2,1)}, u32[]{:S(2)}, u32[]{:S(2)}) collective-permute-start(bf16[512,512]{1,0:T(8,128)(2,1)} %collective-permute-done.14.refs_13_), channel_id=1, source_target_pairs={{4,6},{6,4},{8,10},{10,8},{5,7},{7,5},{9,11},{11,9},{20,22},{22,20... | collective-permute-start | bytes 1572872 | tf_op jit(solution)/shard_map/ppermute | solution.py:116
  77.8 13.4 %collective-permute-start.22 = (bf16[512,512]{1,0:T(8,128)(2,1)}, bf16[512,512]{1,0:T(8,128)(2,1)}, u32[]{:S(2)}, u32[]{:S(2)}) collective-permute-start(bf16[512,512]{1,0:T(8,128)(2,1)} %collective-permute-done.21.refs_11_), channel_id=1, source_target_pairs={{4,6},{6,4},{8,10},{10,8},{5,7},{7,5},{9,11},{11,9},{20,22},{22,20... | collective-permute-start | bytes 1572872 | tf_op jit(solution)/shard_map/ppermute | solution.py:116
  79.3 12.5 %collective-permute-start.24 = (bf16[512,512]{1,0:T(8,128)(2,1)}, bf16[512,512]{1,0:T(8,128)(2,1)}, u32[]{:S(2)}, u32[]{:S(2)}) collective-permute-start(bf16[512,512]{1,0:T(8,128)(2,1)} %collective-permute-done.23.refs_13_), channel_id=1, source_target_pairs={{4,6},{6,4},{8,10},{10,8},{5,7},{7,5},{9,11},{11,9},{20,22},{22,20... | collective-permute-start | bytes 1572872 | tf_op jit(solution)/shard_map/ppermute | solution.py:116
  81.3 1.1 copy-start.2
  82.4 1.1 copy-start.4
  85.7 9.7 %collective-permute-start.11 = (bf16[128,512]{1,0:T(8,128)(2,1)S(1)}, bf16[128,512]{1,0:T(8,128)(2,1)S(1)}, u32[]{:S(2)}, u32[]{:S(2)}) collective-permute-start(bf16[128,512]{1,0:T(8,128)(2,1)S(1)} %get-tuple-element.22), channel_id=1, source_target_pairs={{4,5},{5,4},{6,7},{7,6},{8,9},{9,8},{10,11},{11,10},{20,21},{21,20... | collective-permute-start | bytes 393224 | tf_op jit(solution)/shard_map/ppermute | solution.py:116
  86.4 33.1 %collective-permute-start.17 = (bf16[128,512]{1,0:T(8,128)(2,1)S(1)}, bf16[128,512]{1,0:T(8,128)(2,1)S(1)}, u32[]{:S(2)}, u32[]{:S(2)}) collective-permute-start(bf16[128,512]{1,0:T(8,128)(2,1)S(1)} %get-tuple-element.26), channel_id=1, source_target_pairs={{4,0},{5,1},{6,2},{7,3},{8,12},{9,13},{10,14},{11,15},{20,16},{21,... | collective-permute-start | bytes 393224 | tf_op jit(solution)/shard_map/ppermute | solution.py:116
  87.7 34.1 %collective-permute-start.18 = (bf16[128,512]{1,0:T(8,128)(2,1)S(1)}, bf16[128,512]{1,0:T(8,128)(2,1)S(1)}, u32[]{:S(2)}, u32[]{:S(2)}) collective-permute-start(bf16[128,512]{1,0:T(8,128)(2,1)S(1)} %get-tuple-element.27), channel_id=1, source_target_pairs={{4,1},{5,0},{6,3},{7,2},{8,13},{9,12},{10,15},{11,14},{20,17},{21,... | collective-permute-start | bytes 393224 | tf_op jit(solution)/shard_map/ppermute | solution.py:116
  91.2 31.9 %collective-permute-start.16 = (bf16[128,512]{1,0:T(8,128)(2,1)S(1)}, bf16[128,512]{1,0:T(8,128)(2,1)S(1)}, u32[]{:S(2)}, u32[]{:S(2)}) collective-permute-start(bf16[128,512]{1,0:T(8,128)(2,1)S(1)} %get-tuple-element.25), channel_id=1, source_target_pairs={{4,5},{5,4},{6,7},{7,6},{8,9},{9,8},{10,11},{11,10},{20,21},{21,20... | collective-permute-start | bytes 393224 | tf_op jit(solution)/shard_map/ppermute | solution.py:116
  91.9 39.1 %collective-permute-start.19 = (bf16[128,512]{1,0:T(8,128)(2,1)S(1)}, bf16[128,512]{1,0:T(8,128)(2,1)S(1)}, u32[]{:S(2)}, u32[]{:S(2)}) collective-permute-start(bf16[128,512]{1,0:T(8,128)(2,1)S(1)} %get-tuple-element.28), channel_id=1, source_target_pairs={{4,0},{5,1},{6,2},{7,3},{8,12},{9,13},{10,14},{11,15},{20,16},{21,... | collective-permute-start | bytes 393224 | tf_op jit(solution)/shard_map/ppermute | solution.py:116
  95.4 44.9 %collective-permute-start.20 = (bf16[128,512]{1,0:T(8,128)(2,1)S(1)}, bf16[128,512]{1,0:T(8,128)(2,1)S(1)}, u32[]{:S(2)}, u32[]{:S(2)}) collective-permute-start(bf16[128,512]{1,0:T(8,128)(2,1)S(1)} %get-tuple-element.29), channel_id=1, source_target_pairs={{4,1},{5,0},{6,3},{7,2},{8,13},{9,12},{10,15},{11,14},{20,17},{21,... | collective-permute-start | bytes 393224 | tf_op jit(solution)/shard_map/ppermute | solution.py:116
  119.5 22.2 %collective-permute-start.25 = (bf16[128,512]{1,0:T(8,128)(2,1)S(1)}, bf16[128,512]{1,0:T(8,128)(2,1)S(1)}, u32[]{:S(2)}, u32[]{:S(2)}) collective-permute-start(bf16[128,512]{1,0:T(8,128)(2,1)S(1)} %get-tuple-element.32), channel_id=1, source_target_pairs={{4,5},{5,4},{6,7},{7,6},{8,9},{9,8},{10,11},{11,10},{20,21},{21,20... | collective-permute-start | bytes 393224 | tf_op jit(solution)/shard_map/ppermute | solution.py:116
  121.8 23.0 %collective-permute-start.26 = (bf16[128,512]{1,0:T(8,128)(2,1)S(1)}, bf16[128,512]{1,0:T(8,128)(2,1)S(1)}, u32[]{:S(2)}, u32[]{:S(2)}) collective-permute-start(bf16[128,512]{1,0:T(8,128)(2,1)S(1)} %get-tuple-element.33), channel_id=1, source_target_pairs={{4,0},{5,1},{6,2},{7,3},{8,12},{9,13},{10,14},{11,15},{20,16},{21,... | collective-permute-start | bytes 393224 | tf_op jit(solution)/shard_map/ppermute | solution.py:116
  123.1 23.5 %collective-permute-start.27 = (bf16[128,512]{1,0:T(8,128)(2,1)S(1)}, bf16[128,512]{1,0:T(8,128)(2,1)S(1)}, u32[]{:S(2)}, u32[]{:S(2)}) collective-permute-start(bf16[128,512]{1,0:T(8,128)(2,1)S(1)} %get-tuple-element.34), channel_id=1, source_target_pairs={{4,1},{5,0},{6,3},{7,2},{8,13},{9,12},{10,15},{11,14},{20,17},{21,... | collective-permute-start | bytes 393224 | tf_op jit(solution)/shard_map/ppermute | solution.py:116

commit v3 on v2

--- a/solution.py
+++ b/solution.py
@@ -13,8 +13,8 @@
 LOG2_E = 1.4426950408889634
 DEAD = -1e30
 CORES = 2
-CHUNKS = 3
-VMEM_GRANT = 12 << 20
+FIRST_SHARE = 7, 12
+VMEM_GRANT = 20 << 20
 
 
 def tables(block_lists, block_counts, owner, seq_size):
@@ -131,54 +131,129 @@
         copy.wait()
 
 
-def relayed_kernel(seq_size, panel_size, heads, start, size, *refs):
-    info_ref, code_ref, own_query, guest_query = refs[:4]
-    whole = refs[4:10]
-    stacked = refs[10:15]
-    own_out = refs[15 : 15 + panel_size]
-    guest_out = refs[15 + panel_size : 15 + 2 * panel_size]
+def masked_scores(query, codes, key_block):
+    factor = HEAD_DIM ** (-0.5) * LOG2_E
+    masked = []
+    for j, code in codes:
+        scores = lax.dot_general(
+            key_block(j, code & 1), query, (((1,), (1,)), ((), ())), preferred_element_type=jnp.float32
+        )
+        tiles = query.shape[0] // BLOCK
+        bias = [
+            jnp.full((1, BLOCK), jnp.where((code >> (tile + 1)) & 1 == 1, 0.0, DEAD), jnp.float32)
+            for tile in range(tiles)
+        ]
+        masked.append(scores * factor + jnp.concatenate(bias, axis=1))
+    return masked
+
+
+def weigh(masked, top, codes, value_block):
+    total, mixed = None, None
+    for scores, (j, code) in zip(masked, codes):
+        weights = jnp.exp2(scores - top)
+        total = weights if total is None else total + weights
+        product = lax.dot_general(
+            value_block(j, code & 1),
+            weights.astype(jnp.bfloat16),
+            (((0,), (0,)), ((), ())),
+            preferred_element_type=jnp.float32,
+        )
+        mixed = product if mixed is None else mixed + product
+    return jnp.sum(total, axis=0, keepdims=True), mixed
+
+
+def highest(masked):
+    return jnp.max(functools.reduce(jnp.maximum, masked), axis=0, keepdims=True)
+
+
+def each_unit(size, unit):
+    @pl.loop(0, size // 2)
+    def _(pair):
+        for h in range(2):
+            for side in range(2):
+                unit(pair * 2 + h, side)
+
+    for h in range(size - size % 2, size):
+        for side in range(2):
+            unit(h, side)
+
+
+def columns_of(head):
+    return pl.ds(pl.multiple_of(head * HEAD_DIM, HEAD_DIM), HEAD_DIM)
+
+
+def block_reader(pick):
+    def block(slot, which):
+        ref, first, columns = pick(slot)
+        return ref[pl.ds(pl.multiple_of(first + which * BLOCK, BLOCK), BLOCK), columns]
+
+    return block
+
+
+def early_kernel(seq_size, heads, starts, sizes, *refs):
+    info_ref, code_ref = refs[:2]
+    queries = refs[2:4]
+    whole = refs[4:12]
+    sums, stats = refs[12 : 12 + len(sizes)], refs[12 + len(sizes) :]
+
+    @pl.when(info_ref[0] == 1)
+    def _():
+        for k, (start, size) in enumerate(zip(starts, sizes)):
+
+            def unit(h, side):
+                columns = columns_of(h + start)
+                first = (side * heads + h + start) * (seq_size + 1)
+                codes = [(slot, code_ref[first + slot]) for slot in range(4)]
+                if side == 0:
+                    codes.append((0, code_ref[first + seq_size]))
+                masked = masked_scores(
+                    queries[side][:, columns], codes, block_reader(lambda slot: (whole[2 * slot], 0, columns))
+                )
+                top = highest(masked)
+                total, mixed = weigh(
+                    masked, top, codes, block_reader(lambda slot: (whole[2 * slot + 1], 0, columns))
+                )
+                sums[k][h * 2 + side] = mixed
+                stats[k][h * 2 + side, pl.ds(0, 1), :] = top
+                stats[k][h * 2 + side, pl.ds(1, 1), :] = total
+
+            each_unit(size, unit)
+
+
+def late_kernel(seq_size, panel_size, heads, start, size, *refs):
+    info_ref, code_ref = refs[:2]
+    queries = refs[2:4]
+    sums, stats = refs[4:6]
+    stacked = refs[6:10]
+    outs = refs[10 : 10 + panel_size], refs[10 + panel_size : 10 + 2 * panel_size]
     held = refs[-1]
     panel = info_ref[1]
-    rows = own_query.shape[0]
+    rows = queries[0].shape[0]
     piece = rows // panel_size
 
-    def unit(h, side, spot):
-        query, home, outs = ((own_query, 0, own_out), (guest_query, 4, guest_out))[side]
-        local = pl.ds(pl.multiple_of(h * HEAD_DIM, HEAD_DIM), HEAD_DIM)
-        full = pl.ds(pl.multiple_of((h + start) * HEAD_DIM, HEAD_DIM), HEAD_DIM)
-
-        def read(kind):
-            def block(j, which):
-                slot = home if j == seq_size else j
-                if 1 <= slot <= 3:
-                    ref, first, columns = whole[2 * (slot - 1) + kind], 0, full
-                else:
-                    ref, first, columns = stacked[slot - 3 if slot else 0], kind * rows, local
-                return ref[pl.ds(pl.multiple_of(first + which * BLOCK, BLOCK), BLOCK), columns]
-
-            return block
-
+    def unit(h, side):
+        local = columns_of(h)
         first = (side * heads + h + start) * (seq_size + 1)
-        codes = [code_ref[first + j] for j in range(seq_size + 1)]
-        result = attend(query[:, full], codes, read(0), read(1))
-        held[spot] = result
+        codes = [(slot, code_ref[first + slot]) for slot in range(4, seq_size)]
+        if side == 1:
+            codes.append((4, code_ref[first + seq_size]))
+        read = lambda kind: block_reader(lambda slot: (stacked[slot - 4], kind * rows, local))
+        masked = masked_scores(queries[side][:, columns_of(h + start)], codes, read(0))
+        before = stats[h * 2 + side, pl.ds(0, 1), :]
+        top = jnp.maximum(before, highest(masked))
+        kept = jnp.exp2(before - top)
+        total, mixed = weigh(masked, top, codes, read(1))
+        total = total + kept * stats[h * 2 + side, pl.ds(1, 1), :]
+        mixed = mixed + kept * sums[h * 2 + side]
+        spot = (h % 2) * 2 + side
+        held[spot] = (mixed / total).T
         for shift in range(panel_size):
             first_row = pl.multiple_of(lax.rem(panel + shift, panel_size) * piece, piece)
-            outs[shift][:, local] = held[spot, pl.ds(first_row, piece), :].astype(outs[shift].dtype)
+            outs[side][shift][:, local] = held[spot, pl.ds(first_row, piece), :].astype(outs[side][shift].dtype)
 
     @pl.when(info_ref[0] == 1)
     def _():
-        if size > 1:
-
-            @pl.loop(0, size // 2)
-            def _(pair):
-                for h in range(2):
-                    for side in range(2):
-                        unit(pair * 2 + h, side, h * 2 + side)
-
-        for h in range(size - size % 2, size):
-            for side in range(2):
-                unit(h, side, side)
+        each_unit(size, unit)
 
 
 def assemble_kernel(panel_size, starts, sizes, aliased, info_ref, *refs):
@@ -224,9 +299,10 @@
     outward = [(target, source) for source, target in inward]
     in_vmem, in_smem, anywhere = (pl.BlockSpec(memory_space=s) for s in (pltpu.VMEM, pltpu.SMEM, pl.ANY))
 
-    chunks = min(CHUNKS, heads)
-    starts = [heads * k // chunks for k in range(chunks)]
-    sizes = [heads * (k + 1) // chunks - heads * k // chunks for k in range(chunks)]
+    front = max(1, heads * FIRST_SHARE[0] // FIRST_SHARE[1])
+    sizes = [front, heads - front]
+    starts = [0, front]
+    chunks = len(sizes)
 
     middle = [send(x, across) for x in (key_rows, value_rows)]
     packed = pl.pallas_call(
@@ -262,25 +338,38 @@
     codes = jnp.stack([arranged(position), arranged(guest)]).reshape(-1)
     info = jnp.stack([is_inner.astype(jnp.int32), panel])
 
+    units = [2 * size for size in sizes]
+    params = pltpu.CompilerParams(vmem_limit_bytes=VMEM_GRANT)
+    cost = lambda count, blocks: pl.CostEstimate(
+        flops=count * 4 * rows * blocks * BLOCK * HEAD_DIM,
+        bytes_accessed=count * blocks * 4 * BLOCK * HEAD_DIM,
+        transcendentals=count * rows * blocks * BLOCK,
+    )
+    state = pl.pallas_call(
+        functools.partial(early_kernel, seq_size, heads, starts, sizes),
+        out_shape=[jax.ShapeDtypeStruct((count, HEAD_DIM, rows), jnp.float32) for count in units]
+        + [jax.ShapeDtypeStruct((count, 8, rows), jnp.float32) for count in units],
+        in_specs=[in_smem] * 2 + [in_vmem] * 10,
+        out_specs=[in_vmem] * (2 * chunks),
+        compiler_params=params,
+        cost_estimate=cost(2 * heads, 5),
+        name="early",
+    )(info, codes, queries, guest_query, key_rows, value_rows, *beside, *middle, *middle_beside)
+
     own_pieces, guest_pieces = [], []
     for k, (start, size) in enumerate(zip(starts, sizes)):
         far = send(ends[k], across)
         ends_beside = send(ends[k], partner)
         far_beside = send(far, partner)
-        stacked = [packed[k], ends[k], ends_beside, far, far_beside]
         outs = pl.pallas_call(
-            functools.partial(relayed_kernel, seq_size, panel_size, heads, start, size),
+            functools.partial(late_kernel, seq_size, panel_size, heads, start, size),
             out_shape=[jax.ShapeDtypeStruct((rows // panel_size, size * HEAD_DIM), queries.dtype)] * (2 * panel_size),
-            in_specs=[in_smem] * 2 + [in_vmem] * 13,
+            in_specs=[in_smem] * 2 + [in_vmem] * 8,
             out_specs=[in_vmem] * (2 * panel_size),
             scratch_shapes=[pltpu.VMEM((4, rows, HEAD_DIM), jnp.float32)],
-            compiler_params=pltpu.CompilerParams(vmem_limit_bytes=VMEM_GRANT),
-            cost_estimate=pl.CostEstimate(
-                flops=size * 8 * rows * (seq_size + 1) * BLOCK * HEAD_DIM,
-                bytes_accessed=size * HEAD_DIM * 2 * rows * 20,
-                transcendentals=size * 2 * rows * (seq_size + 1) * BLOCK,
-            ),
-        )(info, codes, queries, guest_query, *beside, *middle, *middle_beside, *stacked)
+            compiler_params=params,
+            cost_estimate=cost(2 * size, 5),
+        )(info, codes, queries, guest_query, state[k], state[chunks + k], ends[k], ends_beside, far, far_beside)
         both = ("seq", "panel")
         for shift in range(panel_size):
             mine, theirs = outs[shift], outs[panel_size + shift]

time: 149 us -> 168 us (1.13)
  waiting for transfers between devices: 80.8 us -> 113 us
  starting transfers between devices: 47.5 us -> 37.1 us
  local copies, waits for them, and re-layouts: 7.8 us -> 4.91 us
    ppermute x28 -> x21, waiting for transfers between devices: 80.8 us -> 113 us  [send(): return lax.ppermute(value, axes, pairs)]
    ppermute x28 -> x21, starting transfers between devices: 47.5 us -> 37.1 us  [send(): return lax.ppermute(value, axes, pairs)]
    unnamed x20 -> x10, local copies, waits for them, and re-layouts: 6.81 us -> 2.27 us
  transfers between devices with their start and end apart: 28 -> 21, of which waited for: 10 -> 5; matrix products, arithmetic and copies ran while one was open for 1% -> 3% of each run, Pallas kernels for 6% -> 5%
where the time goes in v3:
time: 168 us; the launch traced here: 167 us
  waiting for transfers between devices  113 us (67%)
  starting transfers between devices  37.1 us (22%)
  Pallas kernels  10 us (6%)
  local copies, waits for them, and re-layouts  4.91 us (3%)
    ppermute x21, waiting for transfers between devices, send(): return lax.ppermute(value, axes, pairs)  113 us
    ppermute x21, starting transfers between devices, send(): return lax.ppermute(value, axes, pairs)  37.1 us
    pallas_call x2, Pallas kernels, relayed(): pl.pallas_call(functools.partial(late_kernel, seq_size, panel_size, heads...  3.74 us
  transfers between devices with their start and end apart: 21, of which 5 were waited for; matrix products, arithmetic and copies ran while one was open for 3% of the time, Pallas kernels for 5%

profile of v3, /device:TPU:0, one launch (start us, length us, event | category | flops | bytes accessed | tf_op | source)
XLA Modules:
  0.0 167.2 jit_solution(16396692321026750847)
XLA Ops:
  0.0 1.7 %collective-permute-start.3 = (bf16[256,1536]{1,0:T(8,128)(2,1)}, bf16[256,1536]{1,0:T(8,128)(2,1)}, u32[]{:S(2)}, u32[]{:S(2)}) collective-permute-start(bf16[256,1536]{1,0:T(8,128)(2,1)} %key_ref.1), channel_id=1, source_target_pairs={{4,8},{6,10},{8,4},{10,6},{5,9},{7,11},{9,5},{11,7},{20,24},{22,26... | collective-permute-start | bytes 2359304 | tf_op jit(solution)/shard_map/ppermute | solution.py:116
  1.7 1.5 collective-permute-start.1
  3.2 7.3 %collective-permute-start = (bf16[256,1536]{1,0:T(8,128)(2,1)}, bf16[256,1536]{1,0:T(8,128)(2,1)S(1)}, u32[]{:S(2)}, u32[]{:S(2)}) collective-permute-start(bf16[256,1536]{1,0:T(8,128)(2,1)} %refs_2_.5), channel_id=1, source_target_pairs={{0,4},{2,6},{12,8},{14,10},{1,5},{3,7},{13,9},{15,11},{16,20},{18,... | collective-permute-start | bytes 2359304 | tf_op jit(solution)/shard_map/ppermute | solution.py:116
  10.6 1.1 copy-done.1
  11.7 1.1 copy-done.3
  12.8 1.3 pack.1
  14.2 2.2 %collective-permute-start.14 = (bf16[512,640]{1,0:T(8,128)(2,1)}, bf16[512,640]{1,0:T(8,128)(2,1)}, u32[]{:S(2)}, u32[]{:S(2)}) collective-permute-start(bf16[512,640]{1,0:T(8,128)(2,1)} %get-tuple-element.28), channel_id=1, source_target_pairs={{0,4},{2,6},{12,8},{14,10},{1,5},{3,7},{13,9},{15,11},{16,20},{18,... | collective-permute-start | bytes 1966088 | tf_op jit(solution)/shard_map/ppermute | solution.py:116
  16.3 2.2 %collective-permute-start.7 = (bf16[512,896]{1,0:T(8,128)(2,1)}, bf16[512,896]{1,0:T(8,128)(2,1)}, u32[]{:S(2)}, u32[]{:S(2)}) collective-permute-start(bf16[512,896]{1,0:T(8,128)(2,1)} %get-tuple-element.21), channel_id=1, source_target_pairs={{0,4},{2,6},{12,8},{14,10},{1,5},{3,7},{13,9},{15,11},{16,20},{18,... | collective-permute-start | bytes 2752520 | tf_op jit(solution)/shard_map/ppermute | solution.py:116
  18.6 0.8 constant_dynamic-slice_fusion
  19.4 1.0 constant_dynamic-slice_fusion.1
  20.4 0.1 copy.25
  20.5 0.1 iota_compare_fusion.2
  20.6 0.1 fusion.3
  20.8 0.1 copy.26
  20.9 0.1 copy.22
  21.0 0.1 fusion.1
  21.2 0.1 copy.23
  21.3 40.6 %collective-permute-done.7.refs_6_ = bf16[512,896]{1,0:T(8,128)(2,1)} collective-permute-done((bf16[512,896]{1,0:T(8,128)(2,1)}, bf16[512,896]{1,0:T(8,128)(2,1)}, u32[]{:S(2)}, u32[]{:S(2)}) %collective-permute-start.7) | collective-permute-done | bytes 917536 | tf_op jit(solution)/shard_map/ppermute | solution.py:116
  62.0 1.6 collective-permute-start.9
  63.6 1.6 collective-permute-start.4
  65.2 1.6 collective-permute-start.2
  66.8 0.7 multiply_reduce_fusion.5
  67.6 1.5 collective-permute-start.16
  69.1 1.5 collective-permute-start.5
  70.8 1.6 collective-permute-start.6
  72.4 1.6 collective-permute-start.8
  74.0 1.6 collective-permute-start.10
  75.7 0.1 multiply_reduce_fusion.1
  75.8 0.1 copy.29
  75.9 0.1 copy.24
  76.0 1.5 collective-permute-start.15
  77.5 1.5 collective-permute-start.17
  79.0 0.1 reshape.60.refs_1_
  79.2 2.3 %early.1 = (f32[14,128,256]{2,1,0:T(8,128)S(1)}, f32[10,128,256]{2,1,0:T(8,128)S(1)}, f32[14,8,256]{2,1,0:T(8,128)S(1)}, f32[10,8,256]{2,1,0:T(8,128)S(1)}) custom-call(s32[2]{0:T(128)S(1)} %pad_add_fusion.3.refs_0_.info_ref, s32[216]{0:T(256)S(1)} %reshape.60.refs_1_, bf16[256,1536]{1,0:T(8,128)(2,1)S(1)} %copy-done, ...), custom_call_target="tpu_custom_call" | custom-call | flops 2013265920 | bytes 7864320 | tf_op jit(solution)/shard_map/early/pallas_call | solution.py:348
  81.6 2.0 %shard_map.73 = (bf16[128,896]{1,0:T(8,128)(2,1)S(1)}, bf16[128,896]{1,0:T(8,128)(2,1)S(1)}, bf16[128,896]{1,0:T(8,128)(2,1)S(1)}, bf16[128,896]{1,0:T(8,128)(2,1)S(1)}) custom-call(s32[2]{0:T(128)S(1)} %pad_add_fusion.3.refs_0_.info_ref, s32[216]{0:T(256)S(1)} %reshape.60.refs_1_, bf16[256,1536]{1,0:T(8,128)(2,1)S(1)} %copy-done, ...), custom_call_target="tpu_custom_call" | custom-call | flops 1174405120 | bytes 4587520 | tf_op jit(solution)/shard_map/pallas_call | solution.py:364
  83.7 0.7 collective-permute-start.11
  84.3 1.3 collective-permute-start.12
  85.6 1.3 collective-permute-start.13
  87.0 1.7 %shard_map.75 = (bf16[128,640]{1,0:T(8,128)(2,1)S(1)}, bf16[128,640]{1,0:T(8,128)(2,1)S(1)}, bf16[128,640]{1,0:T(8,128)(2,1)S(1)}, bf16[128,640]{1,0:T(8,128)(2,1)S(1)}) custom-call(s32[2]{0:T(128)S(1)} %pad_add_fusion.3.refs_0_.info_ref, s32[216]{0:T(256)S(1)} %reshape.60.refs_1_, bf16[256,1536]{1,0:T(8,128)(2,1)S(1)} %copy-done, ...), custom_call_target="tpu_custom_call" | custom-call | flops 838860800 | bytes 3276800 | tf_op jit(solution)/shard_map/pallas_call | solution.py:364
  88.7 0.7 collective-permute-start.18
  89.4 1.3 collective-permute-start.19
  90.7 1.3 collective-permute-start.20
  92.0 61.1 %collective-permute-done.12.refs_2_ = bf16[128,896]{1,0:T(8,128)(2,1)S(1)} collective-permute-done((bf16[128,896]{1,0:T(8,128)(2,1)S(1)}, bf16[128,896]{1,0:T(8,128)(2,1)S(1)}, u32[]{:S(2)}, u32[]{:S(2)}) %collective-permute-start.12) | collective-permute-done | bytes 229408 | tf_op jit(solution)/shard_map/ppermute | solution.py:116
  153.1 3.9 %collective-permute-done.13.refs_3_ = bf16[128,896]{1,0:T(8,128)(2,1)S(1)} collective-permute-done((bf16[128,896]{1,0:T(8,128)(2,1)S(1)}, bf16[128,896]{1,0:T(8,128)(2,1)S(1)}, u32[]{:S(2)}, u32[]{:S(2)}) %collective-permute-start.13) | collective-permute-done | bytes 229408 | tf_op jit(solution)/shard_map/ppermute | solution.py:116
  157.0 1.3 shard_map.74.refs_0_
  158.4 4.4 %collective-permute-done.19.refs_3_ = bf16[128,640]{1,0:T(8,128)(2,1)S(1)} collective-permute-done((bf16[128,640]{1,0:T(8,128)(2,1)S(1)}, bf16[128,640]{1,0:T(8,128)(2,1)S(1)}, u32[]{:S(2)}, u32[]{:S(2)}) %collective-permute-start.19) | collective-permute-done | bytes 163872 | tf_op jit(solution)/shard_map/ppermute | solution.py:116
  162.7 3.2 %collective-permute-done.20.refs_4_ = bf16[128,640]{1,0:T(8,128)(2,1)S(1)} collective-permute-done((bf16[128,640]{1,0:T(8,128)(2,1)S(1)}, bf16[128,640]{1,0:T(8,128)(2,1)S(1)}, u32[]{:S(2)}, u32[]{:S(2)}) %collective-permute-start.20) | collective-permute-done | bytes 163872 | tf_op jit(solution)/shard_map/ppermute | solution.py:116
  165.9 1.3 shard_map.76
  (41 shorter events, 0.6 us)
Async XLA Ops:
  0.0 79.2 %copy-start = (bf16[256,1536]{1,0:T(8,128)(2,1)S(1)}, bf16[256,1536]{1,0:T(8,128)(2,1)}, u32[]{:S(2)}) copy-start(bf16[256,1536]{1,0:T(8,128)(2,1)} %refs_2_.5) | copy-start | bytes 2359300
  0.0 67.6 %collective-permute-start.3 = (bf16[256,1536]{1,0:T(8,128)(2,1)}, bf16[256,1536]{1,0:T(8,128)(2,1)}, u32[]{:S(2)}, u32[]{:S(2)}) collective-permute-start(bf16[256,1536]{1,0:T(8,128)(2,1)} %key_ref.1), channel_id=1, source_target_pairs={{4,8},{6,10},{8,4},{10,6},{5,9},{7,11},{9,5},{11,7},{20,24},{22,26... | collective-permute-start | bytes 2359304 | tf_op jit(solution)/shard_map/ppermute | solution.py:116
  1.7 67.4 %collective-permute-start.1 = (bf16[256,1536]{1,0:T(8,128)(2,1)}, bf16[256,1536]{1,0:T(8,128)(2,1)}, u32[]{:S(2)}, u32[]{:S(2)}) collective-permute-start(bf16[256,1536]{1,0:T(8,128)(2,1)} %key_ref.1), channel_id=1, source_target_pairs={{4,6},{6,4},{8,10},{10,8},{5,7},{7,5},{9,11},{11,9},{20,22},{22,20... | collective-permute-start | bytes 2359304 | tf_op jit(solution)/shard_map/ppermute | solution.py:116
  3.2 62.0 %collective-permute-start = (bf16[256,1536]{1,0:T(8,128)(2,1)}, bf16[256,1536]{1,0:T(8,128)(2,1)S(1)}, u32[]{:S(2)}, u32[]{:S(2)}) collective-permute-start(bf16[256,1536]{1,0:T(8,128)(2,1)} %refs_2_.5), channel_id=1, source_target_pairs={{0,4},{2,6},{12,8},{14,10},{1,5},{3,7},{13,9},{15,11},{16,20},{18,... | collective-permute-start | bytes 2359304 | tf_op jit(solution)/shard_map/ppermute | solution.py:116
  10.6 1.1 copy-start.1
  11.7 1.1 copy-start.3
  12.8 66.4 %copy-start.2 = (bf16[256,1536]{1,0:T(8,128)(2,1)S(1)}, bf16[256,1536]{1,0:T(8,128)(2,1)}, u32[]{:S(2)}) copy-start(bf16[256,1536]{1,0:T(8,128)(2,1)} %key_ref.1) | copy-start | bytes 2359300
  12.8 66.4 %copy-start.4 = (bf16[256,1536]{1,0:T(8,128)(2,1)S(1)}, bf16[256,1536]{1,0:T(8,128)(2,1)}, u32[]{:S(2)}) copy-start(bf16[256,1536]{1,0:T(8,128)(2,1)} %value_ref.1) | copy-start | bytes 2359300
  14.2 49.4 %collective-permute-start.14 = (bf16[512,640]{1,0:T(8,128)(2,1)}, bf16[512,640]{1,0:T(8,128)(2,1)}, u32[]{:S(2)}, u32[]{:S(2)}) collective-permute-start(bf16[512,640]{1,0:T(8,128)(2,1)} %get-tuple-element.28), channel_id=1, source_target_pairs={{0,4},{2,6},{12,8},{14,10},{1,5},{3,7},{13,9},{15,11},{16,20},{18,... | collective-permute-start | bytes 1966088 | tf_op jit(solution)/shard_map/ppermute | solution.py:116
  16.3 45.6 %collective-permute-start.7 = (bf16[512,896]{1,0:T(8,128)(2,1)}, bf16[512,896]{1,0:T(8,128)(2,1)}, u32[]{:S(2)}, u32[]{:S(2)}) collective-permute-start(bf16[512,896]{1,0:T(8,128)(2,1)} %get-tuple-element.21), channel_id=1, source_target_pairs={{0,4},{2,6},{12,8},{14,10},{1,5},{3,7},{13,9},{15,11},{16,20},{18,... | collective-permute-start | bytes 2752520 | tf_op jit(solution)/shard_map/ppermute | solution.py:116
  62.0 12.0 %collective-permute-start.9 = (bf16[512,896]{1,0:T(8,128)(2,1)}, bf16[512,896]{1,0:T(8,128)(2,1)}, u32[]{:S(2)}, u32[]{:S(2)}) collective-permute-start(bf16[512,896]{1,0:T(8,128)(2,1)} %collective-permute-done.7.refs_6_), channel_id=1, source_target_pairs={{4,8},{6,10},{8,4},{10,6},{5,9},{7,11},{9,5},{11,7},{20,24},{22,26... | collective-permute-start | bytes 2752520 | tf_op jit(solution)/shard_map/ppermute | solution.py:116
  63.6 7.2 %collective-permute-start.4 = (bf16[256,1536]{1,0:T(8,128)(2,1)}, bf16[256,1536]{1,0:T(8,128)(2,1)}, u32[]{:S(2)}, u32[]{:S(2)}) collective-permute-start(bf16[256,1536]{1,0:T(8,128)(2,1)} %value_ref.1), channel_id=1, source_target_pairs={{4,8},{6,10},{8,4},{10,6},{5,9},{7,11},{9,5},{11,7},{20,24},{22,26... | collective-permute-start | bytes 2359304 | tf_op jit(solution)/shard_map/ppermute | solution.py:116
  65.2 7.3 %collective-permute-start.2 = (bf16[256,1536]{1,0:T(8,128)(2,1)}, bf16[256,1536]{1,0:T(8,128)(2,1)}, u32[]{:S(2)}, u32[]{:S(2)}) collective-permute-start(bf16[256,1536]{1,0:T(8,128)(2,1)} %value_ref.1), channel_id=1, source_target_pairs={{4,6},{6,4},{8,10},{10,8},{5,7},{7,5},{9,11},{11,9},{20,22},{22,20... | collective-permute-start | bytes 2359304 | tf_op jit(solution)/shard_map/ppermute | solution.py:116
  67.6 8.4 %collective-permute-start.16 = (bf16[512,640]{1,0:T(8,128)(2,1)}, bf16[512,640]{1,0:T(8,128)(2,1)}, u32[]{:S(2)}, u32[]{:S(2)}) collective-permute-start(bf16[512,640]{1,0:T(8,128)(2,1)} %collective-permute-done.14.refs_6_), channel_id=1, source_target_pairs={{4,8},{6,10},{8,4},{10,6},{5,9},{7,11},{9,5},{11,7},{20,24},{22,26... | collective-permute-start | bytes 1966088 | tf_op jit(solution)/shard_map/ppermute | solution.py:116
  69.1 8.4 %collective-permute-start.5 = (bf16[256,1536]{1,0:T(8,128)(2,1)}, bf16[256,1536]{1,0:T(8,128)(2,1)}, u32[]{:S(2)}, u32[]{:S(2)}) collective-permute-start(bf16[256,1536]{1,0:T(8,128)(2,1)} %collective-permute-done.3.refs_8_), channel_id=1, source_target_pairs={{4,6},{6,4},{8,10},{10,8},{5,7},{7,5},{9,11},{11,9},{20,22},{22,20... | collective-permute-start | bytes 2359304 | tf_op jit(solution)/shard_map/ppermute | solution.py:116
  70.8 8.4 %collective-permute-start.6 = (bf16[256,1536]{1,0:T(8,128)(2,1)}, bf16[256,1536]{1,0:T(8,128)(2,1)}, u32[]{:S(2)}, u32[]{:S(2)}) collective-permute-start(bf16[256,1536]{1,0:T(8,128)(2,1)} %collective-permute-done.4.refs_9_), channel_id=1, source_target_pairs={{4,6},{6,4},{8,10},{10,8},{5,7},{7,5},{9,11},{11,9},{20,22},{22,20... | collective-permute-start | bytes 2359304 | tf_op jit(solution)/shard_map/ppermute | solution.py:116
  72.4 9.2 %collective-permute-start.8 = (bf16[512,896]{1,0:T(8,128)(2,1)}, bf16[512,896]{1,0:T(8,128)(2,1)}, u32[]{:S(2)}, u32[]{:S(2)}) collective-permute-start(bf16[512,896]{1,0:T(8,128)(2,1)} %collective-permute-done.7.refs_6_), channel_id=1, source_target_pairs={{4,6},{6,4},{8,10},{10,8},{5,7},{7,5},{9,11},{11,9},{20,22},{22,20... | collective-permute-start | bytes 2752520 | tf_op jit(solution)/shard_map/ppermute | solution.py:116
  74.0 7.6 %collective-permute-start.10 = (bf16[512,896]{1,0:T(8,128)(2,1)}, bf16[512,896]{1,0:T(8,128)(2,1)}, u32[]{:S(2)}, u32[]{:S(2)}) collective-permute-start(bf16[512,896]{1,0:T(8,128)(2,1)} %collective-permute-done.9.refs_8_), channel_id=1, source_target_pairs={{4,6},{6,4},{8,10},{10,8},{5,7},{7,5},{9,11},{11,9},{20,22},{22,20... | collective-permute-start | bytes 2752520 | tf_op jit(solution)/shard_map/ppermute | solution.py:116
  76.0 10.9 %collective-permute-start.15 = (bf16[512,640]{1,0:T(8,128)(2,1)}, bf16[512,640]{1,0:T(8,128)(2,1)}, u32[]{:S(2)}, u32[]{:S(2)}) collective-permute-start(bf16[512,640]{1,0:T(8,128)(2,1)} %collective-permute-done.14.refs_6_), channel_id=1, source_target_pairs={{4,6},{6,4},{8,10},{10,8},{5,7},{7,5},{9,11},{11,9},{20,22},{22,20... | collective-permute-start | bytes 1966088 | tf_op jit(solution)/shard_map/ppermute | solution.py:116
  77.5 9.4 %collective-permute-start.17 = (bf16[512,640]{1,0:T(8,128)(2,1)}, bf16[512,640]{1,0:T(8,128)(2,1)}, u32[]{:S(2)}, u32[]{:S(2)}) collective-permute-start(bf16[512,640]{1,0:T(8,128)(2,1)} %collective-permute-done.16.refs_8_), channel_id=1, source_target_pairs={{4,6},{6,4},{8,10},{10,8},{5,7},{7,5},{9,11},{11,9},{20,22},{22,20... | collective-permute-start | bytes 1966088 | tf_op jit(solution)/shard_map/ppermute | solution.py:116
  83.7 7.0 %collective-permute-start.11 = (bf16[128,896]{1,0:T(8,128)(2,1)S(1)}, bf16[128,896]{1,0:T(8,128)(2,1)S(1)}, u32[]{:S(2)}, u32[]{:S(2)}) collective-permute-start(bf16[128,896]{1,0:T(8,128)(2,1)S(1)} %get-tuple-element.23), channel_id=1, source_target_pairs={{4,5},{5,4},{6,7},{7,6},{8,9},{9,8},{10,11},{11,10},{20,21},{21,20... | collective-permute-start | bytes 688136 | tf_op jit(solution)/shard_map/ppermute | solution.py:116
  84.3 68.8 %collective-permute-start.12 = (bf16[128,896]{1,0:T(8,128)(2,1)S(1)}, bf16[128,896]{1,0:T(8,128)(2,1)S(1)}, u32[]{:S(2)}, u32[]{:S(2)}) collective-permute-start(bf16[128,896]{1,0:T(8,128)(2,1)S(1)} %get-tuple-element.24), channel_id=1, source_target_pairs={{4,0},{5,1},{6,2},{7,3},{8,12},{9,13},{10,14},{11,15},{20,16},{21,... | collective-permute-start | bytes 688136 | tf_op jit(solution)/shard_map/ppermute | solution.py:116
  85.6 71.4 %collective-permute-start.13 = (bf16[128,896]{1,0:T(8,128)(2,1)S(1)}, bf16[128,896]{1,0:T(8,128)(2,1)S(1)}, u32[]{:S(2)}, u32[]{:S(2)}) collective-permute-start(bf16[128,896]{1,0:T(8,128)(2,1)S(1)} %get-tuple-element.25), channel_id=1, source_target_pairs={{4,1},{5,0},{6,3},{7,2},{8,13},{9,12},{10,15},{11,14},{20,17},{21,... | collective-permute-start | bytes 688136 | tf_op jit(solution)/shard_map/ppermute | solution.py:116
  88.7 69.7 %collective-permute-start.18 = (bf16[128,640]{1,0:T(8,128)(2,1)S(1)}, bf16[128,640]{1,0:T(8,128)(2,1)S(1)}, u32[]{:S(2)}, u32[]{:S(2)}) collective-permute-start(bf16[128,640]{1,0:T(8,128)(2,1)S(1)} %get-tuple-element.30), channel_id=1, source_target_pairs={{4,5},{5,4},{6,7},{7,6},{8,9},{9,8},{10,11},{11,10},{20,21},{21,20... | collective-permute-start | bytes 491528 | tf_op jit(solution)/shard_map/ppermute | solution.py:116
  89.4 73.4 %collective-permute-start.19 = (bf16[128,640]{1,0:T(8,128)(2,1)S(1)}, bf16[128,640]{1,0:T(8,128)(2,1)S(1)}, u32[]{:S(2)}, u32[]{:S(2)}) collective-permute-start(bf16[128,640]{1,0:T(8,128)(2,1)S(1)} %get-tuple-element.31), channel_id=1, source_target_pairs={{4,0},{5,1},{6,2},{7,3},{8,12},{9,13},{10,14},{11,15},{20,16},{21,... | collective-permute-start | bytes 491528 | tf_op jit(solution)/shard_map/ppermute | solution.py:116
  90.7 75.3 %collective-permute-start.20 = (bf16[128,640]{1,0:T(8,128)(2,1)S(1)}, bf16[128,640]{1,0:T(8,128)(2,1)S(1)}, u32[]{:S(2)}, u32[]{:S(2)}) collective-permute-start(bf16[128,640]{1,0:T(8,128)(2,1)S(1)} %get-tuple-element.32), channel_id=1, source_target_pairs={{4,1},{5,0},{6,3},{7,2},{8,13},{9,12},{10,15},{11,14},{20,17},{21,... | collective-permute-start | bytes 491528 | tf_op jit(solution)/shard_map/ppermute | solution.py:116

commit v4 on v3

--- a/solution.py
+++ b/solution.py
@@ -13,7 +13,10 @@
 LOG2_E = 1.4426950408889634
 DEAD = -1e30
 CORES = 2
-FIRST_SHARE = 7, 12
+FIRST_SHARE = 8, 12
+UNROLL = 4
+EARLY_SLOTS = 0, 1, 2, 3, 4, 5
+HOMES = 0, 4
 VMEM_GRANT = 20 << 20
 
 
@@ -166,16 +169,16 @@
     return jnp.max(functools.reduce(jnp.maximum, masked), axis=0, keepdims=True)
 
 
-def each_unit(size, unit):
-    @pl.loop(0, size // 2)
-    def _(pair):
-        for h in range(2):
-            for side in range(2):
-                unit(pair * 2 + h, side)
-
-    for h in range(size - size % 2, size):
-        for side in range(2):
-            unit(h, side)
+def each_unit(count, unit):
+    whole = count // UNROLL
+
+    @pl.loop(0, whole)
+    def _(group):
+        for i in range(UNROLL):
+            unit(group * UNROLL, i)
+
+    for i in range(count - whole * UNROLL):
+        unit(whole * UNROLL, i)
 
 
 def columns_of(head):
@@ -190,70 +193,76 @@
     return block
 
 
-def early_kernel(seq_size, heads, starts, sizes, *refs):
-    info_ref, code_ref = refs[:2]
-    queries = refs[2:4]
-    whole = refs[4:12]
-    sums, stats = refs[12 : 12 + len(sizes)], refs[12 + len(sizes) :]
+def early_kernel(seq_size, heads, starts, sizes, side, *refs):
+    info_ref, code_ref, queries = refs[:3]
+    whole = refs[3:11]
+    near = refs[11 : 11 + 2 * (len(sizes) - 1)]
+    sums = refs[11 + len(near) : 11 + len(near) + len(sizes)]
+    stats = refs[11 + len(near) + len(sizes) :]
+    rows = queries.shape[0]
 
     @pl.when(info_ref[0] == 1)
     def _():
         for k, (start, size) in enumerate(zip(starts, sizes)):
-
-            def unit(h, side):
+            slots = EARLY_SLOTS[: 4 if k == len(sizes) - 1 else 6]
+
+            def unit(base, i):
+                h = base + i
                 columns = columns_of(h + start)
                 first = (side * heads + h + start) * (seq_size + 1)
-                codes = [(slot, code_ref[first + slot]) for slot in range(4)]
-                if side == 0:
-                    codes.append((0, code_ref[first + seq_size]))
-                masked = masked_scores(
-                    queries[side][:, columns], codes, block_reader(lambda slot: (whole[2 * slot], 0, columns))
-                )
+                codes = [(slot, code_ref[first + slot]) for slot in slots]
+                if HOMES[side] in slots:
+                    codes.append((HOMES[side], code_ref[first + seq_size]))
+
+                def pick(kind, slot):
+                    if slot < 4:
+                        return whole[2 * slot + kind], 0, columns
+                    return near[2 * k + slot - 4], kind * rows, columns_of(h)
+
+                masked = masked_scores(queries[:, columns], codes, block_reader(functools.partial(pick, 0)))
                 top = highest(masked)
-                total, mixed = weigh(
-                    masked, top, codes, block_reader(lambda slot: (whole[2 * slot + 1], 0, columns))
-                )
-                sums[k][h * 2 + side] = mixed
-                stats[k][h * 2 + side, pl.ds(0, 1), :] = top
-                stats[k][h * 2 + side, pl.ds(1, 1), :] = total
+                total, mixed = weigh(masked, top, codes, block_reader(functools.partial(pick, 1)))
+                sums[k][h] = mixed
+                stats[k][h, pl.ds(0, 1), :] = top
+                stats[k][h, pl.ds(1, 1), :] = total
 
             each_unit(size, unit)
 
 
-def late_kernel(seq_size, panel_size, heads, start, size, *refs):
+def late_kernel(seq_size, panel_size, heads, start, size, near, *refs):
     info_ref, code_ref = refs[:2]
-    queries = refs[2:4]
-    sums, stats = refs[4:6]
-    stacked = refs[6:10]
-    outs = refs[10 : 10 + panel_size], refs[10 + panel_size : 10 + 2 * panel_size]
+    queries, sums, stats = refs[2:4], refs[4:6], refs[6:8]
+    stacked = refs[8 : 8 + (4 if near else 2)]
+    outs = refs[8 + len(stacked) : -1]
     held = refs[-1]
     panel = info_ref[1]
     rows = queries[0].shape[0]
     piece = rows // panel_size
-
-    def unit(h, side):
+    slots = range(seq_size - len(stacked), seq_size)
+
+    def unit(base, i):
+        h, side = base // 2 + i // 2, i % 2
         local = columns_of(h)
         first = (side * heads + h + start) * (seq_size + 1)
-        codes = [(slot, code_ref[first + slot]) for slot in range(4, seq_size)]
-        if side == 1:
-            codes.append((4, code_ref[first + seq_size]))
-        read = lambda kind: block_reader(lambda slot: (stacked[slot - 4], kind * rows, local))
+        codes = [(slot, code_ref[first + slot]) for slot in slots]
+        if HOMES[side] in slots:
+            codes.append((HOMES[side], code_ref[first + seq_size]))
+        read = lambda kind: block_reader(lambda slot: (stacked[slot - slots[0]], kind * rows, local))
         masked = masked_scores(queries[side][:, columns_of(h + start)], codes, read(0))
-        before = stats[h * 2 + side, pl.ds(0, 1), :]
+        before = stats[side][h, pl.ds(0, 1), :]
         top = jnp.maximum(before, highest(masked))
         kept = jnp.exp2(before - top)
         total, mixed = weigh(masked, top, codes, read(1))
-        total = total + kept * stats[h * 2 + side, pl.ds(1, 1), :]
-        mixed = mixed + kept * sums[h * 2 + side]
-        spot = (h % 2) * 2 + side
-        held[spot] = (mixed / total).T
+        total = total + kept * stats[side][h, pl.ds(1, 1), :]
+        mixed = mixed + kept * sums[side][h]
+        held[i] = (mixed / total).astype(held.dtype).T
         for shift in range(panel_size):
             first_row = pl.multiple_of(lax.rem(panel + shift, panel_size) * piece, piece)
-            outs[side][shift][:, local] = held[spot, pl.ds(first_row, piece), :].astype(outs[side][shift].dtype)
+            outs[side * panel_size + shift][:, local] = held[i, pl.ds(first_row, piece), :]
 
     @pl.when(info_ref[0] == 1)
     def _():
-        each_unit(size, unit)
+        each_unit(2 * size, unit)
 
 
 def assemble_kernel(panel_size, starts, sizes, aliased, info_ref, *refs):
@@ -338,38 +347,48 @@
     codes = jnp.stack([arranged(position), arranged(guest)]).reshape(-1)
     info = jnp.stack([is_inner.astype(jnp.int32), panel])
 
-    units = [2 * size for size in sizes]
     params = pltpu.CompilerParams(vmem_limit_bytes=VMEM_GRANT)
     cost = lambda count, blocks: pl.CostEstimate(
         flops=count * 4 * rows * blocks * BLOCK * HEAD_DIM,
         bytes_accessed=count * blocks * 4 * BLOCK * HEAD_DIM,
         transcendentals=count * rows * blocks * BLOCK,
     )
-    state = pl.pallas_call(
-        functools.partial(early_kernel, seq_size, heads, starts, sizes),
-        out_shape=[jax.ShapeDtypeStruct((count, HEAD_DIM, rows), jnp.float32) for count in units]
-        + [jax.ShapeDtypeStruct((count, 8, rows), jnp.float32) for count in units],
-        in_specs=[in_smem] * 2 + [in_vmem] * 10,
-        out_specs=[in_vmem] * (2 * chunks),
-        compiler_params=params,
-        cost_estimate=cost(2 * heads, 5),
-        name="early",
-    )(info, codes, queries, guest_query, key_rows, value_rows, *beside, *middle, *middle_beside)
+    ends_beside = [send(x, partner) for x in ends]
+    near = [x for pair in zip(ends, ends_beside) for x in pair]
+    early = []
+    for side, side_queries in enumerate((queries, guest_query)):
+        early.append(
+            pl.pallas_call(
+                functools.partial(early_kernel, seq_size, heads, starts, sizes, side),
+                out_shape=[jax.ShapeDtypeStruct((size, HEAD_DIM, rows), jnp.float32) for size in sizes]
+                + [jax.ShapeDtypeStruct((size, 8, rows), jnp.float32) for size in sizes],
+                in_specs=[in_smem] * 2 + [in_vmem] * (9 + 2 * (chunks - 1)),
+                out_specs=[in_vmem] * (2 * chunks),
+                compiler_params=params,
+                cost_estimate=cost(heads, 6),
+            )(info, codes, side_queries, key_rows, value_rows, *beside, *middle, *middle_beside, *near[:-2])
+        )
 
     own_pieces, guest_pieces = [], []
     for k, (start, size) in enumerate(zip(starts, sizes)):
         far = send(ends[k], across)
-        ends_beside = send(ends[k], partner)
-        far_beside = send(far, partner)
+        stacked = [far, send(far, partner)]
+        if k == chunks - 1:
+            stacked = near[-2:] + stacked
         outs = pl.pallas_call(
-            functools.partial(late_kernel, seq_size, panel_size, heads, start, size),
+            functools.partial(late_kernel, seq_size, panel_size, heads, start, size, len(stacked) == 4),
             out_shape=[jax.ShapeDtypeStruct((rows // panel_size, size * HEAD_DIM), queries.dtype)] * (2 * panel_size),
-            in_specs=[in_smem] * 2 + [in_vmem] * 8,
+            in_specs=[in_smem] * 2 + [in_vmem] * (6 + len(stacked)),
             out_specs=[in_vmem] * (2 * panel_size),
-            scratch_shapes=[pltpu.VMEM((4, rows, HEAD_DIM), jnp.float32)],
+            scratch_shapes=[pltpu.VMEM((UNROLL, rows, HEAD_DIM), queries.dtype)],
             compiler_params=params,
-            cost_estimate=cost(2 * size, 5),
-        )(info, codes, queries, guest_query, state[k], state[chunks + k], ends[k], ends_beside, far, far_beside)
+            cost_estimate=cost(2 * size, len(stacked)),
+        )(
+            *(info, codes, queries, guest_query),
+            *(early[side][k] for side in range(2)),
+            *(early[side][chunks + k] for side in range(2)),
+            *stacked,
+        )
         both = ("seq", "panel")
         for shift in range(panel_size):
             mine, theirs = outs[shift], outs[panel_size + shift]

time: 168 us -> 134 us (0.80)
  waiting for transfers between devices: 113 us -> 49.5 us
  starting transfers between devices: 37.1 us -> 62.7 us
  Pallas kernels: 10 us -> 13.2 us
    ppermute x21, waiting for transfers between devices: 113 us -> 49.5 us  [send(): return lax.ppermute(value, axes, pairs)]
    ppermute x21, starting transfers between devices: 37.1 us -> 62.7 us  [send(): return lax.ppermute(value, axes, pairs)]
    pallas_call x1 -> x2, Pallas kernels: 2.35 us -> 4.98 us  [relayed(): pl.pallas_call(functools.partial(early_kernel, seq_size, heads, starts, s...]
    unnamed x10 -> x16, local copies, waits for them, and re-layouts: 2.27 us -> 4.05 us
  transfers between devices with their start and end apart: 21 -> 21, of which waited for: 5 -> 7; matrix products, arithmetic and copies ran while one was open for 3% -> 3% of each run, Pallas kernels for 5% -> 7%
where the time goes in v4:
time: 134 us; the launch traced here: 133 us
  starting transfers between devices  62.7 us (47%)
  waiting for transfers between devices  49.5 us (37%)
  Pallas kernels  13.2 us (10%)
  local copies, waits for them, and re-layouts  5.82 us (4%)
  other arithmetic  1.62 us (1%)
    ppermute x21, starting transfers between devices, send(): return lax.ppermute(value, axes, pairs)  62.7 us
    ppermute x21, waiting for transfers between devices, send(): return lax.ppermute(value, axes, pairs)  49.5 us
    pallas_call x2, Pallas kernels, relayed(): pl.pallas_call(functools.partial(early_kernel, seq_size, heads, starts, s...  4.98 us
    unnamed x16, local copies, waits for them, and re-layouts  4.05 us
    pallas_call x2, Pallas kernels, relayed(): pl.pallas_call(functools.partial(late_kernel, seq_size, panel_size, heads...  3.11 us
  transfers between devices with their start and end apart: 21, of which 7 were waited for; matrix products, arithmetic and copies ran while one was open for 3% of the time, Pallas kernels for 7%

profile of v4, /device:TPU:0, one launch (start us, length us, event | category | flops | bytes accessed | tf_op | source)
XLA Modules:
  0.0 133.2 jit_solution(5923824267707913139)
XLA Ops:
  0.0 2.5 %pack.1 = (bf16[512,1024]{1,0:T(8,128)(2,1)}, bf16[512,512]{1,0:T(8,128)(2,1)}) custom-call(bf16[256,1536]{1,0:T(8,128)(2,1)} %refs_3_.3, bf16[256,1536]{1,0:T(8,128)(2,1)} %refs_4_.3), custom_call_target="tpu_custom_call" | custom-call | tf_op jit(solution)/shard_map/pack/pallas_call | solution.py:317
  2.5 5.2 %collective-permute-start.7 = (bf16[512,1024]{1,0:T(8,128)(2,1)}, bf16[512,1024]{1,0:T(8,128)(2,1)S(1)}, u32[]{:S(2)}, u32[]{:S(2)}) collective-permute-start(bf16[512,1024]{1,0:T(8,128)(2,1)} %get-tuple-element.23), channel_id=1, source_target_pairs={{0,4},{2,6},{12,8},{14,10},{1,5},{3,7},{13,9},{15,11},{16,20},{18,... | collective-permute-start | bytes 3145736 | tf_op jit(solution)/shard_map/ppermute | solution.py:119
  7.7 0.7 collective-permute-start.3
  8.4 1.5 %collective-permute-start.4 = (bf16[256,1536]{1,0:T(8,128)(2,1)}, bf16[256,1536]{1,0:T(8,128)(2,1)}, u32[]{:S(2)}, u32[]{:S(2)}) collective-permute-start(bf16[256,1536]{1,0:T(8,128)(2,1)} %refs_4_.3), channel_id=1, source_target_pairs={{4,8},{6,10},{8,4},{10,6},{5,9},{7,11},{9,5},{11,7},{20,24},{22,26... | collective-permute-start | bytes 2359304 | tf_op jit(solution)/shard_map/ppermute | solution.py:119
  10.0 0.7 collective-permute-start.1
  10.7 6.9 %collective-permute-start.14 = (bf16[512,512]{1,0:T(8,128)(2,1)}, bf16[512,512]{1,0:T(8,128)(2,1)}, u32[]{:S(2)}, u32[]{:S(2)}) collective-permute-start(bf16[512,512]{1,0:T(8,128)(2,1)} %get-tuple-element.36), channel_id=1, source_target_pairs={{0,4},{2,6},{12,8},{14,10},{1,5},{3,7},{13,9},{15,11},{16,20},{18,... | collective-permute-start | bytes 1572872 | tf_op jit(solution)/shard_map/ppermute | solution.py:119
  17.6 0.1 copy.22
  17.8 0.9 constant_dynamic-slice_fusion
  18.6 0.1 iota_compare_fusion.2
  18.7 0.1 fusion.1
  19.0 0.1 copy.25
  19.2 0.1 fusion.3
  19.4 12.1 %collective-permute-done.7.refs_11_ = bf16[512,1024]{1,0:T(8,128)(2,1)S(1)} collective-permute-done((bf16[512,1024]{1,0:T(8,128)(2,1)}, bf16[512,1024]{1,0:T(8,128)(2,1)S(1)}, u32[]{:S(2)}, u32[]{:S(2)}) %collective-permute-start.7) | collective-permute-done | bytes 1048608 | tf_op jit(solution)/shard_map/ppermute | solution.py:119
  31.5 1.6 %collective-permute-start.9 = (bf16[512,1024]{1,0:T(8,128)(2,1)S(1)}, bf16[512,1024]{1,0:T(8,128)(2,1)}, u32[]{:S(2)}, u32[]{:S(2)}) collective-permute-start(bf16[512,1024]{1,0:T(8,128)(2,1)S(1)} %collective-permute-done.7.refs_11_), channel_id=1, source_target_pairs={{4,8},{6,10},{8,4},{10,6},{5,9},{7,11},{9,5},{11,7},{20,24},{22,26... | collective-permute-start | bytes 3145736 | tf_op jit(solution)/shard_map/ppermute | solution.py:119
  33.2 8.4 %collective-permute-done.14.refs_8_ = bf16[512,512]{1,0:T(8,128)(2,1)} collective-permute-done((bf16[512,512]{1,0:T(8,128)(2,1)}, bf16[512,512]{1,0:T(8,128)(2,1)}, u32[]{:S(2)}, u32[]{:S(2)}) %collective-permute-start.14) | collective-permute-done | bytes 524320 | tf_op jit(solution)/shard_map/ppermute | solution.py:119
  41.6 0.7 collective-permute-start.2
  42.3 0.7 multiply_reduce_fusion.5
  43.1 1.5 %collective-permute-start.16 = (bf16[512,512]{1,0:T(8,128)(2,1)}, bf16[512,512]{1,0:T(8,128)(2,1)}, u32[]{:S(2)}, u32[]{:S(2)}) collective-permute-start(bf16[512,512]{1,0:T(8,128)(2,1)} %collective-permute-done.14.refs_8_), channel_id=1, source_target_pairs={{4,8},{6,10},{8,4},{10,6},{5,9},{7,11},{9,5},{11,7},{20,24},{22,26... | collective-permute-start | bytes 1572872 | tf_op jit(solution)/shard_map/ppermute | solution.py:119
  44.6 1.7 %collective-permute-start.8 = (bf16[512,1024]{1,0:T(8,128)(2,1)S(1)}, bf16[512,1024]{1,0:T(8,128)(2,1)}, u32[]{:S(2)}, u32[]{:S(2)}) collective-permute-start(bf16[512,1024]{1,0:T(8,128)(2,1)S(1)} %collective-permute-done.7.refs_11_), channel_id=1, source_target_pairs={{4,6},{6,4},{8,10},{10,8},{5,7},{7,5},{9,11},{11,9},{20,22},{22,20... | collective-permute-start | bytes 3145736 | tf_op jit(solution)/shard_map/ppermute | solution.py:119
  46.3 0.9 copy-done.1
  47.2 1.6 %collective-permute-start.5 = (bf16[256,1536]{1,0:T(8,128)(2,1)S(1)}, bf16[256,1536]{1,0:T(8,128)(2,1)}, u32[]{:S(2)}, u32[]{:S(2)}) collective-permute-start(bf16[256,1536]{1,0:T(8,128)(2,1)S(1)} %collective-permute-done.3.refs_7_), channel_id=1, source_target_pairs={{4,6},{6,4},{8,10},{10,8},{5,7},{7,5},{9,11},{11,9},{20,22},{22,20... | collective-permute-start | bytes 2359304 | tf_op jit(solution)/shard_map/ppermute | solution.py:119
  48.8 0.9 copy-done.4
  49.7 1.6 %collective-permute-start.6 = (bf16[256,1536]{1,0:T(8,128)(2,1)}, bf16[256,1536]{1,0:T(8,128)(2,1)}, u32[]{:S(2)}, u32[]{:S(2)}) collective-permute-start(bf16[256,1536]{1,0:T(8,128)(2,1)} %collective-permute-done.4.refs_8_), channel_id=1, source_target_pairs={{4,6},{6,4},{8,10},{10,8},{5,7},{7,5},{9,11},{11,9},{20,22},{22,20... | collective-permute-start | bytes 2359304 | tf_op jit(solution)/shard_map/ppermute | solution.py:119
  51.2 1.6 %collective-permute-start.10 = (bf16[512,1024]{1,0:T(8,128)(2,1)}, bf16[512,1024]{1,0:T(8,128)(2,1)}, u32[]{:S(2)}, u32[]{:S(2)}) collective-permute-start(bf16[512,1024]{1,0:T(8,128)(2,1)} %collective-permute-done.9.refs_8_), channel_id=1, source_target_pairs={{4,6},{6,4},{8,10},{10,8},{5,7},{7,5},{9,11},{11,9},{20,22},{22,20... | collective-permute-start | bytes 3145736 | tf_op jit(solution)/shard_map/ppermute | solution.py:119
  53.1 28.0 %collective-permute-start = (bf16[256,1536]{1,0:T(8,128)(2,1)S(1)}, bf16[256,1536]{1,0:T(8,128)(2,1)S(1)}, u32[]{:S(2)}, u32[]{:S(2)}) collective-permute-start(bf16[256,1536]{1,0:T(8,128)(2,1)S(1)} %copy-done), channel_id=1, source_target_pairs={{0,4},{2,6},{12,8},{14,10},{1,5},{3,7},{13,9},{15,11},{16,20},{18,... | collective-permute-start | bytes 2359304 | tf_op jit(solution)/shard_map/ppermute | solution.py:119
  81.1 0.1 multiply_reduce_fusion.1
  81.3 0.1 copy.29
  81.4 1.4 %collective-permute-start.15 = (bf16[512,512]{1,0:T(8,128)(2,1)}, bf16[512,512]{1,0:T(8,128)(2,1)}, u32[]{:S(2)}, u32[]{:S(2)}) collective-permute-start(bf16[512,512]{1,0:T(8,128)(2,1)} %collective-permute-done.14.refs_8_), channel_id=1, source_target_pairs={{4,6},{6,4},{8,10},{10,8},{5,7},{7,5},{9,11},{11,9},{20,22},{22,20... | collective-permute-start | bytes 1572872 | tf_op jit(solution)/shard_map/ppermute | solution.py:119
  82.9 1.5 %collective-permute-start.17 = (bf16[512,512]{1,0:T(8,128)(2,1)}, bf16[512,512]{1,0:T(8,128)(2,1)}, u32[]{:S(2)}, u32[]{:S(2)}) collective-permute-start(bf16[512,512]{1,0:T(8,128)(2,1)} %collective-permute-done.16.refs_10_), channel_id=1, source_target_pairs={{4,6},{6,4},{8,10},{10,8},{5,7},{7,5},{9,11},{11,9},{20,22},{22,20... | collective-permute-start | bytes 1572872 | tf_op jit(solution)/shard_map/ppermute | solution.py:119
  84.6 1.1 copy-done.2
  85.7 1.1 copy-done.5
  86.8 2.5 %shard_map.73 = (f32[8,128,256]{2,1,0:T(8,128)S(1)}, f32[4,128,256]{2,1,0:T(8,128)S(1)}, f32[8,8,256]{2,1,0:T(8,128)S(1)}, f32[4,8,256]{2,1,0:T(8,128)S(1)}) custom-call(s32[2]{0:T(128)S(1)} %pad_add_fusion.3.refs_0_.info_ref, s32[216]{0:T(256)S(1)} %reshape.60.refs_1_, bf16[256,1536]{1,0:T(8,128)(2,1)S(1)} %copy-done, bf16[256,1536]{1,0:T(8,128)(2,1)} %refs_3_.3, ...), custom_call_target="tpu_custom_call" | custom-call | flops 1207959552 | bytes 4718592 | tf_op jit(solution)/shard_map/pallas_call | solution.py:361
  89.4 7.5 %collective-permute-done.refs_2_.refs_3_ = bf16[256,1536]{1,0:T(8,128)(2,1)S(1)} collective-permute-done((bf16[256,1536]{1,0:T(8,128)(2,1)S(1)}, bf16[256,1536]{1,0:T(8,128)(2,1)S(1)}, u32[]{:S(2)}, u32[]{:S(2)}) %collective-permute-start) | collective-permute-done | bytes 786464 | tf_op jit(solution)/shard_map/ppermute | solution.py:119
  96.9 2.4 %shard_map.74 = (f32[8,128,256]{2,1,0:T(8,128)S(1)}, f32[4,128,256]{2,1,0:T(8,128)S(1)}, f32[8,8,256]{2,1,0:T(8,128)S(1)}, f32[4,8,256]{2,1,0:T(8,128)S(1)}) custom-call(s32[2]{0:T(128)S(1)} %pad_add_fusion.3.refs_0_.info_ref, s32[216]{0:T(256)S(1)} %reshape.60.refs_1_, bf16[256,1536]{1,0:T(8,128)(2,1)S(1)} %collective-permute-done.refs_2_.refs_3_, ...), custom_call_target="tpu_custom_call" | custom-call | flops 1207959552 | bytes 4718592 | tf_op jit(solution)/shard_map/pallas_call | solution.py:361
  99.4 1.6 %shard_map.75 = (bf16[128,1024]{1,0:T(8,128)(2,1)S(1)}, bf16[128,1024]{1,0:T(8,128)(2,1)S(1)}, bf16[128,1024]{1,0:T(8,128)(2,1)S(1)}, bf16[128,1024]{1,0:T(8,128)(2,1)S(1)}) custom-call(s32[2]{0:T(128)S(1)} %pad_add_fusion.3.refs_0_.info_ref, s32[216]{0:T(256)S(1)} %reshape.60.refs_1_, bf16[256,1536]{1,0:T(8,128)(2,1)S(1)} %copy-done, ...), custom_call_target="tpu_custom_call" | custom-call | flops 536870912 | bytes 2097152 | tf_op jit(solution)/shard_map/pallas_call | solution.py:378
  100.9 0.7 collective-permute-start.11
  101.6 1.3 collective-permute-start.12
  102.9 1.3 collective-permute-start.13
  104.2 1.5 %shard_map.77 = (bf16[128,512]{1,0:T(8,128)(2,1)S(1)}, bf16[128,512]{1,0:T(8,128)(2,1)S(1)}, bf16[128,512]{1,0:T(8,128)(2,1)S(1)}, bf16[128,512]{1,0:T(8,128)(2,1)S(1)}) custom-call(s32[2]{0:T(128)S(1)} %pad_add_fusion.3.refs_0_.info_ref, s32[216]{0:T(256)S(1)} %reshape.60.refs_1_, bf16[256,1536]{1,0:T(8,128)(2,1)S(1)} %copy-done, ...), custom_call_target="tpu_custom_call" | custom-call | flops 536870912 | bytes 2097152 | tf_op jit(solution)/shard_map/pallas_call | solution.py:378
  105.8 0.7 collective-permute-start.18
  106.5 1.3 collective-permute-start.19
  107.8 1.3 collective-permute-start.20
  109.1 14.4 %collective-permute-done.12.refs_2_ = bf16[128,1024]{1,0:T(8,128)(2,1)S(1)} collective-permute-done((bf16[128,1024]{1,0:T(8,128)(2,1)S(1)}, bf16[128,1024]{1,0:T(8,128)(2,1)S(1)}, u32[]{:S(2)}, u32[]{:S(2)}) %collective-permute-start.12) | collective-permute-done | bytes 262176 | tf_op jit(solution)/shard_map/ppermute | solution.py:119
  123.5 3.5 %collective-permute-done.13.refs_3_ = bf16[128,1024]{1,0:T(8,128)(2,1)S(1)} collective-permute-done((bf16[128,1024]{1,0:T(8,128)(2,1)S(1)}, bf16[128,1024]{1,0:T(8,128)(2,1)S(1)}, u32[]{:S(2)}, u32[]{:S(2)}) %collective-permute-start.13) | collective-permute-done | bytes 262176 | tf_op jit(solution)/shard_map/ppermute | solution.py:119
  127.0 1.4 %shard_map.76.refs_0_ = bf16[128,3072]{1,0:T(8,128)(2,1)} custom-call(s32[2]{0:T(128)S(1)} %pad_add_fusion.3.refs_0_.info_ref, bf16[128,1024]{1,0:T(8,128)(2,1)S(1)} %get-tuple-element.28.refs_0_, bf16[128,1024]{1,0:T(8,128)(2,1)S(1)} %collective-permute-done.11.refs_1_, bf16[128,1024]{1,0:T(8,128)(2,1)S(1)} %collective-permute-done.12.refs_2_, ...), custom_call_target="tpu_custom_call" | custom-call | tf_op jit(solution)/shard_map/pallas_call | solution.py:407
  128.4 2.2 %collective-permute-done.19.refs_3_ = bf16[128,512]{1,0:T(8,128)(2,1)S(1)} collective-permute-done((bf16[128,512]{1,0:T(8,128)(2,1)S(1)}, bf16[128,512]{1,0:T(8,128)(2,1)S(1)}, u32[]{:S(2)}, u32[]{:S(2)}) %collective-permute-start.19) | collective-permute-done | bytes 131104 | tf_op jit(solution)/shard_map/ppermute | solution.py:119
  130.5 1.4 %collective-permute-done.20.refs_4_ = bf16[128,512]{1,0:T(8,128)(2,1)S(1)} collective-permute-done((bf16[128,512]{1,0:T(8,128)(2,1)S(1)}, bf16[128,512]{1,0:T(8,128)(2,1)S(1)}, u32[]{:S(2)}, u32[]{:S(2)}) %collective-permute-start.20) | collective-permute-done | bytes 131104 | tf_op jit(solution)/shard_map/ppermute | solution.py:119
  131.9 1.3 shard_map.78
  (48 shorter events, 1.0 us)
Async XLA Ops:
  0.0 17.6 %copy-start.7 = (s32[12,16,8]{1,2,0:T(8,128)S(1)}, s32[12,16,8]{1,2,0:T(8,128)}, u32[]{:S(2)}) copy-start(s32[12,16,8]{1,2,0:T(8,128)} %param.10) | copy-start | bytes 18436
  2.5 50.5 %copy-start = (bf16[256,1536]{1,0:T(8,128)(2,1)S(1)}, bf16[256,1536]{1,0:T(8,128)(2,1)}, u32[]{:S(2)}) copy-start(bf16[256,1536]{1,0:T(8,128)(2,1)} %refs_2_.5) | copy-start | bytes 2359300
  2.5 28.9 %collective-permute-start.7 = (bf16[512,1024]{1,0:T(8,128)(2,1)}, bf16[512,1024]{1,0:T(8,128)(2,1)S(1)}, u32[]{:S(2)}, u32[]{:S(2)}) collective-permute-start(bf16[512,1024]{1,0:T(8,128)(2,1)} %get-tuple-element.23), channel_id=1, source_target_pairs={{0,4},{2,6},{12,8},{14,10},{1,5},{3,7},{13,9},{15,11},{16,20},{18,... | collective-permute-start | bytes 3145736 | tf_op jit(solution)/shard_map/ppermute | solution.py:119
  7.7 35.4 %collective-permute-start.3 = (bf16[256,1536]{1,0:T(8,128)(2,1)}, bf16[256,1536]{1,0:T(8,128)(2,1)S(1)}, u32[]{:S(2)}, u32[]{:S(2)}) collective-permute-start(bf16[256,1536]{1,0:T(8,128)(2,1)} %refs_3_.3), channel_id=1, source_target_pairs={{4,8},{6,10},{8,4},{10,6},{5,9},{7,11},{9,5},{11,7},{20,24},{22,26... | collective-permute-start | bytes 2359304 | tf_op jit(solution)/shard_map/ppermute | solution.py:119
  8.4 36.2 %collective-permute-start.4 = (bf16[256,1536]{1,0:T(8,128)(2,1)}, bf16[256,1536]{1,0:T(8,128)(2,1)}, u32[]{:S(2)}, u32[]{:S(2)}) collective-permute-start(bf16[256,1536]{1,0:T(8,128)(2,1)} %refs_4_.3), channel_id=1, source_target_pairs={{4,8},{6,10},{8,4},{10,6},{5,9},{7,11},{9,5},{11,7},{20,24},{22,26... | collective-permute-start | bytes 2359304 | tf_op jit(solution)/shard_map/ppermute | solution.py:119
  10.0 36.4 %collective-permute-start.1 = (bf16[256,1536]{1,0:T(8,128)(2,1)}, bf16[256,1536]{1,0:T(8,128)(2,1)S(1)}, u32[]{:S(2)}, u32[]{:S(2)}) collective-permute-start(bf16[256,1536]{1,0:T(8,128)(2,1)} %refs_3_.3), channel_id=1, source_target_pairs={{4,6},{6,4},{8,10},{10,8},{5,7},{7,5},{9,11},{11,9},{20,22},{22,20... | collective-permute-start | bytes 2359304 | tf_op jit(solution)/shard_map/ppermute | solution.py:119
  10.7 30.9 %collective-permute-start.14 = (bf16[512,512]{1,0:T(8,128)(2,1)}, bf16[512,512]{1,0:T(8,128)(2,1)}, u32[]{:S(2)}, u32[]{:S(2)}) collective-permute-start(bf16[512,512]{1,0:T(8,128)(2,1)} %get-tuple-element.36), channel_id=1, source_target_pairs={{0,4},{2,6},{12,8},{14,10},{1,5},{3,7},{13,9},{15,11},{16,20},{18,... | collective-permute-start | bytes 1572872 | tf_op jit(solution)/shard_map/ppermute | solution.py:119
  31.5 19.7 %collective-permute-start.9 = (bf16[512,1024]{1,0:T(8,128)(2,1)S(1)}, bf16[512,1024]{1,0:T(8,128)(2,1)}, u32[]{:S(2)}, u32[]{:S(2)}) collective-permute-start(bf16[512,1024]{1,0:T(8,128)(2,1)S(1)} %collective-permute-done.7.refs_11_), channel_id=1, source_target_pairs={{4,8},{6,10},{8,4},{10,6},{5,9},{7,11},{9,5},{11,7},{20,24},{22,26... | collective-permute-start | bytes 3145736 | tf_op jit(solution)/shard_map/ppermute | solution.py:119
  41.6 7.2 %collective-permute-start.2 = (bf16[256,1536]{1,0:T(8,128)(2,1)}, bf16[256,1536]{1,0:T(8,128)(2,1)S(1)}, u32[]{:S(2)}, u32[]{:S(2)}) collective-permute-start(bf16[256,1536]{1,0:T(8,128)(2,1)} %refs_4_.3), channel_id=1, source_target_pairs={{4,6},{6,4},{8,10},{10,8},{5,7},{7,5},{9,11},{11,9},{20,22},{22,20... | collective-permute-start | bytes 2359304 | tf_op jit(solution)/shard_map/ppermute | solution.py:119
  43.1 10.0 %collective-permute-start.16 = (bf16[512,512]{1,0:T(8,128)(2,1)}, bf16[512,512]{1,0:T(8,128)(2,1)}, u32[]{:S(2)}, u32[]{:S(2)}) collective-permute-start(bf16[512,512]{1,0:T(8,128)(2,1)} %collective-permute-done.14.refs_8_), channel_id=1, source_target_pairs={{4,8},{6,10},{8,4},{10,6},{5,9},{7,11},{9,5},{11,7},{20,24},{22,26... | collective-permute-start | bytes 1572872 | tf_op jit(solution)/shard_map/ppermute | solution.py:119
  44.6 39.9 %collective-permute-start.8 = (bf16[512,1024]{1,0:T(8,128)(2,1)S(1)}, bf16[512,1024]{1,0:T(8,128)(2,1)}, u32[]{:S(2)}, u32[]{:S(2)}) collective-permute-start(bf16[512,1024]{1,0:T(8,128)(2,1)S(1)} %collective-permute-done.7.refs_11_), channel_id=1, source_target_pairs={{4,6},{6,4},{8,10},{10,8},{5,7},{7,5},{9,11},{11,9},{20,22},{22,20... | collective-permute-start | bytes 3145736 | tf_op jit(solution)/shard_map/ppermute | solution.py:119
  46.3 0.9 copy-start.1
  47.2 34.2 %collective-permute-start.5 = (bf16[256,1536]{1,0:T(8,128)(2,1)S(1)}, bf16[256,1536]{1,0:T(8,128)(2,1)}, u32[]{:S(2)}, u32[]{:S(2)}) collective-permute-start(bf16[256,1536]{1,0:T(8,128)(2,1)S(1)} %collective-permute-done.3.refs_7_), channel_id=1, source_target_pairs={{4,6},{6,4},{8,10},{10,8},{5,7},{7,5},{9,11},{11,9},{20,22},{22,20... | collective-permute-start | bytes 2359304 | tf_op jit(solution)/shard_map/ppermute | solution.py:119
  48.8 0.9 copy-start.4
  49.7 33.2 %collective-permute-start.6 = (bf16[256,1536]{1,0:T(8,128)(2,1)}, bf16[256,1536]{1,0:T(8,128)(2,1)}, u32[]{:S(2)}, u32[]{:S(2)}) collective-permute-start(bf16[256,1536]{1,0:T(8,128)(2,1)} %collective-permute-done.4.refs_8_), channel_id=1, source_target_pairs={{4,6},{6,4},{8,10},{10,8},{5,7},{7,5},{9,11},{11,9},{20,22},{22,20... | collective-permute-start | bytes 2359304 | tf_op jit(solution)/shard_map/ppermute | solution.py:119
  51.2 48.1 %collective-permute-start.10 = (bf16[512,1024]{1,0:T(8,128)(2,1)}, bf16[512,1024]{1,0:T(8,128)(2,1)}, u32[]{:S(2)}, u32[]{:S(2)}) collective-permute-start(bf16[512,1024]{1,0:T(8,128)(2,1)} %collective-permute-done.9.refs_8_), channel_id=1, source_target_pairs={{4,6},{6,4},{8,10},{10,8},{5,7},{7,5},{9,11},{11,9},{20,22},{22,20... | collective-permute-start | bytes 3145736 | tf_op jit(solution)/shard_map/ppermute | solution.py:119
  53.1 43.9 %collective-permute-start = (bf16[256,1536]{1,0:T(8,128)(2,1)S(1)}, bf16[256,1536]{1,0:T(8,128)(2,1)S(1)}, u32[]{:S(2)}, u32[]{:S(2)}) collective-permute-start(bf16[256,1536]{1,0:T(8,128)(2,1)S(1)} %copy-done), channel_id=1, source_target_pairs={{0,4},{2,6},{12,8},{14,10},{1,5},{3,7},{13,9},{15,11},{16,20},{18,... | collective-permute-start | bytes 2359304 | tf_op jit(solution)/shard_map/ppermute | solution.py:119
  81.4 22.8 %collective-permute-start.15 = (bf16[512,512]{1,0:T(8,128)(2,1)}, bf16[512,512]{1,0:T(8,128)(2,1)}, u32[]{:S(2)}, u32[]{:S(2)}) collective-permute-start(bf16[512,512]{1,0:T(8,128)(2,1)} %collective-permute-done.14.refs_8_), channel_id=1, source_target_pairs={{4,6},{6,4},{8,10},{10,8},{5,7},{7,5},{9,11},{11,9},{20,22},{22,20... | collective-permute-start | bytes 1572872 | tf_op jit(solution)/shard_map/ppermute | solution.py:119
  82.9 21.4 %collective-permute-start.17 = (bf16[512,512]{1,0:T(8,128)(2,1)}, bf16[512,512]{1,0:T(8,128)(2,1)}, u32[]{:S(2)}, u32[]{:S(2)}) collective-permute-start(bf16[512,512]{1,0:T(8,128)(2,1)} %collective-permute-done.16.refs_10_), channel_id=1, source_target_pairs={{4,6},{6,4},{8,10},{10,8},{5,7},{7,5},{9,11},{11,9},{20,22},{22,20... | collective-permute-start | bytes 1572872 | tf_op jit(solution)/shard_map/ppermute | solution.py:119
  84.6 1.1 copy-start.2
  85.7 1.1 copy-start.5
  86.8 10.1 %copy-start.3 = (bf16[256,1536]{1,0:T(8,128)(2,1)S(1)}, bf16[256,1536]{1,0:T(8,128)(2,1)}, u32[]{:S(2)}) copy-start(bf16[256,1536]{1,0:T(8,128)(2,1)} %copy-done.1) | copy-start | bytes 2359300
  86.8 10.1 %copy-start.6 = (bf16[256,1536]{1,0:T(8,128)(2,1)S(1)}, bf16[256,1536]{1,0:T(8,128)(2,1)}, u32[]{:S(2)}) copy-start(bf16[256,1536]{1,0:T(8,128)(2,1)} %copy-done.4) | copy-start | bytes 2359300
  100.9 6.8 %collective-permute-start.11 = (bf16[128,1024]{1,0:T(8,128)(2,1)S(1)}, bf16[128,1024]{1,0:T(8,128)(2,1)S(1)}, u32[]{:S(2)}, u32[]{:S(2)}) collective-permute-start(bf16[128,1024]{1,0:T(8,128)(2,1)S(1)} %get-tuple-element.29), channel_id=1, source_target_pairs={{4,5},{5,4},{6,7},{7,6},{8,9},{9,8},{10,11},{11,10},{20,21},{21,20... | collective-permute-start | bytes 786440 | tf_op jit(solution)/shard_map/ppermute | solution.py:119
  101.6 21.9 %collective-permute-start.12 = (bf16[128,1024]{1,0:T(8,128)(2,1)S(1)}, bf16[128,1024]{1,0:T(8,128)(2,1)S(1)}, u32[]{:S(2)}, u32[]{:S(2)}) collective-permute-start(bf16[128,1024]{1,0:T(8,128)(2,1)S(1)} %get-tuple-element.30), channel_id=1, source_target_pairs={{4,0},{5,1},{6,2},{7,3},{8,12},{9,13},{10,14},{11,15},{20,16},{21,... | collective-permute-start | bytes 786440 | tf_op jit(solution)/shard_map/ppermute | solution.py:119
  102.9 24.1 %collective-permute-start.13 = (bf16[128,1024]{1,0:T(8,128)(2,1)S(1)}, bf16[128,1024]{1,0:T(8,128)(2,1)S(1)}, u32[]{:S(2)}, u32[]{:S(2)}) collective-permute-start(bf16[128,1024]{1,0:T(8,128)(2,1)S(1)} %get-tuple-element.31), channel_id=1, source_target_pairs={{4,1},{5,0},{6,3},{7,2},{8,13},{9,12},{10,15},{11,14},{20,17},{21,... | collective-permute-start | bytes 786440 | tf_op jit(solution)/shard_map/ppermute | solution.py:119
  105.8 22.5 %collective-permute-start.18 = (bf16[128,512]{1,0:T(8,128)(2,1)S(1)}, bf16[128,512]{1,0:T(8,128)(2,1)S(1)}, u32[]{:S(2)}, u32[]{:S(2)}) collective-permute-start(bf16[128,512]{1,0:T(8,128)(2,1)S(1)} %get-tuple-element.38), channel_id=1, source_target_pairs={{4,5},{5,4},{6,7},{7,6},{8,9},{9,8},{10,11},{11,10},{20,21},{21,20... | collective-permute-start | bytes 393224 | tf_op jit(solution)/shard_map/ppermute | solution.py:119
  106.5 24.0 %collective-permute-start.19 = (bf16[128,512]{1,0:T(8,128)(2,1)S(1)}, bf16[128,512]{1,0:T(8,128)(2,1)S(1)}, u32[]{:S(2)}, u32[]{:S(2)}) collective-permute-start(bf16[128,512]{1,0:T(8,128)(2,1)S(1)} %get-tuple-element.39), channel_id=1, source_target_pairs={{4,0},{5,1},{6,2},{7,3},{8,12},{9,13},{10,14},{11,15},{20,16},{21,... | collective-permute-start | bytes 393224 | tf_op jit(solution)/shard_map/ppermute | solution.py:119
  107.8 24.1 %collective-permute-start.20 = (bf16[128,512]{1,0:T(8,128)(2,1)S(1)}, bf16[128,512]{1,0:T(8,128)(2,1)S(1)}, u32[]{:S(2)}, u32[]{:S(2)}) collective-permute-start(bf16[128,512]{1,0:T(8,128)(2,1)S(1)} %get-tuple-element.40), channel_id=1, source_target_pairs={{4,1},{5,0},{6,3},{7,2},{8,13},{9,12},{10,15},{11,14},{20,17},{21,... | collective-permute-start | bytes 393224 | tf_op jit(solution)/shard_map/ppermute | solution.py:119

commit v5 on v4

--- a/solution.py
+++ b/solution.py
@@ -17,6 +17,7 @@
 UNROLL = 4
 EARLY_SLOTS = 0, 1, 2, 3, 4, 5
 HOMES = 0, 4
+EARLY_CALLS = (0, (0, 1)), (1, (0,)), (1, (1,))
 VMEM_GRANT = 20 << 20
 
 
@@ -119,16 +120,15 @@
     return lax.ppermute(value, axes, pairs)
 
 
-def pack_kernel(starts, sizes, key_ref, value_ref, *refs):
-    outs, sems = refs[:-1], refs[-1]
+def pack_kernel(starts, sizes, key_ref, value_ref, query_ref, *refs):
+    outs, query_outs, sems = refs[: len(sizes)], refs[len(sizes) : -1], refs[-1]
     rows = key_ref.shape[0]
     copies = []
     for k, (start, size) in enumerate(zip(starts, sizes)):
         columns = pl.ds(start * HEAD_DIM, size * HEAD_DIM)
-        for kind, ref in enumerate((key_ref, value_ref)):
-            copies.append(
-                pltpu.make_async_copy(ref.at[:, columns], outs[k].at[pl.ds(kind * rows, rows), :], sems.at[k, kind])
-            )
+        targets = outs[k].at[pl.ds(0, rows), :], outs[k].at[pl.ds(rows, rows), :], query_outs[k]
+        for kind, ref in enumerate((key_ref, value_ref, query_ref)):
+            copies.append(pltpu.make_async_copy(ref.at[:, columns], targets[kind], sems.at[k, kind]))
             copies[-1].start()
     for copy in copies:
         copy.wait()
@@ -193,40 +193,60 @@
     return block
 
 
-def early_kernel(seq_size, heads, starts, sizes, side, *refs):
-    info_ref, code_ref, queries = refs[:3]
-    whole = refs[3:11]
-    near = refs[11 : 11 + 2 * (len(sizes) - 1)]
-    sums = refs[11 + len(near) : 11 + len(near) + len(sizes)]
-    stats = refs[11 + len(near) + len(sizes) :]
-    rows = queries.shape[0]
+def early_kernel(seq_size, heads, starts, sizes, chunks, side, *refs):
+    info_ref, code_ref = refs[:2]
+    count = len(chunks)
+    near_count = sum(k < len(sizes) - 1 for k in chunks)
+    whole = refs[2:10]
+    refs = refs[10:]
+    queries, refs = refs[:count], refs[count:]
+    near, refs = refs[: 2 * near_count], refs[2 * near_count :]
+    sums, stats = refs[:count], refs[count : 2 * count]
+    held, sems = refs[2 * count :]
+    groups = [
+        (n, k, low, min(low + UNROLL, sizes[k])) for n, k in enumerate(chunks) for low in range(0, sizes[k], UNROLL)
+    ]
+
+    def loads(g):
+        _, k, low, high = groups[g]
+        width = (high - low) * HEAD_DIM
+        source = pl.ds((starts[k] + low) * HEAD_DIM, width)
+        return [
+            pltpu.make_async_copy(
+                ref.at[:, source], held.at[g % 2, index, :, pl.ds(0, width)], sems.at[g % 2, index]
+            )
+            for index, ref in enumerate(whole)
+        ]
 
     @pl.when(info_ref[0] == 1)
     def _():
-        for k, (start, size) in enumerate(zip(starts, sizes)):
+        for copy in loads(0):
+            copy.start()
+        for g, (n, k, low, high) in enumerate(groups):
+            if g + 1 < len(groups):
+                for copy in loads(g + 1):
+                    copy.start()
+            for copy in loads(g):
+                copy.wait()
             slots = EARLY_SLOTS[: 4 if k == len(sizes) - 1 else 6]
-
-            def unit(base, i):
-                h = base + i
-                columns = columns_of(h + start)
-                first = (side * heads + h + start) * (seq_size + 1)
+            for h in range(low, high):
+                first = (side * heads + h + starts[k]) * (seq_size + 1)
                 codes = [(slot, code_ref[first + slot]) for slot in slots]
                 if HOMES[side] in slots:
                     codes.append((HOMES[side], code_ref[first + seq_size]))
+                local = pl.ds(h * HEAD_DIM, HEAD_DIM)
 
                 def pick(kind, slot):
                     if slot < 4:
-                        return whole[2 * slot + kind], 0, columns
-                    return near[2 * k + slot - 4], kind * rows, columns_of(h)
-
-                masked = masked_scores(queries[:, columns], codes, block_reader(functools.partial(pick, 0)))
+                        return held.at[g % 2, 2 * slot + kind], 0, pl.ds((h - low) * HEAD_DIM, HEAD_DIM)
+                    return near[2 * n + slot - 4], kind * held.shape[2], local
+
+                masked = masked_scores(queries[n][:, local], codes, block_reader(functools.partial(pick, 0)))
                 top = highest(masked)
                 total, mixed = weigh(masked, top, codes, block_reader(functools.partial(pick, 1)))
-                sums[k][h] = mixed
-                stats[k][h, pl.ds(0, 1), :] = top
-                stats[k][h, pl.ds(1, 1), :] = total
-
-            each_unit(size, unit)
+                sums[n][h] = mixed
+                stats[n][h, pl.ds(0, 1), :] = top
+                stats[n][h, pl.ds(1, 1), :] = total
 
 
 def late_kernel(seq_size, panel_size, heads, start, size, near, *refs):
@@ -248,7 +268,7 @@
         if HOMES[side] in slots:
             codes.append((HOMES[side], code_ref[first + seq_size]))
         read = lambda kind: block_reader(lambda slot: (stacked[slot - slots[0]], kind * rows, local))
-        masked = masked_scores(queries[side][:, columns_of(h + start)], codes, read(0))
+        masked = masked_scores(queries[side][:, local], codes, read(0))
         before = stats[side][h, pl.ds(0, 1), :]
         top = jnp.maximum(before, highest(masked))
         kept = jnp.exp2(before - top)
@@ -306,7 +326,9 @@
     partner = [(z * CORES + c, z * CORES + CORES - 1 - c) for z in (1, 2) for c in cores]
     inner = [(z * CORES + c, z * CORES + c) for z in (1, 2) for c in cores]
     outward = [(target, source) for source, target in inward]
-    in_vmem, in_smem, anywhere = (pl.BlockSpec(memory_space=s) for s in (pltpu.VMEM, pltpu.SMEM, pl.ANY))
+    in_vmem, in_smem, in_hbm, anywhere = (
+        pl.BlockSpec(memory_space=space) for space in (pltpu.VMEM, pltpu.SMEM, pltpu.MemorySpace.HBM, pl.ANY)
+    )
 
     front = max(1, heads * FIRST_SHARE[0] // FIRST_SHARE[1])
     sizes = [front, heads - front]
@@ -316,16 +338,18 @@
     middle = [send(x, across) for x in (key_rows, value_rows)]
     packed = pl.pallas_call(
         functools.partial(pack_kernel, starts, sizes),
-        out_shape=[jax.ShapeDtypeStruct((2 * rows, size * HEAD_DIM), key_rows.dtype) for size in sizes],
-        in_specs=[anywhere] * 2,
-        out_specs=[in_vmem] * chunks,
-        scratch_shapes=[pltpu.SemaphoreType.DMA((chunks, 2))],
+        out_shape=[jax.ShapeDtypeStruct((2 * rows, size * HEAD_DIM), key_rows.dtype) for size in sizes]
+        + [jax.ShapeDtypeStruct((rows, size * HEAD_DIM), queries.dtype) for size in sizes],
+        in_specs=[in_hbm] * 3,
+        out_specs=[in_vmem] * (2 * chunks),
+        scratch_shapes=[pltpu.SemaphoreType.DMA((chunks, 3))],
         compiler_params=pltpu.CompilerParams(vmem_limit_bytes=VMEM_GRANT),
         name="pack",
-    )(key_rows, value_rows)
+    )(key_rows, value_rows, queries)
+    packed, own_queries = packed[:chunks], packed[chunks:]
     beside = [send(x, partner) for x in (key_rows, value_rows)]
     ends = [send(x, inward) for x in packed]
-    guest_query = send(queries, inward)
+    guest_queries = [send(x, inward) for x in own_queries]
     middle_beside = [send(x, partner) for x in middle]
 
     is_inner = (chip >= 1) & (chip < last)
@@ -355,19 +379,29 @@
     )
     ends_beside = [send(x, partner) for x in ends]
     near = [x for pair in zip(ends, ends_beside) for x in pair]
-    early = []
-    for side, side_queries in enumerate((queries, guest_query)):
-        early.append(
-            pl.pallas_call(
-                functools.partial(early_kernel, seq_size, heads, starts, sizes, side),
-                out_shape=[jax.ShapeDtypeStruct((size, HEAD_DIM, rows), jnp.float32) for size in sizes]
-                + [jax.ShapeDtypeStruct((size, 8, rows), jnp.float32) for size in sizes],
-                in_specs=[in_smem] * 2 + [in_vmem] * (9 + 2 * (chunks - 1)),
-                out_specs=[in_vmem] * (2 * chunks),
-                compiler_params=params,
-                cost_estimate=cost(heads, 6),
-            )(info, codes, side_queries, key_rows, value_rows, *beside, *middle, *middle_beside, *near[:-2])
-        )
+    sums, stats = {}, {}
+    for side, some in EARLY_CALLS:
+        side_queries = (own_queries, guest_queries)[side]
+        near_end = [x for k in some if k < chunks - 1 for x in near[2 * k : 2 * k + 2]]
+        results = pl.pallas_call(
+            functools.partial(early_kernel, seq_size, heads, starts, sizes, some, side),
+            out_shape=[jax.ShapeDtypeStruct((sizes[k], HEAD_DIM, rows), jnp.float32) for k in some]
+            + [jax.ShapeDtypeStruct((sizes[k], 8, rows), jnp.float32) for k in some],
+            in_specs=[in_smem] * 2 + [in_hbm] * 8 + [in_vmem] * (len(some) + len(near_end)),
+            out_specs=[in_vmem] * (2 * len(some)),
+            scratch_shapes=[
+                pltpu.VMEM((2, 8, rows, UNROLL * HEAD_DIM), key_rows.dtype),
+                pltpu.SemaphoreType.DMA((2, 8)),
+            ],
+            compiler_params=params,
+            cost_estimate=cost(sum(sizes[k] for k in some), 6),
+        )(
+            *(info, codes, key_rows, value_rows, *beside, *middle, *middle_beside),
+            *(side_queries[k] for k in some),
+            *near_end,
+        )
+        for n, k in enumerate(some):
+            sums[side, k], stats[side, k] = results[n], results[len(some) + n]
 
     own_pieces, guest_pieces = [], []
     for k, (start, size) in enumerate(zip(starts, sizes)):
@@ -384,9 +418,9 @@
             compiler_params=params,
             cost_estimate=cost(2 * size, len(stacked)),
         )(
-            *(info, codes, queries, guest_query),
-            *(early[side][k] for side in range(2)),
-            *(early[side][chunks + k] for side in range(2)),
+            *(info, codes, own_queries[k], guest_queries[k]),
+            *(sums[side, k] for side in range(2)),
+            *(stats[side, k] for side in range(2)),
             *stacked,
         )
         both = ("seq", "panel")

time: 134 us -> 154 us (1.15)
  starting transfers between devices: 62.7 us -> 76.3 us
  waiting for transfers between devices: 49.5 us -> 56.3 us
  Pallas kernels: 13.2 us -> 11.4 us
    ppermute x21 -> x22, starting transfers between devices: 62.7 us -> 76.3 us  [send(): return lax.ppermute(value, axes, pairs)]
    ppermute x21 -> x22, waiting for transfers between devices: 49.5 us -> 56.3 us  [send(): return lax.ppermute(value, axes, pairs)]
    unnamed x16 -> x18, local copies, waits for them, and re-layouts: 4.05 us -> 5.3 us
    pallas_call x2 -> x3, Pallas kernels: 4.98 us -> 4.45 us  [relayed(): pl.pallas_call(functools.partial(early_kernel, seq_size, heads, starts, s...]
  transfers between devices with their start and end apart: 21 -> 22, of which waited for: 7 -> 7; matrix products, arithmetic and copies ran while one was open for 3% -> 2% of each run, Pallas kernels for 7% -> 7%
where the time goes in v5:
time: 154 us; the launch traced here: 153 us
  starting transfers between devices  76.3 us (50%)
  waiting for transfers between devices  56.3 us (37%)
  Pallas kernels  11.4 us (7%)
  local copies, waits for them, and re-layouts  7.08 us (5%)
  other arithmetic  1.62 us (1%)
    ppermute x22, starting transfers between devices, send(): return lax.ppermute(value, axes, pairs)  76.3 us
    ppermute x22, waiting for transfers between devices, send(): return lax.ppermute(value, axes, pairs)  56.3 us
    unnamed x18, local copies, waits for them, and re-layouts  5.3 us
    pallas_call x3, Pallas kernels, relayed(): pl.pallas_call(functools.partial(early_kernel, seq_size, heads, starts, s...  4.45 us
  transfers between devices with their start and end apart: 22, of which 7 were waited for; matrix products, arithmetic and copies ran while one was open for 2% of the time, Pallas kernels for 7%

profile of v5, /device:TPU:0, one launch (start us, length us, event | category | flops | bytes accessed | tf_op | source)
XLA Modules:
  0.0 153.2 jit_solution(13345288018018289301)
XLA Ops:
  0.0 0.7 collective-permute-start.1
  0.7 0.7 collective-permute-start.3
  1.4 1.5 %collective-permute-start.2 = (bf16[256,1536]{1,0:T(8,128)(2,1)}, bf16[256,1536]{1,0:T(8,128)(2,1)}, u32[]{:S(2)}, u32[]{:S(2)}) collective-permute-start(bf16[256,1536]{1,0:T(8,128)(2,1)} %refs_3_.5), channel_id=1, source_target_pairs={{4,6},{6,4},{8,10},{10,8},{5,7},{7,5},{9,11},{11,9},{20,22},{22,20... | collective-permute-start | bytes 2359304 | tf_op jit(solution)/shard_map/ppermute | solution.py:120
  3.0 1.1 copy-done
  4.1 1.1 copy-done.2
  5.2 1.1 copy-done.7
  6.4 1.4 pack.1
  7.8 0.8 copy-done.4
  8.6 10.6 %collective-permute-start.7 = (bf16[512,1024]{1,0:T(8,128)(2,1)}, bf16[512,1024]{1,0:T(8,128)(2,1)}, u32[]{:S(2)}, u32[]{:S(2)}) collective-permute-start(bf16[512,1024]{1,0:T(8,128)(2,1)} %get-tuple-element.27), channel_id=1, source_target_pairs={{0,4},{2,6},{12,8},{14,10},{1,5},{3,7},{13,9},{15,11},{16,20},{18,... | collective-permute-start | bytes 3145736 | tf_op jit(solution)/shard_map/ppermute | solution.py:120
  19.3 2.1 %collective-permute-start.15 = (bf16[512,512]{1,0:T(8,128)(2,1)}, bf16[512,512]{1,0:T(8,128)(2,1)}, u32[]{:S(2)}, u32[]{:S(2)}) collective-permute-start(bf16[512,512]{1,0:T(8,128)(2,1)} %get-tuple-element.40), channel_id=1, source_target_pairs={{0,4},{2,6},{12,8},{14,10},{1,5},{3,7},{13,9},{15,11},{16,20},{18,... | collective-permute-start | bytes 1572872 | tf_op jit(solution)/shard_map/ppermute | solution.py:120
  21.4 0.1 copy.25
  21.6 0.9 constant_dynamic-slice_fusion
  22.5 0.1 fusion.3
  22.8 0.1 copy.22
  22.9 0.1 fusion.1
  23.2 18.9 %collective-permute-done.7.refs_12_.refs_11_ = bf16[512,1024]{1,0:T(8,128)(2,1)} collective-permute-done((bf16[512,1024]{1,0:T(8,128)(2,1)}, bf16[512,1024]{1,0:T(8,128)(2,1)}, u32[]{:S(2)}, u32[]{:S(2)}) %collective-permute-start.7) | collective-permute-done | bytes 1048608 | tf_op jit(solution)/shard_map/ppermute | solution.py:120
  42.1 1.7 %collective-permute-start.9 = (bf16[512,1024]{1,0:T(8,128)(2,1)}, bf16[512,1024]{1,0:T(8,128)(2,1)}, u32[]{:S(2)}, u32[]{:S(2)}) collective-permute-start(bf16[512,1024]{1,0:T(8,128)(2,1)} %collective-permute-done.7.refs_12_.refs_11_), channel_id=1, source_target_pairs={{4,8},{6,10},{8,4},{10,6},{5,9},{7,11},{9,5},{11,7},{20,24},{22,26... | collective-permute-start | bytes 3145736 | tf_op jit(solution)/shard_map/ppermute | solution.py:120
  43.9 8.8 %collective-permute-done.15.refs_8_ = bf16[512,512]{1,0:T(8,128)(2,1)} collective-permute-done((bf16[512,512]{1,0:T(8,128)(2,1)}, bf16[512,512]{1,0:T(8,128)(2,1)}, u32[]{:S(2)}, u32[]{:S(2)}) %collective-permute-start.15) | collective-permute-done | bytes 524320 | tf_op jit(solution)/shard_map/ppermute | solution.py:120
  52.7 1.6 %collective-permute-start.4 = (bf16[256,1536]{1,0:T(8,128)(2,1)S(1)}, bf16[256,1536]{1,0:T(8,128)(2,1)}, u32[]{:S(2)}, u32[]{:S(2)}) collective-permute-start(bf16[256,1536]{1,0:T(8,128)(2,1)S(1)} %copy-done.3), channel_id=1, source_target_pairs={{4,8},{6,10},{8,4},{10,6},{5,9},{7,11},{9,5},{11,7},{20,24},{22,26... | collective-permute-start | bytes 2359304 | tf_op jit(solution)/shard_map/ppermute | solution.py:120
  54.3 0.7 multiply_reduce_fusion.5
  55.1 1.5 collective-permute-start.17
  56.6 1.6 %collective-permute-start.8 = (bf16[512,1024]{1,0:T(8,128)(2,1)}, bf16[512,1024]{1,0:T(8,128)(2,1)}, u32[]{:S(2)}, u32[]{:S(2)}) collective-permute-start(bf16[512,1024]{1,0:T(8,128)(2,1)} %collective-permute-done.7.refs_12_.refs_11_), channel_id=1, source_target_pairs={{4,6},{6,4},{8,10},{10,8},{5,7},{7,5},{9,11},{11,9},{20,22},{22,20... | collective-permute-start | bytes 3145736 | tf_op jit(solution)/shard_map/ppermute | solution.py:120
  58.3 1.6 %collective-permute-start.5 = (bf16[256,1536]{1,0:T(8,128)(2,1)S(1)}, bf16[256,1536]{1,0:T(8,128)(2,1)}, u32[]{:S(2)}, u32[]{:S(2)}) collective-permute-start(bf16[256,1536]{1,0:T(8,128)(2,1)S(1)} %collective-permute-done.3.refs_6_), channel_id=1, source_target_pairs={{4,6},{6,4},{8,10},{10,8},{5,7},{7,5},{9,11},{11,9},{20,22},{22,20... | collective-permute-start | bytes 2359304 | tf_op jit(solution)/shard_map/ppermute | solution.py:120
  59.9 1.6 %collective-permute-start.6 = (bf16[256,1536]{1,0:T(8,128)(2,1)}, bf16[256,1536]{1,0:T(8,128)(2,1)}, u32[]{:S(2)}, u32[]{:S(2)}) collective-permute-start(bf16[256,1536]{1,0:T(8,128)(2,1)} %collective-permute-done.4.refs_7_), channel_id=1, source_target_pairs={{4,6},{6,4},{8,10},{10,8},{5,7},{7,5},{9,11},{11,9},{20,22},{22,20... | collective-permute-start | bytes 2359304 | tf_op jit(solution)/shard_map/ppermute | solution.py:120
  61.5 1.6 %collective-permute-start.10 = (bf16[512,1024]{1,0:T(8,128)(2,1)}, bf16[512,1024]{1,0:T(8,128)(2,1)}, u32[]{:S(2)}, u32[]{:S(2)}) collective-permute-start(bf16[512,1024]{1,0:T(8,128)(2,1)} %collective-permute-done.9.refs_8_), channel_id=1, source_target_pairs={{4,6},{6,4},{8,10},{10,8},{5,7},{7,5},{9,11},{11,9},{20,22},{22,20... | collective-permute-start | bytes 3145736 | tf_op jit(solution)/shard_map/ppermute | solution.py:120
  63.3 38.2 %collective-permute-start = (bf16[256,1024]{1,0:T(8,128)(2,1)}, bf16[256,1024]{1,0:T(8,128)(2,1)}, u32[]{:S(2)}, u32[]{:S(2)}) collective-permute-start(bf16[256,1024]{1,0:T(8,128)(2,1)} %copy-done.4), channel_id=1, source_target_pairs={{0,4},{2,6},{12,8},{14,10},{1,5},{3,7},{13,9},{15,11},{16,20},{18,... | collective-permute-start | bytes 1572872 | tf_op jit(solution)/shard_map/ppermute | solution.py:120
  101.8 0.7 collective-permute-start.16
  102.5 0.7 collective-permute-start.18
  103.3 3.4 %collective-permute-start.14 = (bf16[256,512]{1,0:T(8,128)(2,1)S(1)}, bf16[256,512]{1,0:T(8,128)(2,1)S(1)}, u32[]{:S(2)}, u32[]{:S(2)}) collective-permute-start(bf16[256,512]{1,0:T(8,128)(2,1)S(1)} %get-tuple-element.26.refs_11_.refs_2_), channel_id=1, source_target_pairs={{0,4},{2,6},{12,8},{14,10},{1,5},{3,7},{13,9},{15,11},{16,20},{18,... | collective-permute-start | bytes 786440 | tf_op jit(solution)/shard_map/ppermute | solution.py:120
  106.7 1.0 copy-done.5
  107.7 1.7 %shard_map.73 = (f32[8,128,256]{2,1,0:T(8,128)S(1)}, f32[4,128,256]{2,1,0:T(8,128)S(1)}, f32[8,8,256]{2,1,0:T(8,128)S(1)}, f32[4,8,256]{2,1,0:T(8,128)S(1)}) custom-call(s32[2]{0:T(128)S(1)} %pad_add_fusion.3.refs_0_.info_ref, s32[216]{0:T(256)S(1)} %reshape.60.refs_1_, bf16[256,1536]{1,0:T(8,128)(2,1)S(1)} %copy-done.1, bf16[256,1536]{1,0:T(8,128)(2,1)S(1)} %copy-done.3, ...), custom_call_target="tpu_custom_call" | custom-call | flops 1207959552 | bytes 4718592 | tf_op jit(solution)/shard_map/pallas_call | solution.py:386
  109.5 3.5 %collective-permute-done.refs_10_.refs_3_ = bf16[256,1024]{1,0:T(8,128)(2,1)} collective-permute-done((bf16[256,1024]{1,0:T(8,128)(2,1)}, bf16[256,1024]{1,0:T(8,128)(2,1)}, u32[]{:S(2)}, u32[]{:S(2)}) %collective-permute-start) | collective-permute-done | bytes 524320 | tf_op jit(solution)/shard_map/ppermute | solution.py:120
  113.0 1.9 %shard_map.74 = (f32[8,128,256]{2,1,0:T(8,128)S(1)}, f32[8,8,256]{2,1,0:T(8,128)S(1)}) custom-call(s32[2]{0:T(128)S(1)} %pad_add_fusion.3.refs_0_.info_ref, s32[216]{0:T(256)S(1)} %reshape.60.refs_1_, bf16[256,1536]{1,0:T(8,128)(2,1)S(1)} %copy-done.1, bf16[256,1536]{1,0:T(8,128)(2,1)S(1)} %copy-done.3, ...), custom_call_target="tpu_custom_call" | custom-call | flops 805306368 | bytes 3145728 | tf_op jit(solution)/shard_map/pallas_call | solution.py:386
  114.9 1.7 %shard_map.75 = (bf16[128,1024]{1,0:T(8,128)(2,1)S(1)}, bf16[128,1024]{1,0:T(8,128)(2,1)S(1)}, bf16[128,1024]{1,0:T(8,128)(2,1)S(1)}, bf16[128,1024]{1,0:T(8,128)(2,1)S(1)}) custom-call(s32[2]{0:T(128)S(1)} %pad_add_fusion.3.refs_0_.info_ref, s32[216]{0:T(256)S(1)} %reshape.60.refs_1_, bf16[256,1024]{1,0:T(8,128)(2,1)S(1)} %copy-done.6, ...), custom_call_target="tpu_custom_call" | custom-call | flops 536870912 | bytes 2097152 | tf_op jit(solution)/shard_map/pallas_call | solution.py:412
  116.6 0.7 collective-permute-start.11
  117.3 1.3 collective-permute-start.12
  118.6 1.3 collective-permute-start.13
  119.9 0.9 shard_map.77
  120.8 1.2 shard_map.78
  122.1 0.7 collective-permute-start.19
  122.7 1.3 collective-permute-start.20
  124.0 1.3 collective-permute-start.21
  125.3 14.0 %collective-permute-done.12.refs_2_ = bf16[128,1024]{1,0:T(8,128)(2,1)S(1)} collective-permute-done((bf16[128,1024]{1,0:T(8,128)(2,1)S(1)}, bf16[128,1024]{1,0:T(8,128)(2,1)S(1)}, u32[]{:S(2)}, u32[]{:S(2)}) %collective-permute-start.12) | collective-permute-done | bytes 262176 | tf_op jit(solution)/shard_map/ppermute | solution.py:120
  139.4 4.6 %collective-permute-done.13.refs_3_ = bf16[128,1024]{1,0:T(8,128)(2,1)S(1)} collective-permute-done((bf16[128,1024]{1,0:T(8,128)(2,1)S(1)}, bf16[128,1024]{1,0:T(8,128)(2,1)S(1)}, u32[]{:S(2)}, u32[]{:S(2)}) %collective-permute-start.13) | collective-permute-done | bytes 262176 | tf_op jit(solution)/shard_map/ppermute | solution.py:120
  143.9 1.4 shard_map.76.refs_0_
  145.3 4.0 %collective-permute-done.20.refs_3_ = bf16[128,512]{1,0:T(8,128)(2,1)S(1)} collective-permute-done((bf16[128,512]{1,0:T(8,128)(2,1)S(1)}, bf16[128,512]{1,0:T(8,128)(2,1)S(1)}, u32[]{:S(2)}, u32[]{:S(2)}) %collective-permute-start.20) | collective-permute-done | bytes 131104 | tf_op jit(solution)/shard_map/ppermute | solution.py:120
  149.3 2.5 %collective-permute-done.21.refs_4_ = bf16[128,512]{1,0:T(8,128)(2,1)S(1)} collective-permute-done((bf16[128,512]{1,0:T(8,128)(2,1)S(1)}, bf16[128,512]{1,0:T(8,128)(2,1)S(1)}, u32[]{:S(2)}, u32[]{:S(2)}) %collective-permute-start.21) | collective-permute-done | bytes 131104 | tf_op jit(solution)/shard_map/ppermute | solution.py:120
  151.8 1.3 shard_map.79
  (53 shorter events, 1.3 us)
Async XLA Ops:
  0.0 55.1 %collective-permute-start.1 = (bf16[256,1536]{1,0:T(8,128)(2,1)}, bf16[256,1536]{1,0:T(8,128)(2,1)S(1)}, u32[]{:S(2)}, u32[]{:S(2)}) collective-permute-start(bf16[256,1536]{1,0:T(8,128)(2,1)} %refs_2_.5), channel_id=1, source_target_pairs={{4,6},{6,4},{8,10},{10,8},{5,7},{7,5},{9,11},{11,9},{20,22},{22,20... | collective-permute-start | bytes 2359304 | tf_op jit(solution)/shard_map/ppermute | solution.py:120
  0.7 57.6 %collective-permute-start.3 = (bf16[256,1536]{1,0:T(8,128)(2,1)}, bf16[256,1536]{1,0:T(8,128)(2,1)S(1)}, u32[]{:S(2)}, u32[]{:S(2)}) collective-permute-start(bf16[256,1536]{1,0:T(8,128)(2,1)} %refs_2_.5), channel_id=1, source_target_pairs={{4,8},{6,10},{8,4},{10,6},{5,9},{7,11},{9,5},{11,7},{20,24},{22,26... | collective-permute-start | bytes 2359304 | tf_op jit(solution)/shard_map/ppermute | solution.py:120
  1.4 55.2 %collective-permute-start.2 = (bf16[256,1536]{1,0:T(8,128)(2,1)}, bf16[256,1536]{1,0:T(8,128)(2,1)}, u32[]{:S(2)}, u32[]{:S(2)}) collective-permute-start(bf16[256,1536]{1,0:T(8,128)(2,1)} %refs_3_.5), channel_id=1, source_target_pairs={{4,6},{6,4},{8,10},{10,8},{5,7},{7,5},{9,11},{11,9},{20,22},{22,20... | collective-permute-start | bytes 2359304 | tf_op jit(solution)/shard_map/ppermute | solution.py:120
  3.0 1.1 copy-start
  4.1 1.1 copy-start.2
  5.2 1.1 copy-start.7
  6.4 15.0 %copy-start.8 = (s32[12,16,8]{1,2,0:T(8,128)S(1)}, s32[12,16,8]{1,2,0:T(8,128)}, u32[]{:S(2)}) copy-start(s32[12,16,8]{1,2,0:T(8,128)} %param.10) | copy-start | bytes 18436
  6.4 46.3 %copy-start.3 = (bf16[256,1536]{1,0:T(8,128)(2,1)S(1)}, bf16[256,1536]{1,0:T(8,128)(2,1)}, u32[]{:S(2)}) copy-start(bf16[256,1536]{1,0:T(8,128)(2,1)} %refs_3_.5) | copy-start | bytes 2359300
  7.8 0.9 copy-start.4
  8.6 98.1 %copy-start.1 = (bf16[256,1536]{1,0:T(8,128)(2,1)S(1)}, bf16[256,1536]{1,0:T(8,128)(2,1)}, u32[]{:S(2)}) copy-start(bf16[256,1536]{1,0:T(8,128)(2,1)} %refs_2_.5) | copy-start | bytes 2359300
  8.6 33.5 %collective-permute-start.7 = (bf16[512,1024]{1,0:T(8,128)(2,1)}, bf16[512,1024]{1,0:T(8,128)(2,1)}, u32[]{:S(2)}, u32[]{:S(2)}) collective-permute-start(bf16[512,1024]{1,0:T(8,128)(2,1)} %get-tuple-element.27), channel_id=1, source_target_pairs={{0,4},{2,6},{12,8},{14,10},{1,5},{3,7},{13,9},{15,11},{16,20},{18,... | collective-permute-start | bytes 3145736 | tf_op jit(solution)/shard_map/ppermute | solution.py:120
  19.3 33.4 %collective-permute-start.15 = (bf16[512,512]{1,0:T(8,128)(2,1)}, bf16[512,512]{1,0:T(8,128)(2,1)}, u32[]{:S(2)}, u32[]{:S(2)}) collective-permute-start(bf16[512,512]{1,0:T(8,128)(2,1)} %get-tuple-element.40), channel_id=1, source_target_pairs={{0,4},{2,6},{12,8},{14,10},{1,5},{3,7},{13,9},{15,11},{16,20},{18,... | collective-permute-start | bytes 1572872 | tf_op jit(solution)/shard_map/ppermute | solution.py:120
  42.1 19.3 %collective-permute-start.9 = (bf16[512,1024]{1,0:T(8,128)(2,1)}, bf16[512,1024]{1,0:T(8,128)(2,1)}, u32[]{:S(2)}, u32[]{:S(2)}) collective-permute-start(bf16[512,1024]{1,0:T(8,128)(2,1)} %collective-permute-done.7.refs_12_.refs_11_), channel_id=1, source_target_pairs={{4,8},{6,10},{8,4},{10,6},{5,9},{7,11},{9,5},{11,7},{20,24},{22,26... | collective-permute-start | bytes 3145736 | tf_op jit(solution)/shard_map/ppermute | solution.py:120
  52.7 7.2 %collective-permute-start.4 = (bf16[256,1536]{1,0:T(8,128)(2,1)S(1)}, bf16[256,1536]{1,0:T(8,128)(2,1)}, u32[]{:S(2)}, u32[]{:S(2)}) collective-permute-start(bf16[256,1536]{1,0:T(8,128)(2,1)S(1)} %copy-done.3), channel_id=1, source_target_pairs={{4,8},{6,10},{8,4},{10,6},{5,9},{7,11},{9,5},{11,7},{20,24},{22,26... | collective-permute-start | bytes 2359304 | tf_op jit(solution)/shard_map/ppermute | solution.py:120
  55.1 8.2 %collective-permute-start.17 = (bf16[512,512]{1,0:T(8,128)(2,1)}, bf16[512,512]{1,0:T(8,128)(2,1)}, u32[]{:S(2)}, u32[]{:S(2)}) collective-permute-start(bf16[512,512]{1,0:T(8,128)(2,1)} %collective-permute-done.15.refs_8_), channel_id=1, source_target_pairs={{4,8},{6,10},{8,4},{10,6},{5,9},{7,11},{9,5},{11,7},{20,24},{22,26... | collective-permute-start | bytes 1572872 | tf_op jit(solution)/shard_map/ppermute | solution.py:120
  56.6 46.7 %collective-permute-start.8 = (bf16[512,1024]{1,0:T(8,128)(2,1)}, bf16[512,1024]{1,0:T(8,128)(2,1)}, u32[]{:S(2)}, u32[]{:S(2)}) collective-permute-start(bf16[512,1024]{1,0:T(8,128)(2,1)} %collective-permute-done.7.refs_12_.refs_11_), channel_id=1, source_target_pairs={{4,6},{6,4},{8,10},{10,8},{5,7},{7,5},{9,11},{11,9},{20,22},{22,20... | collective-permute-start | bytes 3145736 | tf_op jit(solution)/shard_map/ppermute | solution.py:120
  58.3 43.5 %collective-permute-start.5 = (bf16[256,1536]{1,0:T(8,128)(2,1)S(1)}, bf16[256,1536]{1,0:T(8,128)(2,1)}, u32[]{:S(2)}, u32[]{:S(2)}) collective-permute-start(bf16[256,1536]{1,0:T(8,128)(2,1)S(1)} %collective-permute-done.3.refs_6_), channel_id=1, source_target_pairs={{4,6},{6,4},{8,10},{10,8},{5,7},{7,5},{9,11},{11,9},{20,22},{22,20... | collective-permute-start | bytes 2359304 | tf_op jit(solution)/shard_map/ppermute | solution.py:120
  59.9 42.6 %collective-permute-start.6 = (bf16[256,1536]{1,0:T(8,128)(2,1)}, bf16[256,1536]{1,0:T(8,128)(2,1)}, u32[]{:S(2)}, u32[]{:S(2)}) collective-permute-start(bf16[256,1536]{1,0:T(8,128)(2,1)} %collective-permute-done.4.refs_7_), channel_id=1, source_target_pairs={{4,6},{6,4},{8,10},{10,8},{5,7},{7,5},{9,11},{11,9},{20,22},{22,20... | collective-permute-start | bytes 2359304 | tf_op jit(solution)/shard_map/ppermute | solution.py:120
  61.5 53.4 %collective-permute-start.10 = (bf16[512,1024]{1,0:T(8,128)(2,1)}, bf16[512,1024]{1,0:T(8,128)(2,1)}, u32[]{:S(2)}, u32[]{:S(2)}) collective-permute-start(bf16[512,1024]{1,0:T(8,128)(2,1)} %collective-permute-done.9.refs_8_), channel_id=1, source_target_pairs={{4,6},{6,4},{8,10},{10,8},{5,7},{7,5},{9,11},{11,9},{20,22},{22,20... | collective-permute-start | bytes 3145736 | tf_op jit(solution)/shard_map/ppermute | solution.py:120
  63.3 49.7 %collective-permute-start = (bf16[256,1024]{1,0:T(8,128)(2,1)}, bf16[256,1024]{1,0:T(8,128)(2,1)}, u32[]{:S(2)}, u32[]{:S(2)}) collective-permute-start(bf16[256,1024]{1,0:T(8,128)(2,1)} %copy-done.4), channel_id=1, source_target_pairs={{0,4},{2,6},{12,8},{14,10},{1,5},{3,7},{13,9},{15,11},{16,20},{18,... | collective-permute-start | bytes 1572872 | tf_op jit(solution)/shard_map/ppermute | solution.py:120
  101.8 19.0 %collective-permute-start.16 = (bf16[512,512]{1,0:T(8,128)(2,1)}, bf16[512,512]{1,0:T(8,128)(2,1)S(1)}, u32[]{:S(2)}, u32[]{:S(2)}) collective-permute-start(bf16[512,512]{1,0:T(8,128)(2,1)} %collective-permute-done.15.refs_8_), channel_id=1, source_target_pairs={{4,6},{6,4},{8,10},{10,8},{5,7},{7,5},{9,11},{11,9},{20,22},{22,20... | collective-permute-start | bytes 1572872 | tf_op jit(solution)/shard_map/ppermute | solution.py:120
  102.5 18.3 %collective-permute-start.18 = (bf16[512,512]{1,0:T(8,128)(2,1)}, bf16[512,512]{1,0:T(8,128)(2,1)S(1)}, u32[]{:S(2)}, u32[]{:S(2)}) collective-permute-start(bf16[512,512]{1,0:T(8,128)(2,1)} %collective-permute-done.17.refs_10_), channel_id=1, source_target_pairs={{4,6},{6,4},{8,10},{10,8},{5,7},{7,5},{9,11},{11,9},{20,22},{22,20... | collective-permute-start | bytes 1572872 | tf_op jit(solution)/shard_map/ppermute | solution.py:120
  103.3 15.3 %collective-permute-start.14 = (bf16[256,512]{1,0:T(8,128)(2,1)S(1)}, bf16[256,512]{1,0:T(8,128)(2,1)S(1)}, u32[]{:S(2)}, u32[]{:S(2)}) collective-permute-start(bf16[256,512]{1,0:T(8,128)(2,1)S(1)} %get-tuple-element.26.refs_11_.refs_2_), channel_id=1, source_target_pairs={{0,4},{2,6},{12,8},{14,10},{1,5},{3,7},{13,9},{15,11},{16,20},{18,... | collective-permute-start | bytes 786440 | tf_op jit(solution)/shard_map/ppermute | solution.py:120
  106.7 1.0 copy-start.5
  109.5 5.4 %copy-start.6 = (bf16[256,1024]{1,0:T(8,128)(2,1)S(1)}, bf16[256,1024]{1,0:T(8,128)(2,1)}, u32[]{:S(2)}) copy-start(bf16[256,1024]{1,0:T(8,128)(2,1)} %copy-done.4) | copy-start | bytes 1572868
  116.6 7.4 %collective-permute-start.11 = (bf16[128,1024]{1,0:T(8,128)(2,1)S(1)}, bf16[128,1024]{1,0:T(8,128)(2,1)S(1)}, u32[]{:S(2)}, u32[]{:S(2)}) collective-permute-start(bf16[128,1024]{1,0:T(8,128)(2,1)S(1)} %get-tuple-element.33), channel_id=1, source_target_pairs={{4,5},{5,4},{6,7},{7,6},{8,9},{9,8},{10,11},{11,10},{20,21},{21,20... | collective-permute-start | bytes 786440 | tf_op jit(solution)/shard_map/ppermute | solution.py:120
  117.3 22.1 %collective-permute-start.12 = (bf16[128,1024]{1,0:T(8,128)(2,1)S(1)}, bf16[128,1024]{1,0:T(8,128)(2,1)S(1)}, u32[]{:S(2)}, u32[]{:S(2)}) collective-permute-start(bf16[128,1024]{1,0:T(8,128)(2,1)S(1)} %get-tuple-element.34), channel_id=1, source_target_pairs={{4,0},{5,1},{6,2},{7,3},{8,12},{9,13},{10,14},{11,15},{20,16},{21,... | collective-permute-start | bytes 786440 | tf_op jit(solution)/shard_map/ppermute | solution.py:120
  118.6 25.3 %collective-permute-start.13 = (bf16[128,1024]{1,0:T(8,128)(2,1)S(1)}, bf16[128,1024]{1,0:T(8,128)(2,1)S(1)}, u32[]{:S(2)}, u32[]{:S(2)}) collective-permute-start(bf16[128,1024]{1,0:T(8,128)(2,1)S(1)} %get-tuple-element.35), channel_id=1, source_target_pairs={{4,1},{5,0},{6,3},{7,2},{8,13},{9,12},{10,15},{11,14},{20,17},{21,... | collective-permute-start | bytes 786440 | tf_op jit(solution)/shard_map/ppermute | solution.py:120
  122.1 23.3 %collective-permute-start.19 = (bf16[128,512]{1,0:T(8,128)(2,1)S(1)}, bf16[128,512]{1,0:T(8,128)(2,1)S(1)}, u32[]{:S(2)}, u32[]{:S(2)}) collective-permute-start(bf16[128,512]{1,0:T(8,128)(2,1)S(1)} %get-tuple-element.42), channel_id=1, source_target_pairs={{4,5},{5,4},{6,7},{7,6},{8,9},{9,8},{10,11},{11,10},{20,21},{21,20... | collective-permute-start | bytes 393224 | tf_op jit(solution)/shard_map/ppermute | solution.py:120
  122.7 26.6 %collective-permute-start.20 = (bf16[128,512]{1,0:T(8,128)(2,1)S(1)}, bf16[128,512]{1,0:T(8,128)(2,1)S(1)}, u32[]{:S(2)}, u32[]{:S(2)}) collective-permute-start(bf16[128,512]{1,0:T(8,128)(2,1)S(1)} %get-tuple-element.43), channel_id=1, source_target_pairs={{4,0},{5,1},{6,2},{7,3},{8,12},{9,13},{10,14},{11,15},{20,16},{21,... | collective-permute-start | bytes 393224 | tf_op jit(solution)/shard_map/ppermute | solution.py:120
  124.0 27.8 %collective-permute-start.21 = (bf16[128,512]{1,0:T(8,128)(2,1)S(1)}, bf16[128,512]{1,0:T(8,128)(2,1)S(1)}, u32[]{:S(2)}, u32[]{:S(2)}) collective-permute-start(bf16[128,512]{1,0:T(8,128)(2,1)S(1)} %get-tuple-element.44), channel_id=1, source_target_pairs={{4,1},{5,0},{6,3},{7,2},{8,13},{9,12},{10,15},{11,14},{20,17},{21,... | collective-permute-start | bytes 393224 | tf_op jit(solution)/shard_map/ppermute | solution.py:120

commit v6 on v3

--- a/solution.py
+++ b/solution.py
@@ -14,7 +14,17 @@
 DEAD = -1e30
 CORES = 2
 FIRST_SHARE = 7, 12
-VMEM_GRANT = 20 << 20
+UNROLL = 5
+VMEM_GRANT = 14 << 20
+HOMES = 0, 4
+STAGES = (
+    ("early_0", ((0, 0, (0, 1), False), (0, 1, (0, 1), False))),
+    ("early_1", ((0, 0, (2, 3, 4, 5), True), (0, 1, (2, 3), True))),
+    ("early_2", ((1, 0, (0, 1, 2, 3, 4, 5), False),)),
+    ("early_3", ((1, 1, (0, 1, 2, 3, 4, 5), False), (0, 1, (4, 5), True))),
+    ("late_0", ((0, 0, (6, 7), True), (1, 0, (6, 7), True))),
+    ("late_1", ((0, 1, (6, 7), True), (1, 1, (6, 7), True))),
+)
 
 
 def tables(block_lists, block_counts, owner, seq_size):
@@ -116,17 +126,16 @@
     return lax.ppermute(value, axes, pairs)
 
 
-def pack_kernel(starts, sizes, key_ref, value_ref, *refs):
-    outs, sems = refs[:-1], refs[-1]
-    rows = key_ref.shape[0]
-    copies = []
-    for k, (start, size) in enumerate(zip(starts, sizes)):
-        columns = pl.ds(start * HEAD_DIM, size * HEAD_DIM)
-        for kind, ref in enumerate((key_ref, value_ref)):
-            copies.append(
-                pltpu.make_async_copy(ref.at[:, columns], outs[k].at[pl.ds(kind * rows, rows), :], sems.at[k, kind])
-            )
-            copies[-1].start()
+def pack_kernel(starts, sizes, chunk, *refs):
+    sources, out, sems = refs[:-2], refs[-2], refs[-1]
+    rows = sources[0].shape[0]
+    columns = pl.ds(starts[chunk] * HEAD_DIM, sizes[chunk] * HEAD_DIM)
+    copies = [
+        pltpu.make_async_copy(ref.at[:, columns], out.at[pl.ds(kind * rows, rows), :], sems.at[kind])
+        for kind, ref in enumerate(sources)
+    ]
+    for copy in copies:
+        copy.start()
     for copy in copies:
         copy.wait()
 
@@ -166,16 +175,18 @@
     return jnp.max(functools.reduce(jnp.maximum, masked), axis=0, keepdims=True)
 
 
-def each_unit(size, unit):
-    @pl.loop(0, size // 2)
-    def _(pair):
-        for h in range(2):
-            for side in range(2):
-                unit(pair * 2 + h, side)
-
-    for h in range(size - size % 2, size):
-        for side in range(2):
-            unit(h, side)
+def each_unit(count, unit):
+    groups = -(-count // UNROLL)
+    size = -(-count // groups)
+    whole = count // size
+
+    @pl.loop(0, whole)
+    def _(group):
+        for i in range(size):
+            unit(group * size, i)
+
+    for i in range(count - whole * size):
+        unit(whole * size, i)
 
 
 def columns_of(head):
@@ -190,70 +201,59 @@
     return block
 
 
-def early_kernel(seq_size, heads, starts, sizes, *refs):
+def stage_kernel(seq_size, panel_size, heads, starts, sizes, jobs, inputs, final, *refs):
     info_ref, code_ref = refs[:2]
-    queries = refs[2:4]
-    whole = refs[4:12]
-    sums, stats = refs[12 : 12 + len(sizes)], refs[12 + len(sizes) :]
+    have = dict(zip(inputs, refs[2:]))
+    results = refs[2 + len(inputs) :]
+    panel = info_ref[1]
+
+    def job(n, side, k, slots, carry):
+        queries = have["query", side, k]
+        rows = queries.shape[0]
+        piece = rows // panel_size
+
+        def unit(base, i):
+            h = base + i
+            local = columns_of(h)
+            first = (side * heads + h + starts[k]) * (seq_size + 1)
+            codes = [(slot, code_ref[first + slot]) for slot in slots]
+            if HOMES[side] in slots:
+                codes.append((HOMES[side], code_ref[first + seq_size]))
+
+            def pick(kind, slot):
+                if ("chunk", slot, k) in have:
+                    return have["chunk", slot, k], kind * rows, local
+                return have["whole", slot, kind], 0, columns_of(h + starts[k])
+
+            masked = masked_scores(queries[:, local], codes, block_reader(functools.partial(pick, 0)))
+            top = highest(masked)
+            if carry:
+                stat = have["stat", side, k]
+                before = stat[h, pl.ds(0, 1), :]
+                top = jnp.maximum(before, top)
+                kept = jnp.exp2(before - top)
+            total, mixed = weigh(masked, top, codes, block_reader(functools.partial(pick, 1)))
+            if carry:
+                total = total + kept * stat[h, pl.ds(1, 1), :]
+                mixed = mixed + kept * have["sum", side, k][h]
+            if final:
+                spare = results[-1]
+                spare[i] = (mixed / total).astype(spare.dtype).T
+                for shift in range(panel_size):
+                    first_row = pl.multiple_of(lax.rem(panel + shift, panel_size) * piece, piece)
+                    results[n * panel_size + shift][:, local] = spare[i, pl.ds(first_row, piece), :]
+            else:
+                sums, stats = results[2 * n : 2 * n + 2]
+                sums[h] = mixed
+                stats[h, pl.ds(0, 1), :] = top
+                stats[h, pl.ds(1, 1), :] = total
+
+        each_unit(sizes[k], unit)
 
     @pl.when(info_ref[0] == 1)
     def _():
-        for k, (start, size) in enumerate(zip(starts, sizes)):
-
-            def unit(h, side):
-                columns = columns_of(h + start)
-                first = (side * heads + h + start) * (seq_size + 1)
-                codes = [(slot, code_ref[first + slot]) for slot in range(4)]
-                if side == 0:
-                    codes.append((0, code_ref[first + seq_size]))
-                masked = masked_scores(
-                    queries[side][:, columns], codes, block_reader(lambda slot: (whole[2 * slot], 0, columns))
-                )
-                top = highest(masked)
-                total, mixed = weigh(
-                    masked, top, codes, block_reader(lambda slot: (whole[2 * slot + 1], 0, columns))
-                )
-                sums[k][h * 2 + side] = mixed
-                stats[k][h * 2 + side, pl.ds(0, 1), :] = top
-                stats[k][h * 2 + side, pl.ds(1, 1), :] = total
-
-            each_unit(size, unit)
-
-
-def late_kernel(seq_size, panel_size, heads, start, size, *refs):
-    info_ref, code_ref = refs[:2]
-    queries = refs[2:4]
-    sums, stats = refs[4:6]
-    stacked = refs[6:10]
-    outs = refs[10 : 10 + panel_size], refs[10 + panel_size : 10 + 2 * panel_size]
-    held = refs[-1]
-    panel = info_ref[1]
-    rows = queries[0].shape[0]
-    piece = rows // panel_size
-
-    def unit(h, side):
-        local = columns_of(h)
-        first = (side * heads + h + start) * (seq_size + 1)
-        codes = [(slot, code_ref[first + slot]) for slot in range(4, seq_size)]
-        if side == 1:
-            codes.append((4, code_ref[first + seq_size]))
-        read = lambda kind: block_reader(lambda slot: (stacked[slot - 4], kind * rows, local))
-        masked = masked_scores(queries[side][:, columns_of(h + start)], codes, read(0))
-        before = stats[h * 2 + side, pl.ds(0, 1), :]
-        top = jnp.maximum(before, highest(masked))
-        kept = jnp.exp2(before - top)
-        total, mixed = weigh(masked, top, codes, read(1))
-        total = total + kept * stats[h * 2 + side, pl.ds(1, 1), :]
-        mixed = mixed + kept * sums[h * 2 + side]
-        spot = (h % 2) * 2 + side
-        held[spot] = (mixed / total).T
-        for shift in range(panel_size):
-            first_row = pl.multiple_of(lax.rem(panel + shift, panel_size) * piece, piece)
-            outs[side][shift][:, local] = held[spot, pl.ds(first_row, piece), :].astype(outs[side][shift].dtype)
-
-    @pl.when(info_ref[0] == 1)
-    def _():
-        each_unit(size, unit)
+        for n, entry in enumerate(jobs):
+            job(n, *entry)
 
 
 def assemble_kernel(panel_size, starts, sizes, aliased, info_ref, *refs):
@@ -305,18 +305,22 @@
     chunks = len(sizes)
 
     middle = [send(x, across) for x in (key_rows, value_rows)]
-    packed = pl.pallas_call(
-        functools.partial(pack_kernel, starts, sizes),
-        out_shape=[jax.ShapeDtypeStruct((2 * rows, size * HEAD_DIM), key_rows.dtype) for size in sizes],
-        in_specs=[anywhere] * 2,
-        out_specs=[in_vmem] * chunks,
-        scratch_shapes=[pltpu.SemaphoreType.DMA((chunks, 2))],
-        compiler_params=pltpu.CompilerParams(vmem_limit_bytes=VMEM_GRANT),
-        name="pack",
-    )(key_rows, value_rows)
+
+    def pack(chunk, *sources):
+        return pl.pallas_call(
+            functools.partial(pack_kernel, starts, sizes, chunk),
+            out_shape=jax.ShapeDtypeStruct((len(sources) * rows, sizes[chunk] * HEAD_DIM), sources[0].dtype),
+            in_specs=[anywhere] * len(sources),
+            out_specs=in_vmem,
+            scratch_shapes=[pltpu.SemaphoreType.DMA((len(sources),))],
+            compiler_params=pltpu.CompilerParams(vmem_limit_bytes=VMEM_GRANT),
+        )(*sources)
+
+    packed = [pack(k, key_rows, value_rows) for k in range(chunks)]
+    own_queries = [pack(k, queries) for k in range(chunks)]
     beside = [send(x, partner) for x in (key_rows, value_rows)]
     ends = [send(x, inward) for x in packed]
-    guest_query = send(queries, inward)
+    guest_queries = [send(x, inward) for x in own_queries]
     middle_beside = [send(x, partner) for x in middle]
 
     is_inner = (chip >= 1) & (chip < last)
@@ -338,41 +342,64 @@
     codes = jnp.stack([arranged(position), arranged(guest)]).reshape(-1)
     info = jnp.stack([is_inner.astype(jnp.int32), panel])
 
-    units = [2 * size for size in sizes]
-    params = pltpu.CompilerParams(vmem_limit_bytes=VMEM_GRANT)
-    cost = lambda count, blocks: pl.CostEstimate(
-        flops=count * 4 * rows * blocks * BLOCK * HEAD_DIM,
-        bytes_accessed=count * blocks * 4 * BLOCK * HEAD_DIM,
-        transcendentals=count * rows * blocks * BLOCK,
-    )
-    state = pl.pallas_call(
-        functools.partial(early_kernel, seq_size, heads, starts, sizes),
-        out_shape=[jax.ShapeDtypeStruct((count, HEAD_DIM, rows), jnp.float32) for count in units]
-        + [jax.ShapeDtypeStruct((count, 8, rows), jnp.float32) for count in units],
-        in_specs=[in_smem] * 2 + [in_vmem] * 10,
-        out_specs=[in_vmem] * (2 * chunks),
-        compiler_params=params,
-        cost_estimate=cost(2 * heads, 5),
-        name="early",
-    )(info, codes, queries, guest_query, key_rows, value_rows, *beside, *middle, *middle_beside)
+    ends_beside = [send(x, partner) for x in ends]
+    far = [send(x, across) for x in ends]
+    far_beside = [send(x, partner) for x in far]
+    arrays = {}
+    for slot, pair in ((1, beside), (2, middle), (3, middle_beside)):
+        for kind in range(2):
+            arrays["whole", slot, kind] = pair[kind]
+    for k in range(chunks):
+        arrays["query", 0, k], arrays["query", 1, k] = own_queries[k], guest_queries[k]
+        for slot, parts in ((0, packed), (4, ends), (5, ends_beside), (6, far), (7, far_beside)):
+            arrays["chunk", slot, k] = parts[k]
 
     own_pieces, guest_pieces = [], []
-    for k, (start, size) in enumerate(zip(starts, sizes)):
-        far = send(ends[k], across)
-        ends_beside = send(ends[k], partner)
-        far_beside = send(far, partner)
-        outs = pl.pallas_call(
-            functools.partial(late_kernel, seq_size, panel_size, heads, start, size),
-            out_shape=[jax.ShapeDtypeStruct((rows // panel_size, size * HEAD_DIM), queries.dtype)] * (2 * panel_size),
-            in_specs=[in_smem] * 2 + [in_vmem] * 8,
-            out_specs=[in_vmem] * (2 * panel_size),
-            scratch_shapes=[pltpu.VMEM((4, rows, HEAD_DIM), jnp.float32)],
-            compiler_params=params,
-            cost_estimate=cost(2 * size, 5),
-        )(info, codes, queries, guest_query, state[k], state[chunks + k], ends[k], ends_beside, far, far_beside)
-        both = ("seq", "panel")
+    both = ("seq", "panel")
+    for name, jobs in STAGES:
+        final = name.startswith("late")
+        inputs = []
+        for side, k, slots, carry in jobs:
+            inputs.append(("query", side, k))
+            for slot in slots:
+                one = ("chunk", slot, k)
+                inputs += [one] if one in arrays else [("whole", slot, kind) for kind in range(2)]
+            if carry:
+                inputs += [("sum", side, k), ("stat", side, k)]
+        inputs = list(dict.fromkeys(inputs))
+        if final:
+            shapes = [
+                jax.ShapeDtypeStruct((rows // panel_size, sizes[k] * HEAD_DIM), queries.dtype)
+                for _, k, _, _ in jobs
+                for _ in range(panel_size)
+            ]
+        else:
+            shapes = [
+                jax.ShapeDtypeStruct((sizes[k], height, rows), jnp.float32)
+                for _, k, _, _ in jobs
+                for height in (HEAD_DIM, 8)
+            ]
+        blocks = sum(sizes[k] * (len(slots) + (HOMES[side] in slots)) for side, k, slots, _ in jobs)
+        results = pl.pallas_call(
+            functools.partial(stage_kernel, seq_size, panel_size, heads, starts, sizes, jobs, inputs, final),
+            out_shape=shapes,
+            in_specs=[in_smem] * 2 + [in_vmem] * len(inputs),
+            out_specs=[in_vmem] * len(shapes),
+            scratch_shapes=[pltpu.VMEM((UNROLL, rows, HEAD_DIM), queries.dtype)] if final else [],
+            compiler_params=pltpu.CompilerParams(vmem_limit_bytes=VMEM_GRANT),
+            cost_estimate=pl.CostEstimate(
+                flops=4 * rows * blocks * BLOCK * HEAD_DIM,
+                bytes_accessed=blocks * 4 * BLOCK * HEAD_DIM,
+                transcendentals=rows * blocks * BLOCK,
+            ),
+        )(info, codes, *(arrays[key] for key in inputs))
+        if not final:
+            for n, (side, k, _, _) in enumerate(jobs):
+                arrays["sum", side, k], arrays["stat", side, k] = results[2 * n : 2 * n + 2]
+            continue
+        k = jobs[0][1]
         for shift in range(panel_size):
-            mine, theirs = outs[shift], outs[panel_size + shift]
+            mine, theirs = results[shift], results[panel_size + shift]
             if shift:
                 mine = send(mine, pieces_of(inner, panel_size, shift), both)
             own_pieces.append(mine)

time: 168 us -> 160 us (0.952)
  waiting for transfers between devices: 113 us -> 51.3 us
  starting transfers between devices: 37.1 us -> 84.7 us
  Pallas kernels: 10 us -> 13.8 us
  local copies, waits for them, and re-layouts: 4.91 us -> 7.83 us
    ppermute x21 -> x22, waiting for transfers between devices: 113 us -> 51.3 us  [send(): return lax.ppermute(value, axes, pairs)]
    ppermute x21 -> x22, starting transfers between devices: 37.1 us -> 84.7 us  [send(): return lax.ppermute(value, axes, pairs)]
    unnamed x10 -> x20, local copies, waits for them, and re-layouts: 2.27 us -> 6.83 us
    pallas_call x4 -> x10, Pallas kernels: 7.4 us -> 11.2 us  [the longest x6 11 us: relayed(): pl.pallas_call(functools.partial(stage_kernel, seq_size, panel_size, head...]
  transfers between devices with their start and end apart: 21 -> 22, of which waited for: 5 -> 5; matrix products, arithmetic and copies ran while one was open for 3% -> 1% of each run, Pallas kernels for 5% -> 8%
where the time goes in v6:
time: 160 us; the launch traced here: 159 us
  starting transfers between devices  84.7 us (53%)
  waiting for transfers between devices  51.3 us (32%)
  Pallas kernels  13.8 us (9%)
  local copies, waits for them, and re-layouts  7.83 us (5%)
    ppermute x22, starting transfers between devices, send(): return lax.ppermute(value, axes, pairs)  84.7 us
    ppermute x22, waiting for transfers between devices, send(): return lax.ppermute(value, axes, pairs)  51.3 us
    pallas_call x6, Pallas kernels, relayed(): pl.pallas_call(functools.partial(stage_kernel, seq_size, panel_size, head...  11 us
    unnamed x20, local copies, waits for them, and re-layouts  6.83 us
  transfers between devices with their start and end apart: 22, of which 5 were waited for; matrix products, arithmetic and copies ran while one was open for 1% of the time, Pallas kernels for 8%

profile of v6, /device:TPU:0, one launch (start us, length us, event | category | flops | bytes accessed | tf_op | source)
XLA Modules:
  0.0 159.2 jit_solution(14201718570265515337)
XLA Ops:
  0.0 0.7 collective-permute-start.8
  0.7 1.5 collective-permute-start.3
  2.2 0.7 collective-permute-start.9
  3.0 1.1 copy-done.3
  4.1 1.1 copy-done.4
  5.2 0.1 shard_map.74.refs_3_
  5.3 10.5 %collective-permute-start = (bf16[512,896]{1,0:T(8,128)(2,1)S(1)}, bf16[512,896]{1,0:T(8,128)(2,1)}, u32[]{:S(2)}, u32[]{:S(2)}) collective-permute-start(bf16[512,896]{1,0:T(8,128)(2,1)S(1)} %shard_map.74.refs_3_), channel_id=1, source_target_pairs={{0,4},{2,6},{12,8},{14,10},{1,5},{3,7},{13,9},{15,11},{16,20},{18,... | collective-permute-start | bytes 2752520 | tf_op jit(solution)/shard_map/ppermute | solution.py:126
  15.9 2.3 %collective-permute-start.14 = (bf16[512,640]{1,0:T(8,128)(2,1)S(1)}, bf16[512,640]{1,0:T(8,128)(2,1)}, u32[]{:S(2)}, u32[]{:S(2)}) collective-permute-start(bf16[512,640]{1,0:T(8,128)(2,1)S(1)} %shard_map.76.refs_7_.refs_3_), channel_id=1, source_target_pairs={{0,4},{2,6},{12,8},{14,10},{1,5},{3,7},{13,9},{15,11},{16,20},{18,... | collective-permute-start | bytes 1966088 | tf_op jit(solution)/shard_map/ppermute | solution.py:126
  18.3 0.1 copy.22
  18.4 0.6 copy-done.8
  19.2 0.1 fusion.1
  19.4 0.1 copy.25
  19.5 0.1 fusion.3
  19.9 29.1 %collective-permute-done.14.refs_10_ = bf16[512,640]{1,0:T(8,128)(2,1)} collective-permute-done((bf16[512,640]{1,0:T(8,128)(2,1)S(1)}, bf16[512,640]{1,0:T(8,128)(2,1)}, u32[]{:S(2)}, u32[]{:S(2)}) %collective-permute-start.14) | collective-permute-done | bytes 655392 | tf_op jit(solution)/shard_map/ppermute | solution.py:126
  49.0 1.5 collective-permute-start.4
  50.5 1.6 %collective-permute-start.1 = (bf16[512,896]{1,0:T(8,128)(2,1)}, bf16[512,896]{1,0:T(8,128)(2,1)}, u32[]{:S(2)}, u32[]{:S(2)}) collective-permute-start(bf16[512,896]{1,0:T(8,128)(2,1)} %collective-permute-done.refs_7_.refs_10_), channel_id=1, source_target_pairs={{4,8},{6,10},{8,4},{10,6},{5,9},{7,11},{9,5},{11,7},{20,24},{22,26... | collective-permute-start | bytes 2752520 | tf_op jit(solution)/shard_map/ppermute | solution.py:126
  52.2 1.1 copy-done.5
  53.5 0.6 copy-done.9
  54.3 1.5 collective-permute-start.15
  55.8 1.6 collective-permute-start.5
  57.4 1.5 collective-permute-start.6
  59.0 1.6 %collective-permute-start.7 = (bf16[512,896]{1,0:T(8,128)(2,1)}, bf16[512,896]{1,0:T(8,128)(2,1)}, u32[]{:S(2)}, u32[]{:S(2)}) collective-permute-start(bf16[512,896]{1,0:T(8,128)(2,1)} %collective-permute-done.refs_7_.refs_10_), channel_id=1, source_target_pairs={{4,6},{6,4},{8,10},{10,8},{5,7},{7,5},{9,11},{11,9},{20,22},{22,20... | collective-permute-start | bytes 2752520 | tf_op jit(solution)/shard_map/ppermute | solution.py:126
  60.6 1.6 %collective-permute-start.2 = (bf16[512,896]{1,0:T(8,128)(2,1)}, bf16[512,896]{1,0:T(8,128)(2,1)}, u32[]{:S(2)}, u32[]{:S(2)}) collective-permute-start(bf16[512,896]{1,0:T(8,128)(2,1)} %collective-permute-done.1.refs_3_), channel_id=1, source_target_pairs={{4,6},{6,4},{8,10},{10,8},{5,7},{7,5},{9,11},{11,9},{20,22},{22,20... | collective-permute-start | bytes 2752520 | tf_op jit(solution)/shard_map/ppermute | solution.py:126
  62.4 46.6 %collective-permute-start.10 = (bf16[256,896]{1,0:T(8,128)(2,1)S(1)}, bf16[256,896]{1,0:T(8,128)(2,1)}, u32[]{:S(2)}, u32[]{:S(2)}) collective-permute-start(bf16[256,896]{1,0:T(8,128)(2,1)S(1)} %shard_map.73.refs_2_), channel_id=1, source_target_pairs={{0,4},{2,6},{12,8},{14,10},{1,5},{3,7},{13,9},{15,11},{16,20},{18,... | collective-permute-start | bytes 1376264 | tf_op jit(solution)/shard_map/ppermute | solution.py:126
  109.0 1.1 copy-done.6
  110.3 1.6 collective-permute-start.18
  111.9 0.1 copy.29
  112.0 1.5 collective-permute-start.16
  113.7 1.8 %collective-permute-start.17 = (bf16[256,640]{1,0:T(8,128)(2,1)S(1)}, bf16[256,640]{1,0:T(8,128)(2,1)S(1)}, u32[]{:S(2)}, u32[]{:S(2)}) collective-permute-start(bf16[256,640]{1,0:T(8,128)(2,1)S(1)} %shard_map.75.refs_6_.refs_11_.refs_12_.refs_2_), channel_id=1, source_target_pairs={{0,4},{2,6},{12,8},{14,10},{1,5},{3,7},{13,9},{15,11},{16,20},{18,... | collective-permute-start | bytes 983048 | tf_op jit(solution)/shard_map/ppermute | solution.py:126
  115.5 1.1 copy-done.1
  116.6 0.6 shard_map.77
  117.2 2.4 %shard_map.78 = (f32[7,128,256]{2,1,0:T(8,128)S(1)}, f32[7,8,256]{2,1,0:T(8,128)S(1)}, f32[5,128,256]{2,1,0:T(8,128)S(1)}, f32[5,8,256]{2,1,0:T(8,128)S(1)}) custom-call(s32[2]{0:T(128)S(1)} %pad_add_fusion.3.refs_0_.info_ref, s32[216]{0:T(256)S(1)} %reshape.60.refs_1_, bf16[256,896]{1,0:T(8,128)(2,1)S(1)} %shard_map.73.refs_2_, ...), custom_call_target="tpu_custom_call" | custom-call | flops 637534208 | bytes 2490368 | tf_op jit(solution)/shard_map/pallas_call | solution.py:383
  119.6 2.6 %shard_map.79 = (f32[7,128,256]{2,1,0:T(8,128)S(1)}, f32[7,8,256]{2,1,0:T(8,128)S(1)}) custom-call(s32[2]{0:T(128)S(1)} %pad_add_fusion.3.refs_0_.info_ref, s32[216]{0:T(256)S(1)} %reshape.60.refs_1_, bf16[256,896]{1,0:T(8,128)(2,1)} %collective-permute-done.10.refs_2_.refs_7_, bf16[512,896]{1,0:T(8,128)(2,1)S(1)} %shard_map.74.refs_3_, ...), custom_call_target="tpu_custom_call" | custom-call | flops 822083584 | bytes 3211264 | tf_op jit(solution)/shard_map/pallas_call | solution.py:383
  122.2 1.7 %shard_map.80 = (bf16[128,896]{1,0:T(8,128)(2,1)S(1)}, bf16[128,896]{1,0:T(8,128)(2,1)S(1)}, bf16[128,896]{1,0:T(8,128)(2,1)S(1)}, bf16[128,896]{1,0:T(8,128)(2,1)S(1)}) custom-call(s32[2]{0:T(128)S(1)} %pad_add_fusion.3.refs_0_.info_ref, s32[216]{0:T(256)S(1)} %reshape.60.refs_1_, bf16[256,896]{1,0:T(8,128)(2,1)S(1)} %shard_map.73.refs_2_, ...), custom_call_target="tpu_custom_call" | custom-call | flops 469762048 | bytes 1835008 | tf_op jit(solution)/shard_map/pallas_call | solution.py:383
  123.9 0.7 collective-permute-start.11
  124.6 1.3 collective-permute-start.12
  125.9 1.3 collective-permute-start.13
  127.2 2.4 %shard_map.82 = (f32[5,128,256]{2,1,0:T(8,128)S(1)}, f32[5,8,256]{2,1,0:T(8,128)S(1)}, f32[5,128,256]{2,1,0:T(8,128)S(1)}, f32[5,8,256]{2,1,0:T(8,128)S(1)}) custom-call(s32[2]{0:T(128)S(1)} %pad_add_fusion.3.refs_0_.info_ref, s32[216]{0:T(256)S(1)} %reshape.60.refs_1_, bf16[256,640]{1,0:T(8,128)(2,1)S(1)} %collective-permute-done.17.refs_2_.refs_7_, ...), custom_call_target="tpu_custom_call" | custom-call | flops 754974720 | bytes 2949120 | tf_op jit(solution)/shard_map/pallas_call | solution.py:383
  129.6 1.3 shard_map.83
  131.0 0.7 collective-permute-start.19
  131.6 1.3 collective-permute-start.20
  133.0 1.3 collective-permute-start.21
  134.3 8.8 %collective-permute-done.12.refs_2_ = bf16[128,896]{1,0:T(8,128)(2,1)S(1)} collective-permute-done((bf16[128,896]{1,0:T(8,128)(2,1)S(1)}, bf16[128,896]{1,0:T(8,128)(2,1)S(1)}, u32[]{:S(2)}, u32[]{:S(2)}) %collective-permute-start.12) | collective-permute-done | bytes 229408 | tf_op jit(solution)/shard_map/ppermute | solution.py:126
  143.1 3.9 %collective-permute-done.13.refs_3_ = bf16[128,896]{1,0:T(8,128)(2,1)S(1)} collective-permute-done((bf16[128,896]{1,0:T(8,128)(2,1)S(1)}, bf16[128,896]{1,0:T(8,128)(2,1)S(1)}, u32[]{:S(2)}, u32[]{:S(2)}) %collective-permute-start.13) | collective-permute-done | bytes 229408 | tf_op jit(solution)/shard_map/ppermute | solution.py:126
  147.0 1.3 shard_map.81.refs_0_
  148.3 6.3 %collective-permute-done.20.refs_3_ = bf16[128,640]{1,0:T(8,128)(2,1)S(1)} collective-permute-done((bf16[128,640]{1,0:T(8,128)(2,1)S(1)}, bf16[128,640]{1,0:T(8,128)(2,1)S(1)}, u32[]{:S(2)}, u32[]{:S(2)}) %collective-permute-start.20) | collective-permute-done | bytes 163872 | tf_op jit(solution)/shard_map/ppermute | solution.py:126
  154.6 3.2 %collective-permute-done.21.refs_4_ = bf16[128,640]{1,0:T(8,128)(2,1)S(1)} collective-permute-done((bf16[128,640]{1,0:T(8,128)(2,1)S(1)}, bf16[128,640]{1,0:T(8,128)(2,1)S(1)}, u32[]{:S(2)}, u32[]{:S(2)}) %collective-permute-start.21) | collective-permute-done | bytes 163872 | tf_op jit(solution)/shard_map/ppermute | solution.py:126
  157.8 1.3 shard_map.84
  (59 shorter events, 1.6 us)
Async XLA Ops:
  0.0 54.3 %collective-permute-start.8 = (bf16[256,1536]{1,0:T(8,128)(2,1)}, bf16[256,1536]{1,0:T(8,128)(2,1)S(1)}, u32[]{:S(2)}, u32[]{:S(2)}) collective-permute-start(bf16[256,1536]{1,0:T(8,128)(2,1)} %refs_0_.7), channel_id=1, source_target_pairs={{4,6},{6,4},{8,10},{10,8},{5,7},{7,5},{9,11},{11,9},{20,22},{22,20... | collective-permute-start | bytes 2359304 | tf_op jit(solution)/shard_map/ppermute | solution.py:126
  0.7 55.1 %collective-permute-start.3 = (bf16[256,1536]{1,0:T(8,128)(2,1)}, bf16[256,1536]{1,0:T(8,128)(2,1)}, u32[]{:S(2)}, u32[]{:S(2)}) collective-permute-start(bf16[256,1536]{1,0:T(8,128)(2,1)} %refs_0_.7), channel_id=1, source_target_pairs={{4,8},{6,10},{8,4},{10,6},{5,9},{7,11},{9,5},{11,7},{20,24},{22,26... | collective-permute-start | bytes 2359304 | tf_op jit(solution)/shard_map/ppermute | solution.py:126
  2.2 56.7 %collective-permute-start.9 = (bf16[256,1536]{1,0:T(8,128)(2,1)}, bf16[256,1536]{1,0:T(8,128)(2,1)S(1)}, u32[]{:S(2)}, u32[]{:S(2)}) collective-permute-start(bf16[256,1536]{1,0:T(8,128)(2,1)} %refs_1_.3), channel_id=1, source_target_pairs={{4,6},{6,4},{8,10},{10,8},{5,7},{7,5},{9,11},{11,9},{20,22},{22,20... | collective-permute-start | bytes 2359304 | tf_op jit(solution)/shard_map/ppermute | solution.py:126
  3.0 1.1 copy-start.3
  4.1 1.1 copy-start.4
  5.3 45.2 %collective-permute-start = (bf16[512,896]{1,0:T(8,128)(2,1)S(1)}, bf16[512,896]{1,0:T(8,128)(2,1)}, u32[]{:S(2)}, u32[]{:S(2)}) collective-permute-start(bf16[512,896]{1,0:T(8,128)(2,1)S(1)} %shard_map.74.refs_3_), channel_id=1, source_target_pairs={{0,4},{2,6},{12,8},{14,10},{1,5},{3,7},{13,9},{15,11},{16,20},{18,... | collective-permute-start | bytes 2752520 | tf_op jit(solution)/shard_map/ppermute | solution.py:126
  15.9 36.3 %copy-start = (bf16[512,640]{1,0:T(8,128)(2,1)}, bf16[512,640]{1,0:T(8,128)(2,1)S(1)}, u32[]{:S(2)}) copy-start(bf16[512,640]{1,0:T(8,128)(2,1)S(1)} %shard_map.76.refs_7_.refs_3_) | copy-start | bytes 1966084
  15.9 2.3 %copy-start.7 = (s32[12,16,8]{1,2,0:T(8,128)S(1)}, s32[12,16,8]{1,2,0:T(8,128)}, u32[]{:S(2)}) copy-start(s32[12,16,8]{1,2,0:T(8,128)} %param.10) | copy-start | bytes 18436
  15.9 33.1 %collective-permute-start.14 = (bf16[512,640]{1,0:T(8,128)(2,1)S(1)}, bf16[512,640]{1,0:T(8,128)(2,1)}, u32[]{:S(2)}, u32[]{:S(2)}) collective-permute-start(bf16[512,640]{1,0:T(8,128)(2,1)S(1)} %shard_map.76.refs_7_.refs_3_), channel_id=1, source_target_pairs={{0,4},{2,6},{12,8},{14,10},{1,5},{3,7},{13,9},{15,11},{16,20},{18,... | collective-permute-start | bytes 1966088 | tf_op jit(solution)/shard_map/ppermute | solution.py:126
  18.3 0.7 copy-start.8
  49.0 8.4 %collective-permute-start.4 = (bf16[256,1536]{1,0:T(8,128)(2,1)}, bf16[256,1536]{1,0:T(8,128)(2,1)}, u32[]{:S(2)}, u32[]{:S(2)}) collective-permute-start(bf16[256,1536]{1,0:T(8,128)(2,1)} %refs_1_.3), channel_id=1, source_target_pairs={{4,8},{6,10},{8,4},{10,6},{5,9},{7,11},{9,5},{11,7},{20,24},{22,26... | collective-permute-start | bytes 2359304 | tf_op jit(solution)/shard_map/ppermute | solution.py:126
  50.5 10.1 %collective-permute-start.1 = (bf16[512,896]{1,0:T(8,128)(2,1)}, bf16[512,896]{1,0:T(8,128)(2,1)}, u32[]{:S(2)}, u32[]{:S(2)}) collective-permute-start(bf16[512,896]{1,0:T(8,128)(2,1)} %collective-permute-done.refs_7_.refs_10_), channel_id=1, source_target_pairs={{4,8},{6,10},{8,4},{10,6},{5,9},{7,11},{9,5},{11,7},{20,24},{22,26... | collective-permute-start | bytes 2752520 | tf_op jit(solution)/shard_map/ppermute | solution.py:126
  52.2 1.1 copy-start.5
  53.5 0.7 copy-start.9
  54.3 8.1 %collective-permute-start.15 = (bf16[512,640]{1,0:T(8,128)(2,1)}, bf16[512,640]{1,0:T(8,128)(2,1)}, u32[]{:S(2)}, u32[]{:S(2)}) collective-permute-start(bf16[512,640]{1,0:T(8,128)(2,1)} %collective-permute-done.14.refs_10_), channel_id=1, source_target_pairs={{4,8},{6,10},{8,4},{10,6},{5,9},{7,11},{9,5},{11,7},{20,24},{22,26... | collective-permute-start | bytes 1966088 | tf_op jit(solution)/shard_map/ppermute | solution.py:126
  55.8 54.5 %collective-permute-start.5 = (bf16[256,1536]{1,0:T(8,128)(2,1)}, bf16[256,1536]{1,0:T(8,128)(2,1)}, u32[]{:S(2)}, u32[]{:S(2)}) collective-permute-start(bf16[256,1536]{1,0:T(8,128)(2,1)} %collective-permute-done.3.refs_3_.refs_6_), channel_id=1, source_target_pairs={{4,6},{6,4},{8,10},{10,8},{5,7},{7,5},{9,11},{11,9},{20,22},{22,20... | collective-permute-start | bytes 2359304 | tf_op jit(solution)/shard_map/ppermute | solution.py:126
  57.4 54.6 %collective-permute-start.6 = (bf16[256,1536]{1,0:T(8,128)(2,1)}, bf16[256,1536]{1,0:T(8,128)(2,1)}, u32[]{:S(2)}, u32[]{:S(2)}) collective-permute-start(bf16[256,1536]{1,0:T(8,128)(2,1)} %collective-permute-done.4.refs_4_.refs_7_), channel_id=1, source_target_pairs={{4,6},{6,4},{8,10},{10,8},{5,7},{7,5},{9,11},{11,9},{20,22},{22,20... | collective-permute-start | bytes 2359304 | tf_op jit(solution)/shard_map/ppermute | solution.py:126
  59.0 54.8 %collective-permute-start.7 = (bf16[512,896]{1,0:T(8,128)(2,1)}, bf16[512,896]{1,0:T(8,128)(2,1)}, u32[]{:S(2)}, u32[]{:S(2)}) collective-permute-start(bf16[512,896]{1,0:T(8,128)(2,1)} %collective-permute-done.refs_7_.refs_10_), channel_id=1, source_target_pairs={{4,6},{6,4},{8,10},{10,8},{5,7},{7,5},{9,11},{11,9},{20,22},{22,20... | collective-permute-start | bytes 2752520 | tf_op jit(solution)/shard_map/ppermute | solution.py:126
  60.6 61.5 %collective-permute-start.2 = (bf16[512,896]{1,0:T(8,128)(2,1)}, bf16[512,896]{1,0:T(8,128)(2,1)}, u32[]{:S(2)}, u32[]{:S(2)}) collective-permute-start(bf16[512,896]{1,0:T(8,128)(2,1)} %collective-permute-done.1.refs_3_), channel_id=1, source_target_pairs={{4,6},{6,4},{8,10},{10,8},{5,7},{7,5},{9,11},{11,9},{20,22},{22,20... | collective-permute-start | bytes 2752520 | tf_op jit(solution)/shard_map/ppermute | solution.py:126
  62.4 57.2 %collective-permute-start.10 = (bf16[256,896]{1,0:T(8,128)(2,1)S(1)}, bf16[256,896]{1,0:T(8,128)(2,1)}, u32[]{:S(2)}, u32[]{:S(2)}) collective-permute-start(bf16[256,896]{1,0:T(8,128)(2,1)S(1)} %shard_map.73.refs_2_), channel_id=1, source_target_pairs={{0,4},{2,6},{12,8},{14,10},{1,5},{3,7},{13,9},{15,11},{16,20},{18,... | collective-permute-start | bytes 1376264 | tf_op jit(solution)/shard_map/ppermute | solution.py:126
  109.0 1.1 copy-start.6
  110.3 16.9 %collective-permute-start.18 = (bf16[512,640]{1,0:T(8,128)(2,1)}, bf16[512,640]{1,0:T(8,128)(2,1)}, u32[]{:S(2)}, u32[]{:S(2)}) collective-permute-start(bf16[512,640]{1,0:T(8,128)(2,1)} %collective-permute-done.14.refs_10_), channel_id=1, source_target_pairs={{4,6},{6,4},{8,10},{10,8},{5,7},{7,5},{9,11},{11,9},{20,22},{22,20... | collective-permute-start | bytes 1966088 | tf_op jit(solution)/shard_map/ppermute | solution.py:126
  112.0 17.7 %collective-permute-start.16 = (bf16[512,640]{1,0:T(8,128)(2,1)}, bf16[512,640]{1,0:T(8,128)(2,1)}, u32[]{:S(2)}, u32[]{:S(2)}) collective-permute-start(bf16[512,640]{1,0:T(8,128)(2,1)} %collective-permute-done.15.refs_3_), channel_id=1, source_target_pairs={{4,6},{6,4},{8,10},{10,8},{5,7},{7,5},{9,11},{11,9},{20,22},{22,20... | collective-permute-start | bytes 1966088 | tf_op jit(solution)/shard_map/ppermute | solution.py:126
  113.7 12.1 %collective-permute-start.17 = (bf16[256,640]{1,0:T(8,128)(2,1)S(1)}, bf16[256,640]{1,0:T(8,128)(2,1)S(1)}, u32[]{:S(2)}, u32[]{:S(2)}) collective-permute-start(bf16[256,640]{1,0:T(8,128)(2,1)S(1)} %shard_map.75.refs_6_.refs_11_.refs_12_.refs_2_), channel_id=1, source_target_pairs={{0,4},{2,6},{12,8},{14,10},{1,5},{3,7},{13,9},{15,11},{16,20},{18,... | collective-permute-start | bytes 983048 | tf_op jit(solution)/shard_map/ppermute | solution.py:126
  115.5 1.1 copy-start.1
  122.2 5.0 %copy-start.2 = (bf16[512,640]{1,0:T(8,128)(2,1)S(1)}, bf16[512,640]{1,0:T(8,128)(2,1)}, u32[]{:S(2)}) copy-start(bf16[512,640]{1,0:T(8,128)(2,1)} %copy-done) | copy-start | bytes 1966084
  123.9 9.1 %collective-permute-start.11 = (bf16[128,896]{1,0:T(8,128)(2,1)S(1)}, bf16[128,896]{1,0:T(8,128)(2,1)S(1)}, u32[]{:S(2)}, u32[]{:S(2)}) collective-permute-start(bf16[128,896]{1,0:T(8,128)(2,1)S(1)} %get-tuple-element.36), channel_id=1, source_target_pairs={{4,5},{5,4},{6,7},{7,6},{8,9},{9,8},{10,11},{11,10},{20,21},{21,20... | collective-permute-start | bytes 688136 | tf_op jit(solution)/shard_map/ppermute | solution.py:126
  124.6 18.5 %collective-permute-start.12 = (bf16[128,896]{1,0:T(8,128)(2,1)S(1)}, bf16[128,896]{1,0:T(8,128)(2,1)S(1)}, u32[]{:S(2)}, u32[]{:S(2)}) collective-permute-start(bf16[128,896]{1,0:T(8,128)(2,1)S(1)} %get-tuple-element.37), channel_id=1, source_target_pairs={{4,0},{5,1},{6,2},{7,3},{8,12},{9,13},{10,14},{11,15},{20,16},{21,... | collective-permute-start | bytes 688136 | tf_op jit(solution)/shard_map/ppermute | solution.py:126
  125.9 21.1 %collective-permute-start.13 = (bf16[128,896]{1,0:T(8,128)(2,1)S(1)}, bf16[128,896]{1,0:T(8,128)(2,1)S(1)}, u32[]{:S(2)}, u32[]{:S(2)}) collective-permute-start(bf16[128,896]{1,0:T(8,128)(2,1)S(1)} %get-tuple-element.38), channel_id=1, source_target_pairs={{4,1},{5,0},{6,3},{7,2},{8,13},{9,12},{10,15},{11,14},{20,17},{21,... | collective-permute-start | bytes 688136 | tf_op jit(solution)/shard_map/ppermute | solution.py:126
  131.0 17.4 %collective-permute-start.19 = (bf16[128,640]{1,0:T(8,128)(2,1)S(1)}, bf16[128,640]{1,0:T(8,128)(2,1)S(1)}, u32[]{:S(2)}, u32[]{:S(2)}) collective-permute-start(bf16[128,640]{1,0:T(8,128)(2,1)S(1)} %get-tuple-element.46), channel_id=1, source_target_pairs={{4,5},{5,4},{6,7},{7,6},{8,9},{9,8},{10,11},{11,10},{20,21},{21,20... | collective-permute-start | bytes 491528 | tf_op jit(solution)/shard_map/ppermute | solution.py:126
  131.6 22.9 %collective-permute-start.20 = (bf16[128,640]{1,0:T(8,128)(2,1)S(1)}, bf16[128,640]{1,0:T(8,128)(2,1)S(1)}, u32[]{:S(2)}, u32[]{:S(2)}) collective-permute-start(bf16[128,640]{1,0:T(8,128)(2,1)S(1)} %get-tuple-element.47), channel_id=1, source_target_pairs={{4,0},{5,1},{6,2},{7,3},{8,12},{9,13},{10,14},{11,15},{20,16},{21,... | collective-permute-start | bytes 491528 | tf_op jit(solution)/shard_map/ppermute | solution.py:126
  133.0 24.8 %collective-permute-start.21 = (bf16[128,640]{1,0:T(8,128)(2,1)S(1)}, bf16[128,640]{1,0:T(8,128)(2,1)S(1)}, u32[]{:S(2)}, u32[]{:S(2)}) collective-permute-start(bf16[128,640]{1,0:T(8,128)(2,1)S(1)} %get-tuple-element.48), channel_id=1, source_target_pairs={{4,1},{5,0},{6,3},{7,2},{8,13},{9,12},{10,15},{11,14},{20,17},{21,... | collective-permute-start | bytes 491528 | tf_op jit(solution)/shard_map/ppermute | solution.py:126

commit v7 on v6

--- a/solution.py
+++ b/solution.py
@@ -22,8 +22,10 @@
     ("early_1", ((0, 0, (2, 3, 4, 5), True), (0, 1, (2, 3), True))),
     ("early_2", ((1, 0, (0, 1, 2, 3, 4, 5), False),)),
     ("early_3", ((1, 1, (0, 1, 2, 3, 4, 5), False), (0, 1, (4, 5), True))),
-    ("late_0", ((0, 0, (6, 7), True), (1, 0, (6, 7), True))),
-    ("late_1", ((0, 1, (6, 7), True), (1, 1, (6, 7), True))),
+    ("late_0", ((1, 0, (6, 7), True),)),
+    ("late_3", ((0, 0, (6, 7), True),)),
+    ("late_1", ((1, 1, (6, 7), True),)),
+    ("late_2", ((0, 1, (6, 7), True),)),
 )
 
 
@@ -354,7 +356,7 @@
         for slot, parts in ((0, packed), (4, ends), (5, ends_beside), (6, far), (7, far_beside)):
             arrays["chunk", slot, k] = parts[k]
 
-    own_pieces, guest_pieces = [], []
+    pieces = {}
     both = ("seq", "panel")
     for name, jobs in STAGES:
         final = name.startswith("late")
@@ -397,30 +399,30 @@
             for n, (side, k, _, _) in enumerate(jobs):
                 arrays["sum", side, k], arrays["stat", side, k] = results[2 * n : 2 * n + 2]
             continue
-        k = jobs[0][1]
-        for shift in range(panel_size):
-            mine, theirs = results[shift], results[panel_size + shift]
-            if shift:
-                mine = send(mine, pieces_of(inner, panel_size, shift), both)
-            own_pieces.append(mine)
-            guest_pieces.append(send(theirs, pieces_of(outward, panel_size, shift), both))
-
-    split = (chunks - 1) * panel_size
+        for n, (side, k, _, _) in enumerate(jobs):
+            for shift in range(panel_size):
+                piece = results[n * panel_size + shift]
+                if side == 1:
+                    piece = send(piece, pieces_of(outward, panel_size, shift), both)
+                elif shift:
+                    piece = send(piece, pieces_of(inner, panel_size, shift), both)
+                pieces[side, k, shift] = piece
+
     out = None
-    for lo, hi, first, final in ((0, split, 0, chunks - 1), (split, chunks * panel_size, chunks - 1, chunks)):
-        if lo == hi:
-            continue
-        pieces = own_pieces[lo:hi] + guest_pieces[lo:hi]
+    for first, final in ((0, chunks - 1), (chunks - 1, chunks)):
+        parts = [
+            pieces[side, k, shift] for side in range(2) for k in range(first, final) for shift in range(panel_size)
+        ]
         before = [] if out is None else [out]
         out = pl.pallas_call(
             functools.partial(assemble_kernel, panel_size, starts[first:final], sizes[first:final], len(before)),
             out_shape=jax.ShapeDtypeStruct((rows // panel_size, width * panel_size), queries.dtype),
-            in_specs=[in_smem] + [anywhere] * len(before) + [in_vmem] * len(pieces),
+            in_specs=[in_smem] + [anywhere] * len(before) + [in_vmem] * len(parts),
             out_specs=anywhere,
             scratch_shapes=[pltpu.SemaphoreType.DMA((panel_size, final - first))],
             input_output_aliases={1: 0} if before else {},
             compiler_params=pltpu.CompilerParams(vmem_limit_bytes=VMEM_GRANT),
-        )(info, *before, *pieces)
+        )(info, *before, *parts)
     return out
 
 

time: 160 us -> 170 us (1.062)
  Pallas kernels: 13.8 us -> 17.9 us
  waiting for transfers between devices: 51.3 us -> 54.2 us
  starting transfers between devices: 84.7 us -> 86.8 us
    pallas_call x6 -> x8, Pallas kernels: 11 us -> 14.2 us  [relayed(): pl.pallas_call(functools.partial(stage_kernel, seq_size, panel_size, head...]
    ppermute x22, waiting for transfers between devices: 51.3 us -> 54.2 us  [send(): return lax.ppermute(value, axes, pairs)]
    ppermute x22, starting transfers between devices: 84.7 us -> 86.8 us  [send(): return lax.ppermute(value, axes, pairs)]
    unnamed x20 -> x18, local copies, waits for them, and re-layouts: 6.83 us -> 6.41 us
  transfers between devices with their start and end apart: 22 -> 22, of which waited for: 5 -> 4; matrix products, arithmetic and copies ran while one was open for 1% -> 1% of each run, Pallas kernels for 8% -> 10%
where the time goes in v7:
time: 170 us; the launch traced here: 168 us
  starting transfers between devices  86.8 us (51%)
  waiting for transfers between devices  54.2 us (32%)
  Pallas kernels  17.9 us (11%)
  local copies, waits for them, and re-layouts  7.41 us (4%)
    ppermute x22, starting transfers between devices, send(): return lax.ppermute(value, axes, pairs)  86.8 us
    ppermute x22, waiting for transfers between devices, send(): return lax.ppermute(value, axes, pairs)  54.2 us
    pallas_call x8, Pallas kernels, relayed(): pl.pallas_call(functools.partial(stage_kernel, seq_size, panel_size, head...  14.2 us
    unnamed x18, local copies, waits for them, and re-layouts  6.41 us
  transfers between devices with their start and end apart: 22, of which 4 were waited for; matrix products, arithmetic and copies ran while one was open for 1% of the time, Pallas kernels for 10%

profile of v7, /device:TPU:0, one launch (start us, length us, event | category | flops | bytes accessed | tf_op | source)
XLA Modules:
  0.0 167.9 jit_solution(3362016772799998623)
XLA Ops:
  0.0 0.7 collective-permute-start.8
  0.7 1.5 collective-permute-start.3
  2.2 1.1 copy-done
  3.4 1.1 copy-done.1
  4.6 9.2 %collective-permute-start = (bf16[512,896]{1,0:T(8,128)(2,1)S(1)}, bf16[512,896]{1,0:T(8,128)(2,1)}, u32[]{:S(2)}, u32[]{:S(2)}) collective-permute-start(bf16[512,896]{1,0:T(8,128)(2,1)S(1)} %shard_map.74.refs_3_), channel_id=1, source_target_pairs={{0,4},{2,6},{12,8},{14,10},{1,5},{3,7},{13,9},{15,11},{16,20},{18,... | collective-permute-start | bytes 2752520 | tf_op jit(solution)/shard_map/ppermute | solution.py:128
  13.8 0.9 shard_map.76.refs_7_.refs_3_
  14.7 2.1 %collective-permute-start.14 = (bf16[512,640]{1,0:T(8,128)(2,1)}, bf16[512,640]{1,0:T(8,128)(2,1)}, u32[]{:S(2)}, u32[]{:S(2)}) collective-permute-start(bf16[512,640]{1,0:T(8,128)(2,1)} %shard_map.76.refs_7_.refs_3_), channel_id=1, source_target_pairs={{0,4},{2,6},{12,8},{14,10},{1,5},{3,7},{13,9},{15,11},{16,20},{18,... | collective-permute-start | bytes 1966088 | tf_op jit(solution)/shard_map/ppermute | solution.py:128
  17.0 1.4 collective-permute-start.11
  18.6 0.1 copy.22
  18.7 0.6 copy-done.7
  19.4 0.1 fusion.1
  19.7 0.1 copy.25
  19.9 0.1 fusion.3
  20.1 36.6 %collective-permute-done.11.refs_2_ = bf16[256,896]{1,0:T(8,128)(2,1)S(1)} collective-permute-done((bf16[256,896]{1,0:T(8,128)(2,1)S(1)}, bf16[256,896]{1,0:T(8,128)(2,1)S(1)}, u32[]{:S(2)}, u32[]{:S(2)}) %collective-permute-start.11) | collective-permute-done | bytes 458784 | tf_op jit(solution)/shard_map/ppermute | solution.py:128
  56.8 0.8 copy-done.4
  57.5 0.7 collective-permute-start.9
  58.2 1.6 collective-permute-start.1
  59.9 1.6 collective-permute-start.4
  61.5 0.7 copy-done.8
  62.2 1.6 collective-permute-start.5
  64.0 1.5 collective-permute-start.15
  65.5 1.6 collective-permute-start.7
  67.2 1.5 collective-permute-start.6
  68.7 1.6 collective-permute-start.2
  70.5 1.6 collective-permute-start.18
  72.1 1.6 collective-permute-start.16
  73.7 1.1 copy-done.3
  75.2 50.4 %collective-permute-start.17 = (bf16[256,640]{1,0:T(8,128)(2,1)S(1)}, bf16[256,640]{1,0:T(8,128)(2,1)S(1)}, u32[]{:S(2)}, u32[]{:S(2)}) collective-permute-start(bf16[256,640]{1,0:T(8,128)(2,1)S(1)} %shard_map.75.refs_6_.refs_11_.refs_12_.refs_2_), channel_id=1, source_target_pairs={{0,4},{2,6},{12,8},{14,10},{1,5},{3,7},{13,9},{15,11},{16,20},{18,... | collective-permute-start | bytes 983048 | tf_op jit(solution)/shard_map/ppermute | solution.py:128
  125.7 1.0 copy-done.5
  126.7 2.4 %shard_map.80 = (f32[7,128,256]{2,1,0:T(8,128)S(1)}, f32[7,8,256]{2,1,0:T(8,128)S(1)}) custom-call(s32[2]{0:T(128)S(1)} %pad_add_fusion.3.refs_0_.info_ref, s32[216]{0:T(256)S(1)} %reshape.60.refs_1_, bf16[256,896]{1,0:T(8,128)(2,1)S(1)} %copy-done.5, bf16[512,896]{1,0:T(8,128)(2,1)S(1)} %shard_map.74.refs_3_, ...), custom_call_target="tpu_custom_call" | custom-call | flops 822083584 | bytes 3211264 | tf_op jit(solution)/shard_map/pallas_call | solution.py:385
  129.1 1.5 shard_map.81
  130.6 1.3 collective-permute-start.12
  131.9 1.1 shard_map.77
  133.0 2.4 %shard_map.78 = (f32[7,128,256]{2,1,0:T(8,128)S(1)}, f32[7,8,256]{2,1,0:T(8,128)S(1)}, f32[5,128,256]{2,1,0:T(8,128)S(1)}, f32[5,8,256]{2,1,0:T(8,128)S(1)}) custom-call(s32[2]{0:T(128)S(1)} %pad_add_fusion.3.refs_0_.info_ref, s32[216]{0:T(256)S(1)} %reshape.60.refs_1_, bf16[256,896]{1,0:T(8,128)(2,1)S(1)} %shard_map.73.refs_2_, ...), custom_call_target="tpu_custom_call" | custom-call | flops 637534208 | bytes 2490368 | tf_op jit(solution)/shard_map/pallas_call | solution.py:385
  135.5 1.3 collective-permute-start.13
  136.8 1.5 shard_map.79
  138.3 0.7 collective-permute-start.10
  139.0 2.6 %shard_map.83 = (f32[5,128,256]{2,1,0:T(8,128)S(1)}, f32[5,8,256]{2,1,0:T(8,128)S(1)}, f32[5,128,256]{2,1,0:T(8,128)S(1)}, f32[5,8,256]{2,1,0:T(8,128)S(1)}) custom-call(s32[2]{0:T(128)S(1)} %pad_add_fusion.3.refs_0_.info_ref, s32[216]{0:T(256)S(1)} %reshape.60.refs_1_, bf16[256,640]{1,0:T(8,128)(2,1)S(1)} %collective-permute-done.17.refs_2_, ...), custom_call_target="tpu_custom_call" | custom-call | flops 754974720 | bytes 2949120 | tf_op jit(solution)/shard_map/pallas_call | solution.py:385
  141.6 1.3 shard_map.85
  142.9 1.3 collective-permute-start.20
  144.2 1.3 collective-permute-start.21
  145.5 1.3 shard_map.84
  146.9 0.7 collective-permute-start.19
  147.6 3.2 %collective-permute-done.13.refs_3_ = bf16[128,896]{1,0:T(8,128)(2,1)S(1)} collective-permute-done((bf16[128,896]{1,0:T(8,128)(2,1)S(1)}, bf16[128,896]{1,0:T(8,128)(2,1)S(1)}, u32[]{:S(2)}, u32[]{:S(2)}) %collective-permute-start.13) | collective-permute-done | bytes 229408 | tf_op jit(solution)/shard_map/ppermute | solution.py:128
  150.8 1.3 shard_map.82.refs_0_
  152.1 11.9 %collective-permute-done.20.refs_3_ = bf16[128,640]{1,0:T(8,128)(2,1)S(1)} collective-permute-done((bf16[128,640]{1,0:T(8,128)(2,1)S(1)}, bf16[128,640]{1,0:T(8,128)(2,1)S(1)}, u32[]{:S(2)}, u32[]{:S(2)}) %collective-permute-start.20) | collective-permute-done | bytes 163872 | tf_op jit(solution)/shard_map/ppermute | solution.py:128
  164.0 2.5 %collective-permute-done.21.refs_4_ = bf16[128,640]{1,0:T(8,128)(2,1)S(1)} collective-permute-done((bf16[128,640]{1,0:T(8,128)(2,1)S(1)}, bf16[128,640]{1,0:T(8,128)(2,1)S(1)}, u32[]{:S(2)}, u32[]{:S(2)}) %collective-permute-start.21) | collective-permute-done | bytes 163872 | tf_op jit(solution)/shard_map/ppermute | solution.py:128
  166.5 1.3 shard_map.86
  (59 shorter events, 1.7 us)
Async XLA Ops:
  0.0 64.0 %collective-permute-start.8 = (bf16[256,1536]{1,0:T(8,128)(2,1)}, bf16[256,1536]{1,0:T(8,128)(2,1)S(1)}, u32[]{:S(2)}, u32[]{:S(2)}) collective-permute-start(bf16[256,1536]{1,0:T(8,128)(2,1)} %refs_0_.7), channel_id=1, source_target_pairs={{4,6},{6,4},{8,10},{10,8},{5,7},{7,5},{9,11},{11,9},{20,22},{22,20... | collective-permute-start | bytes 2359304 | tf_op jit(solution)/shard_map/ppermute | solution.py:128
  0.7 61.5 %collective-permute-start.3 = (bf16[256,1536]{1,0:T(8,128)(2,1)}, bf16[256,1536]{1,0:T(8,128)(2,1)}, u32[]{:S(2)}, u32[]{:S(2)}) collective-permute-start(bf16[256,1536]{1,0:T(8,128)(2,1)} %refs_0_.7), channel_id=1, source_target_pairs={{4,8},{6,10},{8,4},{10,6},{5,9},{7,11},{9,5},{11,7},{20,24},{22,26... | collective-permute-start | bytes 2359304 | tf_op jit(solution)/shard_map/ppermute | solution.py:128
  2.2 1.1 copy-start
  3.4 1.1 copy-start.1
  4.6 12.3 %copy-start.2 = (bf16[256,1536]{1,0:T(8,128)(2,1)S(1)}, bf16[256,1536]{1,0:T(8,128)(2,1)}, u32[]{:S(2)}) copy-start(bf16[256,1536]{1,0:T(8,128)(2,1)} %refs_0_.6) | copy-start | bytes 2359300
  4.6 53.6 %collective-permute-start = (bf16[512,896]{1,0:T(8,128)(2,1)S(1)}, bf16[512,896]{1,0:T(8,128)(2,1)}, u32[]{:S(2)}, u32[]{:S(2)}) collective-permute-start(bf16[512,896]{1,0:T(8,128)(2,1)S(1)} %shard_map.74.refs_3_), channel_id=1, source_target_pairs={{0,4},{2,6},{12,8},{14,10},{1,5},{3,7},{13,9},{15,11},{16,20},{18,... | collective-permute-start | bytes 2752520 | tf_op jit(solution)/shard_map/ppermute | solution.py:128
  14.7 45.2 %collective-permute-start.14 = (bf16[512,640]{1,0:T(8,128)(2,1)}, bf16[512,640]{1,0:T(8,128)(2,1)}, u32[]{:S(2)}, u32[]{:S(2)}) collective-permute-start(bf16[512,640]{1,0:T(8,128)(2,1)} %shard_map.76.refs_7_.refs_3_), channel_id=1, source_target_pairs={{0,4},{2,6},{12,8},{14,10},{1,5},{3,7},{13,9},{15,11},{16,20},{18,... | collective-permute-start | bytes 1966088 | tf_op jit(solution)/shard_map/ppermute | solution.py:128
  17.0 1.5 copy-start.6
  17.0 39.8 %collective-permute-start.11 = (bf16[256,896]{1,0:T(8,128)(2,1)S(1)}, bf16[256,896]{1,0:T(8,128)(2,1)S(1)}, u32[]{:S(2)}, u32[]{:S(2)}) collective-permute-start(bf16[256,896]{1,0:T(8,128)(2,1)S(1)} %shard_map.73.refs_2_), channel_id=1, source_target_pairs={{0,4},{2,6},{12,8},{14,10},{1,5},{3,7},{13,9},{15,11},{16,20},{18,... | collective-permute-start | bytes 1376264 | tf_op jit(solution)/shard_map/ppermute | solution.py:128
  18.6 0.7 copy-start.7
  56.8 0.8 copy-start.4
  57.5 8.0 %collective-permute-start.9 = (bf16[256,1536]{1,0:T(8,128)(2,1)}, bf16[256,1536]{1,0:T(8,128)(2,1)S(1)}, u32[]{:S(2)}, u32[]{:S(2)}) collective-permute-start(bf16[256,1536]{1,0:T(8,128)(2,1)} %refs_1_.3), channel_id=1, source_target_pairs={{4,6},{6,4},{8,10},{10,8},{5,7},{7,5},{9,11},{11,9},{20,22},{22,20... | collective-permute-start | bytes 2359304 | tf_op jit(solution)/shard_map/ppermute | solution.py:128
  58.2 10.5 %collective-permute-start.1 = (bf16[512,896]{1,0:T(8,128)(2,1)}, bf16[512,896]{1,0:T(8,128)(2,1)}, u32[]{:S(2)}, u32[]{:S(2)}) collective-permute-start(bf16[512,896]{1,0:T(8,128)(2,1)} %collective-permute-done.refs_7_.refs_10_), channel_id=1, source_target_pairs={{4,8},{6,10},{8,4},{10,6},{5,9},{7,11},{9,5},{11,7},{20,24},{22,26... | collective-permute-start | bytes 2752520 | tf_op jit(solution)/shard_map/ppermute | solution.py:128
  59.9 7.3 %collective-permute-start.4 = (bf16[256,1536]{1,0:T(8,128)(2,1)}, bf16[256,1536]{1,0:T(8,128)(2,1)}, u32[]{:S(2)}, u32[]{:S(2)}) collective-permute-start(bf16[256,1536]{1,0:T(8,128)(2,1)} %refs_1_.3), channel_id=1, source_target_pairs={{4,8},{6,10},{8,4},{10,6},{5,9},{7,11},{9,5},{11,7},{20,24},{22,26... | collective-permute-start | bytes 2359304 | tf_op jit(solution)/shard_map/ppermute | solution.py:128
  61.5 0.7 copy-start.8
  62.2 9.9 %collective-permute-start.5 = (bf16[256,1536]{1,0:T(8,128)(2,1)}, bf16[256,1536]{1,0:T(8,128)(2,1)}, u32[]{:S(2)}, u32[]{:S(2)}) collective-permute-start(bf16[256,1536]{1,0:T(8,128)(2,1)} %collective-permute-done.3.refs_3_.refs_6_), channel_id=1, source_target_pairs={{4,6},{6,4},{8,10},{10,8},{5,7},{7,5},{9,11},{11,9},{20,22},{22,20... | collective-permute-start | bytes 2359304 | tf_op jit(solution)/shard_map/ppermute | solution.py:128
  64.0 6.5 %collective-permute-start.15 = (bf16[512,640]{1,0:T(8,128)(2,1)}, bf16[512,640]{1,0:T(8,128)(2,1)}, u32[]{:S(2)}, u32[]{:S(2)}) collective-permute-start(bf16[512,640]{1,0:T(8,128)(2,1)} %collective-permute-done.14.refs_10_), channel_id=1, source_target_pairs={{4,8},{6,10},{8,4},{10,6},{5,9},{7,11},{9,5},{11,7},{20,24},{22,26... | collective-permute-start | bytes 1966088 | tf_op jit(solution)/shard_map/ppermute | solution.py:128
  65.5 60.1 %collective-permute-start.7 = (bf16[512,896]{1,0:T(8,128)(2,1)}, bf16[512,896]{1,0:T(8,128)(2,1)}, u32[]{:S(2)}, u32[]{:S(2)}) collective-permute-start(bf16[512,896]{1,0:T(8,128)(2,1)} %collective-permute-done.refs_7_.refs_10_), channel_id=1, source_target_pairs={{4,6},{6,4},{8,10},{10,8},{5,7},{7,5},{9,11},{11,9},{20,22},{22,20... | collective-permute-start | bytes 2752520 | tf_op jit(solution)/shard_map/ppermute | solution.py:128
  67.2 8.0 %collective-permute-start.6 = (bf16[256,1536]{1,0:T(8,128)(2,1)}, bf16[256,1536]{1,0:T(8,128)(2,1)}, u32[]{:S(2)}, u32[]{:S(2)}) collective-permute-start(bf16[256,1536]{1,0:T(8,128)(2,1)} %collective-permute-done.4.refs_4_.refs_7_), channel_id=1, source_target_pairs={{4,6},{6,4},{8,10},{10,8},{5,7},{7,5},{9,11},{11,9},{20,22},{22,20... | collective-permute-start | bytes 2359304 | tf_op jit(solution)/shard_map/ppermute | solution.py:128
  68.7 60.4 %collective-permute-start.2 = (bf16[512,896]{1,0:T(8,128)(2,1)}, bf16[512,896]{1,0:T(8,128)(2,1)}, u32[]{:S(2)}, u32[]{:S(2)}) collective-permute-start(bf16[512,896]{1,0:T(8,128)(2,1)} %collective-permute-done.1.refs_3_), channel_id=1, source_target_pairs={{4,6},{6,4},{8,10},{10,8},{5,7},{7,5},{9,11},{11,9},{20,22},{22,20... | collective-permute-start | bytes 2752520 | tf_op jit(solution)/shard_map/ppermute | solution.py:128
  70.5 68.4 %collective-permute-start.18 = (bf16[512,640]{1,0:T(8,128)(2,1)}, bf16[512,640]{1,0:T(8,128)(2,1)}, u32[]{:S(2)}, u32[]{:S(2)}) collective-permute-start(bf16[512,640]{1,0:T(8,128)(2,1)} %collective-permute-done.14.refs_10_), channel_id=1, source_target_pairs={{4,6},{6,4},{8,10},{10,8},{5,7},{7,5},{9,11},{11,9},{20,22},{22,20... | collective-permute-start | bytes 1966088 | tf_op jit(solution)/shard_map/ppermute | solution.py:128
  72.1 69.5 %collective-permute-start.16 = (bf16[512,640]{1,0:T(8,128)(2,1)}, bf16[512,640]{1,0:T(8,128)(2,1)}, u32[]{:S(2)}, u32[]{:S(2)}) collective-permute-start(bf16[512,640]{1,0:T(8,128)(2,1)} %collective-permute-done.15.refs_3_), channel_id=1, source_target_pairs={{4,6},{6,4},{8,10},{10,8},{5,7},{7,5},{9,11},{11,9},{20,22},{22,20... | collective-permute-start | bytes 1966088 | tf_op jit(solution)/shard_map/ppermute | solution.py:128
  73.7 1.1 copy-start.3
  75.2 63.1 %collective-permute-start.17 = (bf16[256,640]{1,0:T(8,128)(2,1)S(1)}, bf16[256,640]{1,0:T(8,128)(2,1)S(1)}, u32[]{:S(2)}, u32[]{:S(2)}) collective-permute-start(bf16[256,640]{1,0:T(8,128)(2,1)S(1)} %shard_map.75.refs_6_.refs_11_.refs_12_.refs_2_), channel_id=1, source_target_pairs={{0,4},{2,6},{12,8},{14,10},{1,5},{3,7},{13,9},{15,11},{16,20},{18,... | collective-permute-start | bytes 983048 | tf_op jit(solution)/shard_map/ppermute | solution.py:128
  125.7 1.0 copy-start.5
  130.6 16.2 %collective-permute-start.12 = (bf16[128,896]{1,0:T(8,128)(2,1)S(1)}, bf16[128,896]{1,0:T(8,128)(2,1)S(1)}, u32[]{:S(2)}, u32[]{:S(2)}) collective-permute-start(bf16[128,896]{1,0:T(8,128)(2,1)S(1)} %get-tuple-element.37), channel_id=1, source_target_pairs={{4,0},{5,1},{6,2},{7,3},{8,12},{9,13},{10,14},{11,15},{20,16},{21,... | collective-permute-start | bytes 688136 | tf_op jit(solution)/shard_map/ppermute | solution.py:128
  135.5 15.3 %collective-permute-start.13 = (bf16[128,896]{1,0:T(8,128)(2,1)S(1)}, bf16[128,896]{1,0:T(8,128)(2,1)S(1)}, u32[]{:S(2)}, u32[]{:S(2)}) collective-permute-start(bf16[128,896]{1,0:T(8,128)(2,1)S(1)} %get-tuple-element.38), channel_id=1, source_target_pairs={{4,1},{5,0},{6,3},{7,2},{8,13},{9,12},{10,15},{11,14},{20,17},{21,... | collective-permute-start | bytes 688136 | tf_op jit(solution)/shard_map/ppermute | solution.py:128
  138.3 12.5 %collective-permute-start.10 = (bf16[128,896]{1,0:T(8,128)(2,1)S(1)}, bf16[128,896]{1,0:T(8,128)(2,1)S(1)}, u32[]{:S(2)}, u32[]{:S(2)}) collective-permute-start(bf16[128,896]{1,0:T(8,128)(2,1)S(1)} %get-tuple-element.34), channel_id=1, source_target_pairs={{4,5},{5,4},{6,7},{7,6},{8,9},{9,8},{10,11},{11,10},{20,21},{21,20... | collective-permute-start | bytes 688136 | tf_op jit(solution)/shard_map/ppermute | solution.py:128
  142.9 21.0 %collective-permute-start.20 = (bf16[128,640]{1,0:T(8,128)(2,1)S(1)}, bf16[128,640]{1,0:T(8,128)(2,1)S(1)}, u32[]{:S(2)}, u32[]{:S(2)}) collective-permute-start(bf16[128,640]{1,0:T(8,128)(2,1)S(1)} %get-tuple-element.47), channel_id=1, source_target_pairs={{4,0},{5,1},{6,2},{7,3},{8,12},{9,13},{10,14},{11,15},{20,16},{21,... | collective-permute-start | bytes 491528 | tf_op jit(solution)/shard_map/ppermute | solution.py:128
  144.2 22.2 %collective-permute-start.21 = (bf16[128,640]{1,0:T(8,128)(2,1)S(1)}, bf16[128,640]{1,0:T(8,128)(2,1)S(1)}, u32[]{:S(2)}, u32[]{:S(2)}) collective-permute-start(bf16[128,640]{1,0:T(8,128)(2,1)S(1)} %get-tuple-element.48), channel_id=1, source_target_pairs={{4,1},{5,0},{6,3},{7,2},{8,13},{9,12},{10,15},{11,14},{20,17},{21,... | collective-permute-start | bytes 491528 | tf_op jit(solution)/shard_map/ppermute | solution.py:128
  146.9 19.6 %collective-permute-start.19 = (bf16[128,640]{1,0:T(8,128)(2,1)S(1)}, bf16[128,640]{1,0:T(8,128)(2,1)S(1)}, u32[]{:S(2)}, u32[]{:S(2)}) collective-permute-start(bf16[128,640]{1,0:T(8,128)(2,1)S(1)} %get-tuple-element.44), channel_id=1, source_target_pairs={{4,5},{5,4},{6,7},{7,6},{8,9},{9,8},{10,11},{11,10},{20,21},{21,20... | collective-permute-start | bytes 491528 | tf_op jit(solution)/shard_map/ppermute | solution.py:128
